TPU v7x, 32 devices: a whole 2x2x4 slice. The times are simulated.
32 devices in a mesh: group: 2 (over core), replica: 16 (over z, y, x).
Axes of the slice: x: 2, y: 2, z: 4, core: 2. Of those that a mesh axis runs over, the one named last changes fastest.
Arguments:
- tokens: bfloat16 [2, 2, 2048, 1088], P(None, 'group', 'replica'), may hold values from -6 to 6
- out_grad: bfloat16 [2, 2, 2048, 1088], P(None, 'group', 'replica'), may hold values from -6 to 6
- positions: int32 [2, 2, 2048], P(None, 'group', 'replica'), may hold values from 0 to 2047, each once within a row
- prefix: int32 [2, 2], P(None, 'group'), may hold values from 204 to 1024
- ln1_gain: bfloat16 [1088], P('group'), may hold values from 0.099609375 to 1.8984375
- ln1_bias: bfloat16 [1088], P('group'), may hold values from -1.75 to 1.75
- w_qkv: bfloat16 [1088, 3264], P('group'), may hold values from -0.1875 to 0.1875
- b_query: bfloat16 [1088], P('group'), may hold values from -1.75 to 1.75
- b_value: bfloat16 [1088], P('group'), may hold values from -0.1875 to 0.1875
- w_attn_out: bfloat16 [1088, 1088], P('group'), may hold values from -3 to 3
- b_attn_out: bfloat16 [1088], P('group'), may hold values from -1.75 to 1.75
- ln2_gain: bfloat16 [1088], P('group'), may hold values from 0.099609375 to 1.8984375
- ln2_bias: bfloat16 [1088], P('group'), may hold values from -1.75 to 1.75
- w_fc: bfloat16 [1088, 4352], P('group'), may hold values from -0.1875 to 0.1875
- b_fc: bfloat16 [4352], P('group'), may hold values from -1.75 to 1.75
- w_proj: bfloat16 [4352, 1088], P('group'), may hold values from -0.09375 to 0.09375
- b_proj: bfloat16 [1088], P('group'), may hold values from -1.75 to 1.75
Outputs:
- result: bfloat16 [2, 2, 2048, 1088], P(None, 'group', 'replica')
- tokens_grad: bfloat16 [2, 2, 2048, 1088], P(None, 'group', 'replica')
- ln1_gain_grad: float32 [1088], P('group')
- ln1_bias_grad: float32 [1088], P('group')
- w_qkv_grad: float32 [1088, 3264], P('group')
- b_query_grad: float32 [1088], P('group')
- b_value_grad: float32 [1088], P('group')
- w_attn_out_grad: float32 [1088, 1088], P('group')
- b_attn_out_grad: float32 [1088], P('group')
- ln2_gain_grad: float32 [1088], P('group')
- ln2_bias_grad: float32 [1088], P('group')
- w_fc_grad: float32 [1088, 4352], P('group')
- b_fc_grad: float32 [4352], P('group')
- w_proj_grad: float32 [4352, 1088], P('group')
- b_proj_grad: float32 [1088], P('group')
Inputs may be any that keep to these rules, and one draw needn't show every extreme that they name: Each sequence's positions are a permutation of 0 to 2048 - 1 over its slots.
All inputs are finite; a program needn't handle non-finite values.
Results may differ from a plain program's by a relative error of at most 0.02.
Values may be sent and summed in bfloat16 or wider, within the bound.
A program may use at most 256 MiB of HBM per device.

v0:
```python
import jax
import jax.numpy as jnp
from jax import lax
from jax.sharding import PartitionSpec as P

HEADS = 17
HEAD_DIM = 64


def for_sending(array):

    def short(part):
        return part.astype(jnp.bfloat16) if part.dtype == jnp.float32 else part

    return jax.tree.map(short, array)


def norm_rows(values, gain, shift):
    center = values - jnp.mean(values, -1, keepdims=True)
    spread = jnp.mean(center * center, -1, keepdims=True)
    return center * lax.rsqrt(spread + 1e-05) * gain + shift


def gelu_tanh(values):
    return jax.nn.gelu(values, approximate=True)


def inner_rows(left, right):
    return lax.dot_general(
        left, right, (((0,), (0,)), ((), ())), preferred_element_type=jnp.float32
    )


def times_transposed(left, right):
    return lax.dot_general(
        left, right, (((1,), (1,)), ((), ())), preferred_element_type=jnp.float32
    )


def masked_scores(queries, keys, query_place, key_place, prefix_len, scale):
    scores = jnp.einsum("qhe,khe->hqk", queries, keys, preferred_element_type=jnp.float32) * scale
    allowed = (key_place[None, :] <= query_place[:, None]) | (key_place[None, :] < prefix_len)
    return jnp.where(allowed[None], scores, -1e30)


def reduce_grads(terms):
    owned = jax.tree.map(
        lambda part: part.astype(jnp.float32),
        lax.psum_scatter(for_sending(terms), "group", scatter_dimension=0, tiled=True),
    )
    return jax.tree.map(
        lambda part: part.astype(jnp.float32), lax.psum(for_sending(owned), "replica")
    )


def per_device(
    tokens,
    out_grad,
    positions,
    prefix,
    ln1_gain,
    ln1_bias,
    w_qkv,
    b_query,
    b_value,
    w_attn_out,
    b_attn_out,
    ln2_gain,
    ln2_bias,
    w_fc,
    b_fc,
    w_proj,
    b_proj,
):
    shards = (
        ln1_gain,
        ln1_bias,
        w_qkv,
        b_query,
        b_value,
        w_attn_out,
        b_attn_out,
        ln2_gain,
        ln2_bias,
        w_fc,
        b_fc,
        w_proj,
        b_proj,
    )
    micro = tokens.shape[0]
    rows_here = tokens.shape[2]
    width = tokens.shape[3]
    scale = HEAD_DIM ** (-0.5)
    head_shape = (rows_here, HEADS, HEAD_DIM)
    all_places = lax.all_gather(positions, "replica", axis=2, tiled=True)
    outputs_list = []
    grads_list = []
    kept = None
    owned = None
    for step in range(micro):
        full = (
            lax.all_gather(shards[0], "group", axis=0, tiled=True),
            lax.all_gather(shards[1], "group", axis=0, tiled=True),
            lax.all_gather(shards[2], "group", axis=0, tiled=True),
            lax.all_gather(shards[3], "group", axis=0, tiled=True),
            lax.all_gather(shards[4], "group", axis=0, tiled=True),
            lax.all_gather(shards[5], "group", axis=0, tiled=True),
            lax.all_gather(shards[6], "group", axis=0, tiled=True),
            lax.all_gather(shards[7], "group", axis=0, tiled=True),
            lax.all_gather(shards[8], "group", axis=0, tiled=True),
            lax.all_gather(shards[9], "group", axis=0, tiled=True),
            lax.all_gather(shards[10], "group", axis=0, tiled=True),
            lax.all_gather(shards[11], "group", axis=0, tiled=True),
            lax.all_gather(shards[12], "group", axis=0, tiled=True),
        )
        (
            gain_one,
            shift_one,
            mat_qkv,
            bias_query,
            bias_value,
            mat_out,
            bias_out,
            gain_two,
            shift_two,
            mat_fc,
            bias_fc,
            mat_proj,
            bias_proj,
        ) = full
        gain_one = gain_one.astype(jnp.float32)
        shift_one = shift_one.astype(jnp.float32)
        bias_query = bias_query.astype(jnp.float32)
        bias_value = bias_value.astype(jnp.float32)
        bias_out = bias_out.astype(jnp.float32)
        gain_two = gain_two.astype(jnp.float32)
        shift_two = shift_two.astype(jnp.float32)
        bias_fc = bias_fc.astype(jnp.float32)
        bias_proj = bias_proj.astype(jnp.float32)
        rows_in = tokens[step, 0].astype(jnp.float32)
        query_place = positions[step, 0]
        key_place = all_places[step, 0]
        prefix_len = prefix[step, 0]
        normed_one, norm_one_pull = jax.vjp(norm_rows, rows_in, gain_one, shift_one)
        first = normed_one.astype(jnp.bfloat16)
        joined = jnp.dot(first, mat_qkv, preferred_element_type=jnp.float32)
        queries = (joined[:, :width] + bias_query).astype(jnp.bfloat16)
        keys = joined[:, width : 2 * width].astype(jnp.bfloat16)
        values = (joined[:, 2 * width :] + bias_value).astype(jnp.bfloat16)
        key_all, value_all = (
            lax.all_gather(keys, "replica", axis=0, tiled=True),
            lax.all_gather(values, "replica", axis=0, tiled=True),
        )
        length = key_all.shape[0]
        block = min(512, length)
        nblocks = length // block
        query_heads = queries.reshape(head_shape)
        key_blocks = key_all.reshape(nblocks, block, HEADS, HEAD_DIM)
        value_blocks = value_all.reshape(nblocks, block, HEADS, HEAD_DIM)
        place_blocks = key_place.reshape(nblocks, block)

        def attend_step(carry, blockargs):
            highest, total, summed = carry
            key_part, value_part, place_part = blockargs
            scores = masked_scores(
                query_heads, key_part, query_place, place_part, prefix_len, scale
            )
            new_high = jnp.maximum(highest, jnp.max(scores, -1))
            factor = jnp.exp(highest - new_high)
            expo = jnp.exp(scores - new_high[..., None])
            total = total * factor + jnp.sum(expo, -1)
            summed = summed * jnp.transpose(factor)[..., None] + jnp.einsum(
                "hqk,khe->qhe",
                expo.astype(jnp.bfloat16),
                value_part,
                preferred_element_type=jnp.float32,
            )
            return ((new_high, total, summed), None)

        start_carry = (
            jnp.full((HEADS, rows_here), -1e30, jnp.float32),
            jnp.zeros((HEADS, rows_here), jnp.float32),
            jnp.zeros(head_shape, jnp.float32),
        )
        (highest, total, summed), _ = lax.scan(
            attend_step, start_carry, (key_blocks, value_blocks, place_blocks)
        )
        log_total = highest + jnp.log(total)
        attended_f = summed / jnp.transpose(total)[..., None]
        attended = attended_f.reshape(rows_here, width).astype(jnp.bfloat16)
        middle = rows_in + jnp.dot(attended, mat_out, preferred_element_type=jnp.float32) + bias_out
        normed_two, norm_two_pull = jax.vjp(norm_rows, middle, gain_two, shift_two)
        second = normed_two.astype(jnp.bfloat16)
        hidden_in = jnp.dot(second, mat_fc, preferred_element_type=jnp.float32) + bias_fc
        hidden_f, gelu_pull = jax.vjp(gelu_tanh, hidden_in)
        hidden = hidden_f.astype(jnp.bfloat16)
        output_rows = (
            middle + jnp.dot(hidden, mat_proj, preferred_element_type=jnp.float32) + bias_proj
        )
        outputs_list.append(output_rows.astype(jnp.bfloat16))
        grad_top = out_grad[step, 0].astype(jnp.float32)
        grad_low = out_grad[step, 0]
        grad_bias_proj = jnp.sum(grad_top, 0)
        grad_mat_proj = inner_rows(hidden, grad_low)
        grad_hidden = times_transposed(grad_low, mat_proj)
        (grad_hidden_in,) = gelu_pull(grad_hidden)
        grad_hidden_in = grad_hidden_in.astype(jnp.bfloat16)
        grad_bias_fc = jnp.sum(grad_hidden_in, 0, dtype=jnp.float32)
        grad_mat_fc = inner_rows(second, grad_hidden_in)
        grad_second = times_transposed(grad_hidden_in, mat_fc)
        grad_middle_norm, grad_gain_two, grad_shift_two = norm_two_pull(grad_second)
        grad_middle = grad_top + grad_middle_norm
        grad_bias_out = jnp.sum(grad_middle, 0)
        grad_branch = grad_middle.astype(jnp.bfloat16)
        grad_mat_out = inner_rows(attended, grad_branch)
        grad_attended = times_transposed(grad_branch, mat_out).astype(jnp.bfloat16)
        grad_heads = grad_attended.reshape(head_shape)
        delta = jnp.transpose(jnp.sum(grad_heads.astype(jnp.float32) * attended_f, -1))

        def score_grads(
            query_part, grad_part, key_part, value_part, qplace, kplace, lse_part, delta_part
        ):
            scores = masked_scores(query_part, key_part, qplace, kplace, prefix_len, scale)
            probs = jnp.exp(scores - lse_part[..., None])
            grad_probs = jnp.einsum(
                "qhe,khe->hqk", grad_part, value_part, preferred_element_type=jnp.float32
            )
            grad_scores = (probs * (grad_probs - delta_part[..., None])).astype(jnp.bfloat16)
            return (probs.astype(jnp.bfloat16), grad_scores)

        def grad_step(summed, blockargs):
            key_part, value_part, place_part = blockargs
            probs, grad_scores = score_grads(
                query_heads,
                grad_heads,
                key_part,
                value_part,
                query_place,
                place_part,
                log_total,
                delta,
            )
            summed = summed + jnp.einsum(
                "hqk,khe->qhe", grad_scores, key_part, preferred_element_type=jnp.float32
            )
            key_grad = jnp.einsum(
                "hqk,qhe->khe", grad_scores, query_heads, preferred_element_type=jnp.float32
            )
            value_grad = jnp.einsum(
                "hqk,qhe->khe", probs, grad_heads, preferred_element_type=jnp.float32
            )
            return (summed, (key_grad, value_grad))

        grad_query, (key_grads, value_grads) = lax.scan(
            grad_step, jnp.zeros(head_shape, jnp.float32), (key_blocks, value_blocks, place_blocks)
        )
        grad_key, grad_value = (
            lax.psum_scatter(
                key_grads.reshape(length, width).astype(jnp.bfloat16),
                "replica",
                scatter_dimension=0,
                tiled=True,
            ).astype(jnp.float32),
            lax.psum_scatter(
                value_grads.reshape(length, width).astype(jnp.bfloat16),
                "replica",
                scatter_dimension=0,
                tiled=True,
            ).astype(jnp.float32),
        )
        grad_query = (grad_query.reshape(rows_here, width) * scale).astype(jnp.bfloat16)
        grad_key = (grad_key * scale).astype(jnp.bfloat16)
        grad_value = grad_value.astype(jnp.bfloat16)
        grad_bias_query = jnp.sum(grad_query, 0, dtype=jnp.float32)
        grad_bias_value = jnp.sum(grad_value, 0, dtype=jnp.float32)
        grad_joined = jnp.concatenate([grad_query, grad_key, grad_value], 1)
        grad_mat_qkv = inner_rows(first, grad_joined)
        grad_first = times_transposed(grad_joined, mat_qkv)
        grad_rows_norm, grad_gain_one, grad_shift_one = norm_one_pull(grad_first)
        grads_list.append((grad_middle + grad_rows_norm).astype(jnp.bfloat16))
        terms = (
            grad_gain_one,
            grad_shift_one,
            grad_mat_qkv,
            grad_bias_query,
            grad_bias_value,
            grad_mat_out,
            grad_bias_out,
            grad_gain_two,
            grad_shift_two,
            grad_mat_fc,
            grad_bias_fc,
            grad_mat_proj,
            grad_bias_proj,
        )
        kept = (
            terms
            if kept is None
            else tuple((first_term + second_term for first_term, second_term in zip(kept, terms)))
        )
    owned = reduce_grads(kept)
    result = jnp.stack(outputs_list).reshape(micro, 1, rows_here, width)
    tokens_grad = jnp.stack(grads_list).reshape(micro, 1, rows_here, width)
    return (result, tokens_grad) + tuple(owned)


def solution(mesh):
    in_specs = (
        P(None, "group", "replica", None),
        P(None, "group", "replica", None),
        P(None, "group", "replica"),
        P(None, "group"),
        P("group"),
        P("group"),
        P("group", None),
        P("group"),
        P("group"),
        P("group", None),
        P("group"),
        P("group"),
        P("group"),
        P("group", None),
        P("group"),
        P("group", None),
        P("group"),
    )
    out_specs = (
        P(None, "group", "replica", None),
        P(None, "group", "replica", None),
        P("group"),
        P("group"),
        P("group", None),
        P("group"),
        P("group"),
        P("group", None),
        P("group"),
        P("group"),
        P("group"),
        P("group", None),
        P("group"),
        P("group", None),
        P("group"),
    )
    return jax.shard_map(
        per_device, mesh=mesh, in_specs=in_specs, out_specs=out_specs, check_vma=False
    )
```

profile of v0, /device:TPU:0, one launch (start us, length us, event | category | flops | bytes accessed | tf_op | source)
XLA Modules:
  0.0 1721.5 jit_solution(15106863747839549173)
XLA Ops:
  15.2 15.3 all-gather.10.cloned.1.call-done
  30.5 6.3 fusion.199
  37.8 6.4 fusion.196
  50.3 41.6 %all_gather.67 = s32[2,1,2048]{2,1,0:T(1,128)S(1)} all-gather(s32[2,1,128]{2,1,0:T(1,128)S(1)} %copy-done.90), channel_id=1, replica_groups=mesh['group'=2,'replica'=16] {'replica'}, dimensions={2}, use_global_device_ids=true | all-gather | bytes 17408 | tf_op jit(solution)/shard_map/all_gather | solution.py:95
  94.7 36.2 %all-gather.22.cloned.1.call-done = bf16[2048,1088]{0,1:T(8,128)(2,1)} async-done(((bf16[128,1088]{0,1:T(8,128)(2,1)}), bf16[2048,1088]{0,1:T(8,128)(2,1)}) %all-gather.22.cloned.1.call-update) | async-done | bytes 4456464 | tf_op jit(solution)/shard_map/all_gather | solution.py:151
  131.0 10.3 reshape.420
  141.3 5.5 copy.82
  146.7 77.6 %all-gather.24.cloned.1.call-done = bf16[2048,1088]{0,1:T(8,128)(2,1)} async-done(((bf16[128,1088]{0,1:T(8,128)(2,1)}), bf16[2048,1088]{0,1:T(8,128)(2,1)}) %all-gather.24.cloned.1.call-update) | async-done | bytes 4456464 | tf_op jit(solution)/shard_map/all_gather | solution.py:152
  224.4 10.3 reshape.422
  234.7 5.4 copy.83
  240.1 76.9 %all-gather.12.cloned.1.call-done = bf16[2048,1088]{0,1:T(8,128)(2,1)} async-done(((bf16[128,1088]{0,1:T(8,128)(2,1)}), bf16[2048,1088]{0,1:T(8,128)(2,1)}) %all-gather.12.cloned.1.call-update) | async-done | bytes 4456464 | tf_op jit(solution)/shard_map/all_gather | solution.py:151
  317.0 10.3 reshape.417
  327.3 5.5 copy.80
  332.8 76.9 %all-gather.14.cloned.1.call-done = bf16[2048,1088]{0,1:T(8,128)(2,1)} async-done(((bf16[128,1088]{0,1:T(8,128)(2,1)}), bf16[2048,1088]{0,1:T(8,128)(2,1)}) %all-gather.14.cloned.1.call-update) | async-done | bytes 4456464 | tf_op jit(solution)/shard_map/all_gather | solution.py:152
  409.7 10.4 reshape.419
  420.1 5.4 copy.81
  425.5 51.0 %while.60 = (s32[]{:T(128)}, f32[17,128]{1,0:T(8,128)S(1)}, f32[17,128]{1,0:T(8,128)S(1)}, f32[128,17,64]{0,2,1:T(8,128)S(1)}, s32[4,512]{1,0:T(4,128)S(1)}, /*i...) while((s32[]{:T(128)}, f32[17,128]{1,0:T(8,128)S(1)}, ...), condition=%wide.region_5.6_spmd.clone, body=%wide.region_2.5_spmd.clone.sunk | while | flops 298030336 | bytes 35225268 | solution.py:185
  426.7 4.6 fusion.295
  431.3 4.4 fusion.297
  440.3 4.4 fusion.295
  451.9 4.7 fusion.295
  456.6 4.3 fusion.297
  465.7 4.4 fusion.295
  480.4 49.7 %while.61 = (s32[]{:T(128)}, f32[17,128]{1,0:T(8,128)S(1)}, f32[17,128]{1,0:T(8,128)S(1)}, f32[128,17,64]{0,2,1:T(8,128)}, s32[4,512]{1,0:T(4,128)S(1)}, /*index...) while((s32[]{:T(128)}, f32[17,128]{1,0:T(8,128)S(1)}, ...), condition=%wide.region_13.14_spmd.clone, body=%wide.region_10.13_spmd.clone.sunk | while | flops 298030336 | bytes 35225268 | solution.py:185
  481.5 4.4 fusion.303
  493.7 4.4 fusion.303
  506.1 4.4 fusion.303
  518.5 4.4 fusion.303
  534.6 7.0 convolution_add_fusion.5
  541.6 8.2 convert_reduce_fusion.1
  571.8 62.5 %while.63 = (s32[]{:T(128)}, f32[128,17,64]{0,2,1:T(8,128)}, bf16[4,512,17,64]{1,3,2,0:T(8,128)(2,1)}, bf16[4,512,17,64]{1,3,2,0:T(8,128)(2,1)}, bf16[4,512,17,6...) while((s32[]{:T(128)}, f32[128,17,64]{0,2,1:T(8,128)}, ...), condition=%wide.region_29.30_spmd.clone, body=%wide.region_28.29_spmd.clone.sunk | while | flops 724582912 | bytes 101618472 | solution.py:254
  634.3 6.1 copy.91
  640.4 4.0 copy.115
  644.4 6.4 copy.108
  651.1 6.1 copy.90
  661.1 6.4 copy.106
  677.4 60.5 %while.62 = (s32[]{:T(128)}, f32[128,17,64]{0,2,1:T(8,128)S(1)}, bf16[4,512,17,64]{1,3,2,0:T(8,128)(2,1)}, bf16[4,512,17,64]{1,3,2,0:T(8,128)(2,1)}, bf16[4,512,...) while((s32[]{:T(128)}, f32[128,17,64]{0,2,1:T(8,128)S(1)}, ...), condition=%wide.region_20.21_spmd.clone, body=%wide.region_19.20_spmd.clone.sunk | while | flops 724582912 | bytes 101618472 | solution.py:254
  737.8 6.3 copy.87
  748.0 6.7 copy.104
  755.2 6.1 copy.86
  765.3 6.6 copy.102
  773.7 7.9 fusion.166
  781.6 11.5 fusion.103
  793.1 13.9 copy.110
  812.4 9.5 fusion.201
  822.0 11.2 fusion.102
  837.7 93.7 %reduce-scatter.29.cloned.1.call-done = bf16[128,1088]{1,0:T(8,128)(2,1)} async-done(((bf16[2048,1088]{1,0:T(8,128)(2,1)}), bf16[128,1088]{1,0:T(8,128)(2,1)}) %reduce-scatter.29.cloned.1.call-update) | async-done | bytes 278544
  932.5 141.9 %reduce-scatter.27.cloned.1.call-done = bf16[128,1088]{1,0:T(8,128)(2,1)} async-done(((bf16[2048,1088]{1,0:T(8,128)(2,1)}), bf16[128,1088]{1,0:T(8,128)(2,1)}) %reduce-scatter.27.cloned.1.call-update) | async-done | bytes 278544
  1076.3 141.6 %reduce-scatter.25.cloned.1.call-done = bf16[128,1088]{1,0:T(8,128)(2,1)} async-done(((bf16[2048,1088]{1,0:T(8,128)(2,1)}), bf16[128,1088]{1,0:T(8,128)(2,1)}) %reduce-scatter.25.cloned.1.call-update) | async-done | bytes 278544
  1223.3 6.4 fusion.104
  1229.7 7.1 reduce-scatter.33.cloned.1.call-done
  1236.8 8.3 copy.111
  1245.1 6.0 reduce-scatter.21.cloned.1.call-done
  1251.1 21.3 %reduce-scatter.23.cloned.1.call-done = bf16[544,4352]{1,0:T(8,128)(2,1)} async-done(((bf16[1088,4352]{1,0:T(8,128)(2,1)}), bf16[544,4352]{1,0:T(8,128)(2,1)}) %reduce-scatter.23.cloned.1.call-update) | async-done | bytes 4734992 | tf_op jit(solution)/shard_map/reduce_scatter | solution.py:49
  1272.4 20.1 %reduce-scatter.19.cloned.1.call-done = bf16[544,3264]{1,0:T(8,128)(2,1)} async-done(((bf16[1088,3264]{1,0:T(8,128)(2,1)}), bf16[544,3264]{1,0:T(8,128)(2,1)}) %reduce-scatter.19.cloned.1.call-update) | async-done | bytes 3551248 | tf_op jit(solution)/shard_map/reduce_scatter | solution.py:49
  1295.0 5.2 fusion.156
  1300.2 5.2 fusion.149
  1310.6 81.8 %all-reduce.17 = (bf16[544]{0:T(1024)(128)(2,1)S(1)}, bf16[544]{0:T(1024)(128)(2,1)S(1)}, bf16[544]{0:T(1024)(128)(2,1)S(1)}, bf16[544]{0:T(1024)(128)(2,1)S(1)}...) all-reduce(bf16[544]{0:T(1024)(128)(2,1)S(1)} %dynamic-slice.9, ...), channel_id=1, replica_groups=mesh['group'=2,'replica'=16] {'replica'}, use_global_device_ids=true, to_apply=%region_37.38 | all-reduce | flops 6528 | bytes 26112 | tf_op jit(solution)/shard_map/psum | solution.py:52
  1397.8 7.2 fusion.112
  1405.0 6.6 fusion.113
  1413.8 284.8 %all-reduce.23.cloned.1.call-done = (bf16[544,3264]{1,0:T(8,128)(2,1)}, bf16[544,1088]{1,0:T(8,128)(2,1)}, bf16[544,4352]{1,0:T(8,128)(2,1)}, bf16[2176,1088]{0,1:T(8,128)(2,1)}) async-done(((bf16[544,3264]{1,0:T(8,128)(2,1)}, bf16[544,1088]{1,0:T(8,128)(2,1)}, bf16[544,4352]{1,0:T(8,128)(2,1)}, bf16[2176,1088]{0,1:T(8,128)(2,1)}), (bf16[544,3264]{1,0:T(8,128)(2,1)}, bf16[544,1088]{1,0:T(8,128)(2,1)}, ...) | async-done | bytes 14204944 | tf_op jit(solution)/shard_map/psum | solution.py:52
  1698.6 5.7 convert_element_type.395
  1705.9 4.5 convert_element_type.414
  1710.4 4.4 convert_element_type.420
  (570 shorter events, 281.9 us)
Async XLA Ops:
  7.3 7.6 copy-start.15
  7.3 23.3 %all-gather.10.cloned.1.call-start = ((), (), s32[]{:S(2)}) async-start(), calls=%async_computation.8 | async-start | bytes 10862592 | tf_op jit(solution)/shard_map/all_gather | solution.py:104
  8.0 122.9 %all-gather.22.cloned.1.call-start = ((), (), s32[]{:S(2)}) async-start(), calls=%async_computation.14 | async-start | bytes 4734976 | tf_op jit(solution)/shard_map/all_gather | solution.py:151
  14.8 23.0 %copy-start.61 = (f32[1088]{0:T(1024)}, f32[1088]{0:T(1024)S(1)}, u32[]{:S(2)}) copy-start(f32[1088]{0:T(1024)S(1)} %convert_element_type.336) | copy-start | bytes 13060
  14.8 22.9 %copy-start.57 = (f32[1088]{0:T(1024)}, f32[1088]{0:T(1024)S(1)}, u32[]{:S(2)}) copy-start(f32[1088]{0:T(1024)S(1)} %convert_element_type.335) | copy-start | bytes 13060
  15.0 21.9 %copy-start.81 = (f32[128]{0:T(128)}, f32[128]{0:T(128)S(1)}, u32[]{:S(2)}) copy-start(f32[128]{0:T(128)S(1)} %get-tuple-element.812) | copy-start | bytes 1540
  15.0 22.8 %copy-start.65 = (f32[128]{0:T(128)}, f32[128]{0:T(128)S(1)}, u32[]{:S(2)}) copy-start(f32[128]{0:T(128)S(1)} %get-tuple-element.813) | copy-start | bytes 1540
  15.2 21.7 %copy-start.101 = (f32[128]{0:T(128)}, f32[128]{0:T(128)S(1)}, u32[]{:S(2)}) copy-start(f32[128]{0:T(128)S(1)} %get-tuple-element.627) | copy-start | bytes 1540
  15.2 22.5 %copy-start.103 = (f32[128]{0:T(128)}, f32[128]{0:T(128)S(1)}, u32[]{:S(2)}) copy-start(f32[128]{0:T(128)S(1)} %get-tuple-element.626) | copy-start | bytes 1540
  15.2 21.7 %copy-start.87 = (f32[128]{0:T(128)}, f32[128]{0:T(128)S(1)}, u32[]{:S(2)}) copy-start(f32[128]{0:T(128)S(1)} %fusion.187) | copy-start | bytes 1540
  37.7 186.7 %all-gather.24.cloned.1.call-start = ((), (), s32[]{:S(2)}) async-start(), calls=%async_computation.15 | async-start | bytes 4734976 | tf_op jit(solution)/shard_map/all_gather | solution.py:152
  37.8 6.4 copy-start.83
  45.6 271.4 %all-gather.12.cloned.1.call-start = ((), (), s32[]{:S(2)}) async-start(), calls=%async_computation.9 | async-start | bytes 4734976 | tf_op jit(solution)/shard_map/all_gather | solution.py:151
  47.5 362.2 %all-gather.14.cloned.1.call-start = ((), (), s32[]{:S(2)}) async-start(), calls=%async_computation.10 | async-start | bytes 4734976 | tf_op jit(solution)/shard_map/all_gather | solution.py:152
  48.1 428.4 %all-gather.16.cloned.1.call-start = ((), (), s32[]{:S(2)}) async-start(), calls=%async_computation.11 | async-start | bytes 3760128 | tf_op jit(solution)/shard_map/all_gather | solution.py:107
  48.7 485.9 %all-gather.18.cloned.1.call-start = ((), (), s32[]{:S(2)}) async-start(), calls=%async_computation.12 | async-start | bytes 14204928 | tf_op jit(solution)/shard_map/all_gather | solution.py:111
  49.4 42.6 %copy-start.100 = (s32[2,1]{0,1:T(1,128)S(1)}, s32[2,1]{0,1:T(1,128)}, u32[]{:S(2)}) copy-start(s32[2,1]{0,1:T(1,128)} %param.28) | copy-start | bytes 28
  49.4 43.1 %copy-start.89 = (bf16[2176]{0:T(1024)(128)(2,1)S(1)}, bf16[2176]{0:T(1024)(128)(2,1)}, u32[]{:S(2)}) copy-start(bf16[2176]{0:T(1024)(128)(2,1)} %param.39) | copy-start | bytes 13060
  49.5 492.1 %all-gather.20.cloned.1.call-start = ((), (), s32[]{:S(2)}) async-start(), calls=%async_computation.13 | async-start | bytes 14204928 | tf_op jit(solution)/shard_map/all_gather | solution.py:113
  50.2 785.6 %reduce-scatter.31.cloned.1.call-start = ((), (), s32[]{:S(2)}) async-start(), calls=%async_computation.22 | async-start | bytes 5013504
  92.6 470.4 %copy-start.50 = (f32[1088]{0:T(1024)}, f32[1088]{0:T(1024)S(1)}, u32[]{:S(2)}) copy-start(f32[1088]{0:T(1024)S(1)} %convert_element_type.345) | copy-start | bytes 13060
  94.7 457.7 %copy-start.59 = (f32[1088]{0:T(1024)}, f32[1088]{0:T(1024)S(1)}, u32[]{:S(2)}) copy-start(f32[1088]{0:T(1024)S(1)} %convert_element_type.346) | copy-start | bytes 13060
  431.3 5.4 copy-start
  456.6 5.2 copy-start
  479.6 83.4 %copy-start.63 = (f32[128]{0:T(128)}, f32[128]{0:T(128)S(1)}, u32[]{:S(2)}) copy-start(f32[128]{0:T(128)S(1)} %broadcast_multiply_fusion.2) | copy-start | bytes 1540
  480.4 50.9 %copy-start.7 = (bf16[1088,1088]{1,0:T(8,128)(2,1)S(1)}, bf16[1088,1088]{1,0:T(8,128)(2,1)}, u32[]{:S(2)}) copy-start(bf16[1088,1088]{1,0:T(8,128)(2,1)} %all-gather.16.cloned.1.call-done) | copy-start | bytes 7102468
  533.6 29.4 %copy-start.77 = (f32[128]{0:T(128)}, f32[128]{0:T(128)S(1)}, u32[]{:S(2)}) copy-start(f32[128]{0:T(128)S(1)} %broadcast_multiply_fusion) | copy-start | bytes 1540
  534.5 28.5 %copy-start.75 = (f32[128]{0:T(128)}, f32[128]{0:T(128)S(1)}, u32[]{:S(2)}) copy-start(f32[128]{0:T(128)S(1)} %fusion.186) | copy-start | bytes 1540
  534.5 28.5 %copy-start.85 = (f32[128]{0:T(128)}, f32[128]{0:T(128)S(1)}, u32[]{:S(2)}) copy-start(f32[128]{0:T(128)S(1)} %fusion.188) | copy-start | bytes 1540
  541.6 8.2 copy-start.2
  578.4 4.7 copy-start.20
  593.8 4.8 copy-start.20
  609.4 4.8 copy-start.20
  624.9 4.9 copy-start.20
  650.8 280.5 %reduce-scatter.29.cloned.1.call-start = ((), (), s32[]{:S(2)}) async-start(), calls=%async_computation.21 | async-start | bytes 5013504
  667.6 406.8 %reduce-scatter.27.cloned.1.call-start = ((), (), s32[]{:S(2)}) async-start(), calls=%async_computation.20 | async-start | bytes 5013504
  694.7 4.6 copy-start.5
  737.8 6.3 copy-start.18
  754.8 463.1 %reduce-scatter.25.cloned.1.call-start = ((), (), s32[]{:S(2)}) async-start(), calls=%async_computation.19 | async-start | bytes 5013504
  772.0 464.8 %reduce-scatter.33.cloned.1.call-start = ((), (), s32[]{:S(2)}) async-start(), calls=%async_computation.23 | async-start | bytes 15040512
  807.1 444.0 %reduce-scatter.21.cloned.1.call-start = ((), (), s32[]{:S(2)}) async-start(), calls=%async_computation.17 | async-start | bytes 3760128 | tf_op jit(solution)/shard_map/reduce_scatter | solution.py:49
  811.4 10.6 copy-start.14
  811.4 10.5 copy-start.33
  811.4 10.5 copy-start.78
  811.4 10.5 copy-start.86
  811.4 461.0 %reduce-scatter.23.cloned.1.call-start = ((), (), s32[]{:S(2)}) async-start(), calls=%async_computation.18 | async-start | bytes 14204928 | tf_op jit(solution)/shard_map/reduce_scatter | solution.py:49
  833.1 459.4 %reduce-scatter.19.cloned.1.call-start = ((), (), s32[]{:S(2)}) async-start(), calls=%async_computation.16 | async-start | bytes 10862592 | tf_op jit(solution)/shard_map/reduce_scatter | solution.py:49
  834.2 385.7 %copy-start.16 = (bf16[2,1,128,1088]{2,3,1,0:T(8,128)(2,1)S(1)}, bf16[2,1,128,1088]{2,3,1,0:T(8,128)(2,1)}, u32[]{:S(2)}) copy-start(bf16[2,1,128,1088]{2,3,1,0:T(8,128)(2,1)} %param.25) | copy-start | bytes 1671172
  834.2 385.7 %copy-start.58 = (f32[1088]{0:T(1024)S(1)}, f32[1088]{0:T(1024)}, u32[]{:S(2)}) copy-start(f32[1088]{0:T(1024)} %copy-done.57) | copy-start | bytes 13060
  834.2 385.7 %copy-start.62 = (f32[1088]{0:T(1024)S(1)}, f32[1088]{0:T(1024)}, u32[]{:S(2)}) copy-start(f32[1088]{0:T(1024)} %copy-done.61) | copy-start | bytes 13060
  834.2 385.7 %copy-start.66 = (f32[128]{0:T(128)S(1)}, f32[128]{0:T(128)}, u32[]{:S(2)}) copy-start(f32[128]{0:T(128)} %copy-done.65) | copy-start | bytes 1540
  834.2 385.7 %copy-start.84 = (f32[128]{0:T(128)S(1)}, f32[128]{0:T(128)}, u32[]{:S(2)}) copy-start(f32[128]{0:T(128)} %copy-done.83) | copy-start | bytes 1540
  1229.7 468.9 %all-reduce.23.cloned.1.call-start = ((), (), s32[]{:S(2)}) async-start(), calls=%async_computation.24 | async-start | bytes 28688384 | tf_op jit(solution)/shard_map/psum | solution.py:52
  1294.9 5.2 copy-start.54
  1295.0 5.2 copy-start.56
  1300.1 5.2 copy-start.104
  1300.2 5.3 copy-start.102
  1397.8 7.3 copy-start.25
  1405.0 7.5 copy-start.28
  1405.0 7.5 copy-start.30
  1698.6 7.4 slice-start.2
  1698.6 5.7 copy-start.49
  1698.6 7.4 slice-start.3
  1704.3 6.1 slice-start
  (95 other events, 244.2 us)
Sparse Core Ops, SparseCore 0:
  9.6 20.8 all-gather.9
  37.8 93.1 all-gather.21
  134.2 90.0 all-gather.23
  226.9 90.0 all-gather.11
  319.6 90.0 all-gather.13
  411.1 9.3 all-gather.15
  422.0 22.8 all-gather.17
  446.5 22.8 all-gather.19
  651.0 137.1 reduce-scatter.30
  793.8 137.5 reduce-scatter.28
  936.5 137.8 reduce-scatter.26
  1079.5 138.3 reduce-scatter.24
  1220.1 16.6 reduce-scatter.32
  1239.5 11.5 reduce-scatter.20
  1253.8 18.5 reduce-scatter.22
  1275.2 17.2 reduce-scatter.18
  1299.3 399.1 all-reduce.22
where the time goes:
time: 1730 us; the launch traced here: 1720 us
  waiting for transfers between devices  1000 us (58%)
  matrix products  277 us (16%)
  local copies, waits for them, and re-layouts  211 us (12%)
  blocking collectives  133 us (8%)
  other arithmetic  77.2 us (4%)
  between operations  17.7 us (1%)
    unnamed x22, waiting for transfers between devices  388 us
    psum x1, waiting for transfers between devices, reduce_grads(): lax.psum(for_sending(owned), 'replica')  285 us
    all_gather x2, waiting for transfers between devices, per_device(): lax.all_gather(values, 'replica', axis=0, tiled=True)  154 us
    all_gather x2, waiting for transfers between devices, per_device(): lax.all_gather(keys, 'replica', axis=0, tiled=True)  113 us
    unnamed x249, local copies, waits for them, and re-layouts  105 us
    psum x1, blocking collectives, reduce_grads(): lax.psum(for_sending(owned), 'replica')  81.8 us
    dot_general x8, matrix products, inner_rows(): lax.dot_general(left, right, (((0,), (0,)), ((), ())), preferred_element_...  52.9 us
    dot_general x16, matrix products, masked_scores(): jnp.einsum('qhe,khe->hqk', queries, keys, preferred_element_type=jnp.floa...  52 us
  transfers between devices with their start and end apart: 17, of which 13 were waited for; matrix products, arithmetic and copies ran while one was open for 24% of the time, Pallas kernels for 0%

commit v1 on v0

--- a/solution.py
+++ b/solution.py
@@ -1,10 +1,15 @@
+import functools
+
 import jax
 import jax.numpy as jnp
 from jax import lax
+from jax.experimental import pallas as pl
+from jax.experimental.pallas import tpu as pltpu
 from jax.sharding import PartitionSpec as P
 
 HEADS = 17
 HEAD_DIM = 64
+MESH = pl.DeviceIdType.MESH
 
 
 def for_sending(array):
@@ -53,7 +58,7 @@
     )
 
 
-def per_device(
+def per_device_gather(
     tokens,
     out_grad,
     positions,
@@ -304,43 +309,611 @@
     return (result, tokens_grad) + tuple(owned)
 
 
+def contract(left, right, left_dim, right_dim):
+    return lax.dot_general(
+        left, right, (((left_dim,), (right_dim,)), ((), ())), preferred_element_type=jnp.float32
+    )
+
+
+def greet(peers, here, group_too):
+    barrier = pltpu.get_barrier_semaphore()
+
+    def one(step, carry):
+        peer = lax.rem(here + step, peers)
+        pl.semaphore_signal(barrier, inc=1, device_id={"replica": peer}, device_id_type=MESH)
+        return carry
+
+    lax.fori_loop(1, peers, one, 0)
+    if group_too:
+        other = 1 - lax.axis_index("group")
+        pl.semaphore_signal(barrier, inc=1, device_id={"group": other}, device_id_type=MESH)
+    pl.semaphore_wait(barrier, peers - 1 + (1 if group_too else 0))
+
+
+def exchange_body(direction, with_places, nweights, *refs):
+    refs = list(refs)
+    chunk, last = refs.pop(0), refs.pop(0)
+    places = refs.pop(0) if with_places else None
+    weights = [refs.pop(0) for _ in range(nweights)]
+    chunk_out, last_out = refs.pop(0), refs.pop(0)
+    places_out = refs.pop(0) if with_places else None
+    weights_out = [refs.pop(0) for _ in range(nweights)]
+    send, recv, last_send, last_recv, own = (refs.pop(0) for _ in range(5))
+    if with_places:
+        place_send, place_recv = refs.pop(0), refs.pop(0)
+    if nweights:
+        weight_send, weight_recv, weight_own = (refs.pop(0) for _ in range(3))
+        bounce = [refs.pop(0) for _ in range(nweights)]
+    peers = chunk.shape[0]
+    here = lax.axis_index("replica")
+    group = lax.axis_index("group")
+    greet(peers, here, nweights > 0)
+    loads, copies = [], []
+    for i in range(nweights):
+        copy = pltpu.make_async_remote_copy(
+            weights[i],
+            weights_out[i].at[group],
+            weight_send.at[i],
+            weight_recv.at[i],
+            device_id={"group": 1 - group},
+            device_id_type=MESH,
+        )
+        copy.start()
+        copies.append(copy)
+        load = pltpu.make_async_copy(weights[i], bounce[i], weight_own.at[i])
+        load.start()
+        loads.append(load)
+    for slot in range(2):
+        half = peers // 2
+        target = lax.rem(here + direction + peers, half) + half * slot
+        copy = pltpu.make_async_remote_copy(
+            last.at[slot],
+            last_out.at[here // half],
+            last_send.at[slot],
+            last_recv.at[here // half],
+            device_id={"replica": target},
+            device_id_type=MESH,
+        )
+        copy.start()
+        copies.append(
+            (
+                copy,
+                pltpu.make_async_remote_copy(
+                    last.at[slot],
+                    last_out.at[slot],
+                    last_send.at[slot],
+                    last_recv.at[slot],
+                    device_id={"replica": target},
+                    device_id_type=MESH,
+                ),
+            )
+        )
+    for step in range(1, peers):
+        peer = lax.rem(here + step, peers)
+        copy = pltpu.make_async_remote_copy(
+            chunk.at[peer],
+            chunk_out.at[here],
+            send.at[step],
+            recv.at[step],
+            device_id={"replica": peer},
+            device_id_type=MESH,
+        )
+        copy.start()
+        copies.append(copy)
+        if with_places:
+            copy = pltpu.make_async_remote_copy(
+                places,
+                places_out.at[here],
+                place_send.at[step],
+                place_recv.at[step],
+                device_id={"replica": peer},
+                device_id_type=MESH,
+            )
+            copy.start()
+            copies.append(copy)
+    owns = [pltpu.make_async_copy(chunk.at[here], chunk_out.at[here], own.at[0])]
+    if with_places:
+        owns.append(pltpu.make_async_copy(places, places_out.at[here], own.at[1]))
+    for copy in owns:
+        copy.start()
+    stores = []
+    for i, load in enumerate(loads):
+        load.wait()
+        store = pltpu.make_async_copy(bounce[i], weights_out[i].at[group], weight_own.at[i])
+        store.start()
+        stores.append(store)
+    for copy in stores + owns:
+        copy.wait()
+    for copy in copies:
+        if isinstance(copy, tuple):
+            copy[0].wait_send()
+            copy[1].wait_recv()
+        else:
+            copy.wait()
+
+
+def exchange(ident, direction, chunk, last, places=None, weights=()):
+    peers = chunk.shape[0]
+    any_spec = pl.BlockSpec(memory_space=pl.ANY)
+    with_places = places is not None
+    args = [chunk, last] + ([places] if with_places else []) + list(weights)
+    shapes = [(chunk.shape, chunk.dtype), (last.shape, last.dtype)]
+    if with_places:
+        shapes.append(((peers,) + places.shape, places.dtype))
+    shapes += [((2,) + weight.shape, weight.dtype) for weight in weights]
+    dma = pltpu.SemaphoreType.DMA
+    scratch = [dma((peers,)), dma((peers,)), dma((2,)), dma((2,)), dma((2,))]
+    if with_places:
+        scratch += [dma((peers,)), dma((peers,))]
+    if weights:
+        count = len(weights)
+        scratch += [dma((count,)), dma((count,)), dma((count,))]
+        scratch += [pltpu.VMEM(weight.shape, weight.dtype) for weight in weights]
+    return pl.pallas_call(
+        functools.partial(exchange_body, direction, with_places, len(weights)),
+        out_shape=[jax.ShapeDtypeStruct(*shape) for shape in shapes],
+        in_specs=[any_spec] * len(args),
+        out_specs=[any_spec] * len(shapes),
+        scratch_shapes=scratch,
+        compiler_params=pltpu.CompilerParams(collective_id=ident, has_side_effects=True),
+        name=f"exchange{ident}",
+    )(*args)
+
+
+def share_body(count, *refs):
+    sources, results = refs[:count], refs[count : 2 * count]
+    send, recv, own = refs[2 * count : 2 * count + 3]
+    bounce = refs[2 * count + 3 :]
+    group = lax.axis_index("group")
+    barrier = pltpu.get_barrier_semaphore()
+    pl.semaphore_signal(barrier, inc=1, device_id={"group": 1 - group}, device_id_type=MESH)
+    pl.semaphore_wait(barrier, 1)
+    copies, loads, stores = [], [], []
+    for i in range(count):
+        copy = pltpu.make_async_remote_copy(
+            sources[i],
+            results[i].at[group],
+            send.at[i],
+            recv.at[i],
+            device_id={"group": 1 - group},
+            device_id_type=MESH,
+        )
+        copy.start()
+        copies.append(copy)
+        load = pltpu.make_async_copy(sources[i], bounce[i], own.at[i])
+        load.start()
+        loads.append(load)
+    for i in range(count):
+        loads[i].wait()
+        store = pltpu.make_async_copy(bounce[i], results[i].at[group], own.at[i])
+        store.start()
+        stores.append(store)
+    for copy in stores + copies:
+        copy.wait()
+
+
+def share(ident, *arrays):
+    count = len(arrays)
+    any_spec = pl.BlockSpec(memory_space=pl.ANY)
+    dma = pltpu.SemaphoreType.DMA
+    return pl.pallas_call(
+        functools.partial(share_body, count),
+        out_shape=[jax.ShapeDtypeStruct((2,) + a.shape, a.dtype) for a in arrays],
+        in_specs=[any_spec] * count,
+        out_specs=[any_spec] * count,
+        scratch_shapes=[dma((count,)), dma((count,)), dma((count,))]
+        + [pltpu.VMEM(a.shape, a.dtype) for a in arrays],
+        compiler_params=pltpu.CompilerParams(collective_id=ident, has_side_effects=True),
+        name=f"share{ident}",
+    )(*arrays)
+
+
+BLOCK = 256
+
+
+def unpack_units(got, last, rows_at, query_out):
+    peers = got.shape[0]
+    half = BLOCK // 128
+    for m in range(2):
+        for s in range(peers):
+            query_out[m * (peers // half) + s // half, :, (s % half) * 128 : (s % half + 1) * 128] = got[
+                s, rows_at : rows_at + 64, m * 128 : (m + 1) * 128
+            ]
+    extra = 2 * (peers // half)
+    for j in range(2):
+        query_out[extra, :, j * 128 : (j + 1) * 128] = last[j]
+
+
+def unit_source(got, u, s, first):
+    if u < 2:
+        return got[s, first : first + 64, u * 128 : (u + 1) * 128]
+    at = 0 if first == 64 else 128
+    return got[s, 192:256, at : at + 128]
+
+
+def attend_body(got, last, limit, places, sent, last_sent, out_f, lse, keys, values, queries, outs):
+    peers = got.shape[0]
+    nblocks = queries.shape[0]
+    per_unit = (nblocks - 1) // 2
+    unpack_units(got, last, 0, queries)
+    for u in range(3):
+        for s in range(peers):
+            span = slice(s * 128, (s + 1) * 128)
+            keys[u, span, :] = unit_source(got, u, s, 64).T
+            values[u, :, span] = unit_source(got, u, s, 128)
+
+    def block(b, carry):
+        u = b // per_unit
+        scores = jnp.dot(keys[u], queries[b], preferred_element_type=jnp.float32)
+        place = places[u]
+        place = jnp.concatenate([place, place], axis=1)
+        scores = jnp.where(place < limit[b], scores, -1e30)
+        high = jnp.max(scores, axis=0, keepdims=True)
+        expo = jnp.exp(scores - high)
+        total = jnp.sum(expo, axis=0, keepdims=True)
+        summed = jnp.dot(values[u], expo.astype(jnp.bfloat16), preferred_element_type=jnp.float32)
+        result = summed / total
+        out_f[b] = result
+        outs[b] = result.astype(jnp.bfloat16)
+        lse[b] = high + jnp.log(total)
+        return carry
+
+    lax.fori_loop(0, nblocks, block, 0)
+    half = BLOCK // 128
+    for m in range(2):
+        for s in range(peers):
+            sent[s, :, m * 128 : (m + 1) * 128] = outs[
+                m * per_unit + s // half, :, (s % half) * 128 : (s % half + 1) * 128
+            ]
+    for j in range(2):
+        last_sent[j] = outs[nblocks - 1, :, j * 128 : (j + 1) * 128]
+
+
+def attend(got, last, limit, places):
+    peers = got.shape[0]
+    nblocks = limit.shape[0]
+    length = places.shape[1]
+    bf, f32 = jnp.bfloat16, jnp.float32
+    return pl.pallas_call(
+        attend_body,
+        out_shape=[
+            jax.ShapeDtypeStruct((peers, 64, 256), bf),
+            jax.ShapeDtypeStruct((2, 64, 128), bf),
+            jax.ShapeDtypeStruct((nblocks, 64, BLOCK), f32),
+            jax.ShapeDtypeStruct((nblocks, 1, BLOCK), f32),
+        ],
+        scratch_shapes=[
+            pltpu.VMEM((3, length, 64), bf),
+            pltpu.VMEM((3, 64, length), bf),
+            pltpu.VMEM((nblocks, 64, BLOCK), bf),
+            pltpu.VMEM((nblocks, 64, BLOCK), bf),
+        ],
+        compiler_params=pltpu.CompilerParams(vmem_limit_bytes=56 << 20),
+        name="attend",
+    )(got, last, limit, places)
+
+
+def attend_grad_body(
+    got,
+    last,
+    limit,
+    places,
+    out_f,
+    lse,
+    grad_got,
+    grad_last,
+    sent,
+    last_sent,
+    keys,
+    keys_t,
+    values,
+    queries,
+    grads,
+    queries_n,
+    grads_n,
+    dqs,
+    dk,
+    dv,
+):
+    peers = got.shape[0]
+    nblocks = queries.shape[0]
+    per_unit = (nblocks - 1) // 2
+    unpack_units(got, last, 0, queries)
+    unpack_units(grad_got, grad_last, 0, grads)
+    for u in range(3):
+        for s in range(peers):
+            span = slice(s * 128, (s + 1) * 128)
+            part = unit_source(got, u, s, 64)
+            keys[u, span, :] = part.T
+            keys_t[u, :, span] = part
+            values[u, span, :] = unit_source(got, u, s, 128).T
+    for b in range(nblocks):
+        queries_n[b] = queries[b].T
+        grads_n[b] = grads[b].T
+    dk[...] = jnp.zeros_like(dk)
+    dv[...] = jnp.zeros_like(dv)
+
+    def block(b, carry):
+        u = b // per_unit
+        grad = grads[b]
+        delta = jnp.sum(grad.astype(jnp.float32) * out_f[b], axis=0, keepdims=True)
+        scores = jnp.dot(keys[u], queries[b], preferred_element_type=jnp.float32)
+        place = places[u]
+        place = jnp.concatenate([place, place], axis=1)
+        scores = jnp.where(place < limit[b], scores, -1e30)
+        probs = jnp.exp(scores - lse[b])
+        grad_probs = jnp.dot(values[u], grad, preferred_element_type=jnp.float32)
+        grad_scores = (probs * (grad_probs - delta)).astype(jnp.bfloat16)
+        dqs[b] = jnp.dot(keys_t[u], grad_scores, preferred_element_type=jnp.float32)
+        dk[u] += jnp.dot(grad_scores, queries_n[b], preferred_element_type=jnp.float32)
+        dv[u] += jnp.dot(probs.astype(jnp.bfloat16), grads_n[b], preferred_element_type=jnp.float32)
+        return carry
+
+    lax.fori_loop(0, nblocks, block, 0)
+    half = BLOCK // 128
+    scale = HEAD_DIM ** (-0.5)
+    for m in range(2):
+        for s in range(peers):
+            at = slice(m * 128, (m + 1) * 128)
+            span = slice(s * 128, (s + 1) * 128)
+            dq = dqs[m * per_unit + s // half, :, (s % half) * 128 : (s % half + 1) * 128]
+            sent[s, 0:64, at] = (dq * scale).astype(jnp.bfloat16)
+            sent[s, 64:128, at] = dk[m, span, :].T.astype(jnp.bfloat16)
+            sent[s, 128:192, at] = dv[m, span, :].T.astype(jnp.bfloat16)
+    for s in range(peers):
+        span = slice(s * 128, (s + 1) * 128)
+        sent[s, 192:256, 0:128] = dk[2, span, :].T.astype(jnp.bfloat16)
+        sent[s, 192:256, 128:256] = dv[2, span, :].T.astype(jnp.bfloat16)
+    for j in range(2):
+        last_sent[j] = (dqs[nblocks - 1, :, j * 128 : (j + 1) * 128] * scale).astype(jnp.bfloat16)
+
+
+def attend_grad(got, last, limit, places, out_f, lse, grad_got, grad_last):
+    peers = got.shape[0]
+    nblocks = limit.shape[0]
+    length = places.shape[1]
+    bf, f32 = jnp.bfloat16, jnp.float32
+    return pl.pallas_call(
+        attend_grad_body,
+        out_shape=[
+            jax.ShapeDtypeStruct((peers, 256, 256), bf),
+            jax.ShapeDtypeStruct((2, 64, 128), bf),
+        ],
+        scratch_shapes=[
+            pltpu.VMEM((3, length, 64), bf),
+            pltpu.VMEM((3, 64, length), bf),
+            pltpu.VMEM((3, length, 64), bf),
+            pltpu.VMEM((nblocks, 64, BLOCK), bf),
+            pltpu.VMEM((nblocks, 64, BLOCK), bf),
+            pltpu.VMEM((nblocks, BLOCK, 64), bf),
+            pltpu.VMEM((nblocks, BLOCK, 64), bf),
+            pltpu.VMEM((nblocks, 64, BLOCK), f32),
+            pltpu.VMEM((3, length, 64), f32),
+            pltpu.VMEM((3, length, 64), f32),
+        ],
+        compiler_params=pltpu.CompilerParams(vmem_limit_bytes=60 << 20),
+        name="attend_grad",
+    )(got, last, limit, places, out_f, lse, grad_got, grad_last)
+
+
+def split_last(array):
+    return jnp.stack([array[:, :128], array[:, 128:]])
+
+
+def per_device_heads(
+    tokens,
+    out_grad,
+    positions,
+    prefix,
+    ln1_gain,
+    ln1_bias,
+    w_qkv,
+    b_query,
+    b_value,
+    w_attn_out,
+    b_attn_out,
+    ln2_gain,
+    ln2_bias,
+    w_fc,
+    b_fc,
+    w_proj,
+    b_proj,
+):
+    bf, f32 = jnp.bfloat16, jnp.float32
+    micro, _, rows_here, width = tokens.shape
+    peers = lax.axis_size("replica")
+    hidden_width = 2 * b_fc.shape[0]
+    half = peers // 2
+    count = micro * rows_here
+    here = lax.axis_index("replica")
+    scale = HEAD_DIM ** (-0.5)
+    split = (peers * HEAD_DIM, width)
+
+    small = jnp.concatenate(
+        [ln1_gain, ln1_bias, b_query, b_value, b_attn_out, ln2_gain, ln2_bias, b_proj, b_fc]
+    ).reshape(1, -1)
+    mat_qkv, vectors = share(1, w_qkv, small)
+    mat_qkv = mat_qkv.reshape(width, 3 * width)
+    vectors = vectors[:, 0].astype(f32)
+    part = width // 2
+    gain_one, shift_one, bias_query, bias_value, bias_out, gain_two, shift_two, bias_proj = (
+        vectors[:, i * part : (i + 1) * part].reshape(width) for i in range(8)
+    )
+    bias_fc = vectors[:, 8 * part :].reshape(hidden_width)
+
+    rows_in = tokens.reshape(count, width).astype(f32)
+    normed_one, norm_one_pull = jax.vjp(norm_rows, rows_in, gain_one, shift_one)
+    first = normed_one.astype(bf)
+    joined = contract(mat_qkv, first, 0, 1)
+    bias_all = jnp.concatenate([bias_query, jnp.zeros_like(bias_query), bias_value])
+    joined = joined + bias_all[:, None]
+    queries = ((joined[:width]).astype(bf).astype(f32) * scale).astype(bf)
+    keys = joined[width : 2 * width].astype(bf)
+    values = joined[2 * width :].astype(bf)
+    cut = split[0]
+    main = [part_[:cut].reshape(peers, HEAD_DIM, count) for part_ in (queries, keys, values)]
+    key_last, value_last = keys[cut:], values[cut:]
+    tails = jnp.stack(
+        [
+            jnp.concatenate(
+                [key_last[:, m * 128 : (m + 1) * 128], value_last[:, m * 128 : (m + 1) * 128]], 1
+            )
+            for m in range(2)
+        ]
+    )
+    tails = jnp.repeat(tails, half, axis=0)
+    chunk = jnp.concatenate(main + [tails], axis=1)
+    got, got_last, all_places, mat_out, mat_fc, mat_proj = exchange(
+        2,
+        1,
+        chunk,
+        split_last(queries[cut:]),
+        positions.reshape(micro, rows_here),
+        (w_attn_out, w_fc, w_proj),
+    )
+    mat_out = mat_out.reshape(width, width)
+    mat_fc = mat_fc.reshape(width, hidden_width)
+    mat_proj = mat_proj.reshape(hidden_width, width)
+
+    place_rows = jnp.transpose(all_places, (1, 0, 2)).reshape(micro, peers * rows_here)
+    limits = jnp.maximum(place_rows + 1, prefix.reshape(micro, 1))
+    mine = here // half
+    at = lax.rem(here - 1 + peers, half)
+    own_limits = lax.dynamic_index_in_dim(limits, mine, 0, False).reshape(peers, rows_here)
+    own_limits = jnp.concatenate(
+        [
+            lax.dynamic_index_in_dim(own_limits, at, 0, True),
+            lax.dynamic_index_in_dim(own_limits, at + half, 0, True),
+        ],
+        1,
+    )
+    limit = jnp.concatenate([limits.reshape(-1, BLOCK), own_limits], 0)[:, None, :]
+    unit_places = jnp.concatenate(
+        [place_rows, lax.dynamic_index_in_dim(place_rows, mine, 0, True)], 0
+    )
+    unit_places = jnp.broadcast_to(unit_places[:, :, None], unit_places.shape + (128,))
+
+    sent, sent_last, out_f, lse = attend(got, got_last, limit, unit_places)
+    heads_out, heads_last = exchange(3, -1, sent, sent_last)
+    attended = jnp.concatenate(
+        [heads_out.reshape(cut, count), jnp.concatenate([heads_last[0], heads_last[1]], 1)], 0
+    )
+
+    middle = rows_in + contract(attended, mat_out, 0, 0) + bias_out
+    normed_two, norm_two_pull = jax.vjp(norm_rows, middle, gain_two, shift_two)
+    second = normed_two.astype(bf)
+    hidden_in = jnp.dot(second, mat_fc, preferred_element_type=f32) + bias_fc
+    hidden_f, gelu_pull = jax.vjp(gelu_tanh, hidden_in)
+    hidden = hidden_f.astype(bf)
+    output_rows = middle + jnp.dot(hidden, mat_proj, preferred_element_type=f32) + bias_proj
+    result = output_rows.astype(bf).reshape(micro, 1, rows_here, width)
+
+    grad_low = out_grad.reshape(count, width)
+    grad_top = grad_low.astype(f32)
+    grad_bias_proj = jnp.sum(grad_top, 0)
+    grad_mat_proj = contract(hidden, grad_low, 0, 0)
+    (grad_hidden_in,) = gelu_pull(times_transposed(grad_low, mat_proj))
+    grad_hidden_in = grad_hidden_in.astype(bf)
+    grad_bias_fc = jnp.sum(grad_hidden_in, 0, dtype=f32)
+    grad_mat_fc = contract(second, grad_hidden_in, 0, 0)
+    grad_second = times_transposed(grad_hidden_in, mat_fc)
+    grad_middle_norm, grad_gain_two, grad_shift_two = norm_two_pull(grad_second)
+    grad_middle = grad_top + grad_middle_norm
+    grad_bias_out = jnp.sum(grad_middle, 0)
+    grad_branch = grad_middle.astype(bf)
+    grad_mat_out = contract(attended, grad_branch, 1, 0)
+    grad_attended = contract(mat_out, grad_branch, 1, 1).astype(bf)
+
+    grad_got, grad_got_last = exchange(
+        4, 1, grad_attended[:cut].reshape(peers, HEAD_DIM, count), split_last(grad_attended[cut:])
+    )
+    grad_sent, grad_sent_last = attend_grad(
+        got, got_last, limit, unit_places, out_f, lse, grad_got, grad_got_last
+    )
+    back, back_last = exchange(5, -1, grad_sent, grad_sent_last)
+    last_parts = back[:, 192:256, :].astype(f32).reshape(2, half, HEAD_DIM, 256)
+    last_sums = jnp.sum(last_parts, 1).astype(bf)
+    grad_query = jnp.concatenate(
+        [back[:, 0:64].reshape(cut, count), jnp.concatenate([back_last[0], back_last[1]], 1)], 0
+    )
+    grad_key = jnp.concatenate(
+        [
+            back[:, 64:128].reshape(cut, count),
+            jnp.concatenate([last_sums[0, :, :128], last_sums[1, :, :128]], 1),
+        ],
+        0,
+    )
+    grad_value = jnp.concatenate(
+        [
+            back[:, 128:192].reshape(cut, count),
+            jnp.concatenate([last_sums[0, :, 128:], last_sums[1, :, 128:]], 1),
+        ],
+        0,
+    )
+    grad_bias_query = jnp.sum(grad_query, 1, dtype=f32)
+    grad_bias_value = jnp.sum(grad_value, 1, dtype=f32)
+    grad_joined = jnp.concatenate([grad_query, grad_key, grad_value], 0)
+    grad_mat_qkv = contract(first, grad_joined, 0, 1)
+    grad_first = contract(grad_joined, mat_qkv, 0, 1)
+    grad_rows_norm, grad_gain_one, grad_shift_one = norm_one_pull(grad_first)
+    tokens_grad = (grad_middle + grad_rows_norm).astype(bf).reshape(micro, 1, rows_here, width)
+
+    matrices = reduce_grads((grad_mat_qkv, grad_mat_out, grad_mat_fc, grad_mat_proj))
+    small_grads = jnp.concatenate(
+        [
+            item.reshape(2, -1)
+            for item in (
+                grad_gain_one,
+                grad_shift_one,
+                grad_bias_query,
+                grad_bias_value,
+                grad_bias_out,
+                grad_gain_two,
+                grad_shift_two,
+                grad_bias_proj,
+                grad_bias_fc,
+            )
+        ],
+        1,
+    )
+    small_grads = lax.psum(small_grads, ("group", "replica"))
+    small_own = lax.dynamic_index_in_dim(small_grads, lax.axis_index("group"), 0, False)
+    vec = [small_own[i * part : (i + 1) * part] for i in range(8)] + [small_own[8 * part :]]
+    return (
+        result,
+        tokens_grad,
+        vec[0],
+        vec[1],
+        matrices[0],
+        vec[2],
+        vec[3],
+        matrices[1],
+        vec[4],
+        vec[5],
+        vec[6],
+        matrices[2],
+        vec[8],
+        matrices[3],
+        vec[7],
+    )
+
+
+def specs():
+    wide = P(None, "group", "replica", None)
+    row, mat = P("group"), P("group", None)
+    in_specs = (wide, wide, P(None, "group", "replica"), P(None, "group"))
+    in_specs += (row, row, mat, row, row, mat, row, row, row, mat, row, mat, row)
+    out_specs = (wide, wide, row, row, mat, row, row, mat, row, row, row, mat, row, mat, row)
+    return in_specs, out_specs
+
+
 def solution(mesh):
-    in_specs = (
-        P(None, "group", "replica", None),
-        P(None, "group", "replica", None),
-        P(None, "group", "replica"),
-        P(None, "group"),
-        P("group"),
-        P("group"),
-        P("group", None),
-        P("group"),
-        P("group"),
-        P("group", None),
-        P("group"),
-        P("group"),
-        P("group"),
-        P("group", None),
-        P("group"),
-        P("group", None),
-        P("group"),
-    )
-    out_specs = (
-        P(None, "group", "replica", None),
-        P(None, "group", "replica", None),
-        P("group"),
-        P("group"),
-        P("group", None),
-        P("group"),
-        P("group"),
-        P("group", None),
-        P("group"),
-        P("group"),
-        P("group"),
-        P("group", None),
-        P("group"),
-        P("group", None),
-        P("group"),
-    )
+    by_heads = mesh.shape["replica"] == HEADS - 1 and mesh.shape["group"] == 2
+    in_specs, out_specs = specs()
     return jax.shard_map(
-        per_device, mesh=mesh, in_specs=in_specs, out_specs=out_specs, check_vma=False
-    )
+        per_device_heads if by_heads else per_device_gather,
+        mesh=mesh,
+        in_specs=in_specs,
+        out_specs=out_specs,
+        check_vma=False,
+    )

time: 1730 us -> 802 us (0.46)
  waiting for transfers between devices: 1000 us -> 373 us
  matrix products: 277 us -> 72.8 us
  Pallas kernels: 0 us -> 194 us
  local copies, waits for them, and re-layouts: 211 us -> 69.2 us
  blocking collectives: 133 us -> 45.2 us
  other arithmetic: 77.2 us -> 27.9 us
    unnamed x22 -> x6, waiting for transfers between devices: 388 us -> 0.1 us
    all_gather x8 -> x0, waiting for transfers between devices: 283 us -> none  [the longest x2 154 us: per_device(): lax.all_gather(values, 'replica', axis=0, tiled=True)]
    pallas_call x0 -> x7, Pallas kernels: none -> 194 us  [the longest x4 130 us: exchange(): pl.pallas_call(functools.partial(exchange_body, direction, with_places, l...]
    dot_general x72 -> x10, matrix products: 245 us -> 54.4 us  [the longest x8 37.9 us: contract(): lax.dot_general(left, right, (((left_dim,), (right_dim,)), ((), ())), pre...]
    unnamed x249 -> x48, local copies, waits for them, and re-layouts: 105 us -> 42.3 us
    psum x1, waiting for transfers between devices: 285 us -> 338 us  [reduce_grads(): lax.psum(for_sending(owned), 'replica')]
    all_gather x2 -> x0, blocking collectives: 43.7 us -> none  [the longest x1 41.6 us: per_device(): all_places = lax.all_gather(positions, 'replica', axis=2, tiled=True)]
    psum x1, blocking collectives: 81.8 us -> 45.2 us  [per_device_heads(): small_grads = lax.psum(small_grads, ('group', 'replica'))]
  transfers between devices with their start and end apart: 17 -> 5, of which waited for: 13 -> 3; matrix products, arithmetic and copies ran while one was open for 24% -> 10% of each run, Pallas kernels for 0% -> 11%
where the time goes in v1:
time: 802 us; the launch traced here: 797 us
  waiting for transfers between devices  373 us (47%)
  Pallas kernels  194 us (24%)
  matrix products  72.8 us (9%)
  local copies, waits for them, and re-layouts  69.2 us (9%)
  blocking collectives  45.2 us (6%)
  other arithmetic  27.9 us (3%)
  between operations  14.7 us (2%)
    psum x1, waiting for transfers between devices, reduce_grads(): lax.psum(for_sending(owned), 'replica')  338 us
    pallas_call x4, Pallas kernels, exchange(): pl.pallas_call(functools.partial(exchange_body, direction, with_places, l...  130 us
    psum x1, blocking collectives, per_device_heads(): small_grads = lax.psum(small_grads, ('group', 'replica'))  45.2 us
    unnamed x48, local copies, waits for them, and re-layouts  42.3 us
    dot_general x8, matrix products, contract(): lax.dot_general(left, right, (((left_dim,), (right_dim,)), ((), ())), pre...  37.9 us
    reduce_scatter x3, waiting for transfers between devices, reduce_grads(): lax.psum_scatter(for_sending(terms), 'group', scatter_dimension=0, tiled=...  34.5 us
    pallas_call x1, Pallas kernels, attend_grad(): pl.pallas_call(attend_grad_body, out_shape=[jax.ShapeDtypeStruct((peers,...  33.4 us
    pallas_call x1, Pallas kernels, attend(): pl.pallas_call(attend_body, out_shape=[jax.ShapeDtypeStruct((peers, 64, 2...  24.4 us
  transfers between devices with their start and end apart: 5, of which 3 were waited for; matrix products, arithmetic and copies ran while one was open for 10% of the time, Pallas kernels for 11%

profile of v1, /device:TPU:0, one launch (start us, length us, event | category | flops | bytes accessed | tf_op | source)
XLA Modules:
  0.0 796.9 jit_solution(4204998812698421968)
XLA Ops:
  7.2 6.2 concatenate.52
  13.5 0.6 reshape.272.refs_1_
  14.1 6.9 share1.1
  21.0 0.8 copy.94
  22.4 0.4 add_convert_fusion.3
  22.8 0.3 copy.53
  23.4 5.6 fusion
  29.2 5.1 copy.52
  34.4 8.2 %copy.54.refs_5_ = bf16[2176,1088]{1,0:T(8,128)(2,1)} copy(bf16[2176,1088]{0,1:T(8,128)(2,1)} %param.32) | data formatting | bytes 9469952 | tf_op args[15]
  42.7 0.6 pad_maximum_fusion.2.refs_1_
  43.4 1.5 pad_maximum_fusion.refs_0_
  44.9 43.9 %exchange2.1 = (bf16[16,256,256]{2,1,0:T(8,128)(2,1)}, bf16[2,64,128]{2,1,0:T(8,128)(2,1)}, s32[16,2,128]{2,1,0:T(2,128)}, bf16[2,544,1088]{2,1,0:T(8,128)(2,1)}...) custom-call(bf16[16,256,256]{2,1,0:T(8,128)(2,1)} %pad_maximum_fusion.refs_0_, ...), custom_call_target="tpu_custom_call" | custom-call | tf_op jit(solution)/shard_map/exchange2/pallas_call | solution.py:452
  88.7 0.7 bitcast_add_fusion
  89.5 0.6 dynamic-slice
  90.2 1.4 add_maximum_fusion
  91.7 0.6 broadcast_in_dim.34.limit
  92.3 0.7 pad_add_fusion
  93.1 2.6 broadcast_in_dim.35.places
  95.7 24.4 %attend.1 = (bf16[16,64,256]{2,1,0:T(8,128)(2,1)}, bf16[2,64,128]{2,1,0:T(8,128)(2,1)}, f32[17,64,256]{2,1,0:T(8,128)}, f32[17,1,256]{2,1,0:T(1,128)}) custom-call(bf16[16,256,256]{2,1,0:T(8,128)(2,1)} %get-tuple-element.37.got, bf16[2,64,128]{2,1,0:T(8,128)(2,1)} %get-tuple-element.38.last, s32[17,1,256]{2,1,0:T(1,128)} %broadcast_in_dim.34.limit, ...), custom_call_target="tpu_custom_call" | custom-call | tf_op jit(solution)/shard_map/attend/pallas_call | solution.py:577
  120.1 28.3 %exchange3.1 = (bf16[16,64,256]{2,1,0:T(8,128)(2,1)}, bf16[2,64,128]{2,1,0:T(8,128)(2,1)}) custom-call(bf16[16,64,256]{2,1,0:T(8,128)(2,1)} %get-tuple-element.40.refs_0_, bf16[2,64,128]{2,1,0:T(8,128)(2,1)} %get-tuple-element.41.refs_1_), custom_call_target="tpu_custom_call" | custom-call | tf_op jit(solution)/shard_map/exchange3/pallas_call | solution.py:452
  148.4 0.7 slice_bitcast_fusion.11
  149.3 3.2 fusion.35
  152.7 4.6 copy.57
  157.3 6.3 convolution_add_fusion
  163.6 2.0 copy-done.6
  165.6 5.6 convolution_convert_fusion
  171.2 13.9 %copy.60 = bf16[4352,1088]{1,0:T(8,128)(2,1)} copy(bf16[4352,1088]{0,1:T(8,128)(2,1)} %convolution_convert_fusion) | data formatting | bytes 18939904
  185.2 9.2 %convert_reduce_fusion = (f32[4352]{0:T(1024)S(1)}, bf16[256,4352]{1,0:T(8,128)(2,1)S(1)}) fusion(f32[256,4352]{1,0:T(8,128)} %copy-done.6, bf16[4352,1088]{1,0:T(8,128)(2,1)} %bitcast.149, bf16[136,8,2,128]{3,2,1,0:T(2,128)(2,1)S(1)} %bitcast.132), kind=kOutput, calls=%fused_computation.17 | convolution fusion | flops 2448813824 | bytes 16729088 | tf_op jit(solution)/shard_map/dot_general | solution.py:40
  194.4 9.2 %fusion.28 = (f32[1088]{0:T(1024)S(1)}, f32[256]{0:T(256)S(1)}, f32[256,1088]{0,1:T(8,128)S(1)}) fusion(f32[1088]{0:T(1024)S(1)} %mul.182, f32[256,1088]{0,1:T(8,128)S(1)} %get-tuple-element.175, f32[256]{0:T(256)S(1)} %broadcast_multiply_fusion, bf16[256,4352]{1,0:T(8,128)(2,1)S(1)} %get-tuple-element.179, bf16[1088,4352]{1,0:T(8,128)(2,1)} %bitcast.124), kind=kOutput, calls=%fused_computation.115 | convolution fusion | flops 2425699072 | bytes 13937152 | tf_op jit(solution)/shard_map/dot_general | solution.py:40
  203.6 0.6 multiply_reduce_fusion
  204.3 0.4 copy-done.12
  204.7 0.6 fusion.30
  205.3 0.5 copy-done.14
  205.8 2.4 convolution_convert_fusion.3
  208.2 2.6 convolution_convert_fusion.4
  210.8 0.8 slice.250
  211.7 0.6 pad_maximum_fusion.3.refs_1_
  212.3 16.2 %exchange4.1 = (bf16[16,64,256]{2,1,0:T(8,128)(2,1)}, bf16[2,64,128]{2,1,0:T(8,128)(2,1)}) custom-call(bf16[16,64,256]{2,1,0:T(8,128)(2,1)} %bitcast.134, bf16[2,64,128]{2,1,0:T(8,128)(2,1)} %pad_maximum_fusion.3.refs_1_), custom_call_target="tpu_custom_call" | custom-call | tf_op jit(solution)/shard_map/exchange4/pallas_call | solution.py:452
  228.5 33.4 %attend_grad.1 = (bf16[16,256,256]{2,1,0:T(8,128)(2,1)}, bf16[2,64,128]{2,1,0:T(8,128)(2,1)}) custom-call(bf16[16,256,256]{2,1,0:T(8,128)(2,1)} %get-tuple-element.37.got, bf16[2,64,128]{2,1,0:T(8,128)(2,1)} %get-tuple-element.38.last, s32[17,1,256]{2,1,0:T(1,128)} %broadcast_in_dim.34.limit, s32[3,2048,128]{2,1,0:T(8,128)} %broadcast_in_dim.35.places, ...), custom_call_target="tpu_custom_call" | custom-call | tf_op jit(solution)/shard_map/attend_grad/pallas_call | solution.py:676
  261.9 41.2 %exchange5.1 = (bf16[16,256,256]{2,1,0:T(8,128)(2,1)}, bf16[2,64,128]{2,1,0:T(8,128)(2,1)}) custom-call(bf16[16,256,256]{2,1,0:T(8,128)(2,1)} %get-tuple-element.51.refs_0_, bf16[2,64,128]{2,1,0:T(8,128)(2,1)} %get-tuple-element.52.refs_1_), custom_call_target="tpu_custom_call" | custom-call | tf_op jit(solution)/shard_map/exchange5/pallas_call | solution.py:452
  303.1 1.5 fusion.31
  304.8 1.4 bitcast_reduce_fusion
  306.3 6.1 fusion.29
  312.4 5.2 convolution_convert_fusion.2
  317.7 7.2 convolution_convert_fusion.1
  325.0 8.6 %copy.61 = bf16[2176,1088]{0,1:T(8,128)(2,1)} copy(bf16[2176,1088]{1,0:T(8,128)(2,1)} %reduce-scatter.13.cloned.1.call-done) | data formatting | bytes 9469952
  333.6 13.2 %reduce-scatter.7.cloned.1.call-done = bf16[544,3264]{1,0:T(8,128)(2,1)} async-done(((bf16[1088,3264]{1,0:T(8,128)(2,1)}), bf16[544,3264]{1,0:T(8,128)(2,1)}) %reduce-scatter.7.cloned.1.call-update) | async-done | bytes 3551248 | tf_op jit(solution)/shard_map/reduce_scatter | solution.py:54
  346.8 21.3 %reduce-scatter.11.cloned.1.call-done = bf16[544,4352]{1,0:T(8,128)(2,1)} async-done(((bf16[1088,4352]{1,0:T(8,128)(2,1)}), bf16[544,4352]{1,0:T(8,128)(2,1)}) %reduce-scatter.11.cloned.1.call-update) | async-done | bytes 4734992 | tf_op jit(solution)/shard_map/reduce_scatter | solution.py:54
  368.2 10.2 %fusion.10 = bf16[256,1088]{0,1:T(8,128)(2,1)} fusion(f32[256,1088]{0,1:T(8,128)S(1)} %get-tuple-element.175, bf16[4352,1088]{1,0:T(8,128)(2,1)} %bitcast.150, f32[1088]{0:T(1024)S(1)} %add.197, f32[256,4352]{1,0:T(8,128)} %copy-done.6), kind=kOutput, calls=%fused_computation.24 | convolution fusion | flops 2435170304 | bytes 15601920 | tf_op jit(solution)/shard_map/dot_general | solution.py:808
  378.5 2.5 reshape.287
  381.0 2.1 copy.58
  383.1 0.6 multiply_reduce_fusion.1
  383.7 1.2 add_convert_fusion.1
  384.9 1.9 reshape.295
  386.8 0.9 copy.59
  388.7 0.3 convert_reduce_fusion.1
  389.2 45.2 %psum.35 = f32[2,6528]{1,0:T(2,128)S(1)} all-reduce(f32[2,6528]{1,0:T(2,128)S(1)} %concatenate.68), channel_id=1, replica_groups=mesh['group'=2,'replica'=16] {'group','replica'}, use_global_device_ids=true, to_apply=%region_18.19 | all-reduce | flops 13056 | bytes 104448 | tf_op jit(solution)/shard_map/psum | solution.py:879
  434.4 0.7 dynamic-slice_reduce_fusion
  435.1 0.7 dynamic-slice_reduce_fusion.1
  435.8 338.0 %all-reduce.3.cloned.1.call-done = (bf16[544,3264]{1,0:T(8,128)(2,1)}, bf16[544,1088]{1,0:T(8,128)(2,1)}, bf16[544,4352]{1,0:T(8,128)(2,1)}, bf16[2176,1088]{0,1:T(8,128)(2,1)}) async-done(((bf16[544,3264]{1,0:T(8,128)(2,1)}, bf16[544,1088]{1,0:T(8,128)(2,1)}, bf16[544,4352]{1,0:T(8,128)(2,1)}, bf16[2176,1088]{0,1:T(8,128)(2,1)}), (bf16[544,3264]{1,0:T(8,128)(2,1)}, bf16[544,1088]{1,0:T(8,128)(2,1)}, ...) | async-done | bytes 14204944 | tf_op jit(solution)/shard_map/psum | solution.py:57
  773.7 5.7 convert_element_type.130
  779.5 1.6 convert_element_type.132
  781.1 4.5 convert_element_type.134
  785.6 4.4 convert_element_type.136
  (108 shorter events, 3.7 us)
Async XLA Ops:
  7.2 317.8 %reduce-scatter.13.cloned.1.call-start = ((), (), s32[]{:S(2)}) async-start(), calls=%async_computation.7 | async-start | bytes 15040512
  14.1 8.0 %copy-start = (bf16[2,1,128,1088]{2,3,1,0:T(8,128)(2,1)S(1)}, bf16[2,1,128,1088]{2,3,1,0:T(8,128)(2,1)}, u32[]{:S(2)}) copy-start(bf16[2,1,128,1088]{2,3,1,0:T(8,128)(2,1)} %param.17) | copy-start | bytes 1671172
  44.9 44.6 %copy-start.16 = (s32[2,1]{0,1:T(1,128)S(1)}, s32[2,1]{0,1:T(1,128)}, u32[]{:S(2)}) copy-start(s32[2,1]{0,1:T(1,128)} %param.20) | copy-start | bytes 28
  149.3 3.4 copy-start.9
  157.3 27.9 %copy-start.11 = (bf16[2,1,128,1088]{2,0,3,1:T(2,128)(2,1)}, bf16[2,1,128,1088]{2,0,3,1:T(2,128)(2,1)S(1)}, u32[]{:S(2)}) copy-start(bf16[2,1,128,1088]{2,0,3,1:T(2,128)(2,1)S(1)} %copy.57) | copy-start | bytes 1671172
  163.6 2.0 copy-start.6
  185.1 148.5 %reduce-scatter.9.cloned.1.call-start = ((), (), s32[]{:S(2)}) async-start(), calls=%async_computation.5 | async-start | bytes 3760128 | tf_op jit(solution)/shard_map/reduce_scatter | solution.py:54
  194.4 9.2 %copy-start.8 = (bf16[256,4352]{1,0:T(8,128)(2,1)}, bf16[256,4352]{1,0:T(8,128)(2,1)S(1)}, u32[]{:S(2)}) copy-start(bf16[256,4352]{1,0:T(8,128)(2,1)S(1)} %get-tuple-element.179) | copy-start | bytes 6684676
  203.6 1.1 copy-start.12
  204.7 1.1 copy-start.14
  208.2 138.6 %reduce-scatter.7.cloned.1.call-start = ((), (), s32[]{:S(2)}) async-start(), calls=%async_computation.4 | async-start | bytes 10862592 | tf_op jit(solution)/shard_map/reduce_scatter | solution.py:54
  303.1 1.6 copy-start.15
  304.7 1.6 copy-start.2
  304.7 1.6 copy-start.4
  317.7 50.4 %reduce-scatter.11.cloned.1.call-start = ((), (), s32[]{:S(2)}) async-start(), calls=%async_computation.6 | async-start | bytes 14204928 | tf_op jit(solution)/shard_map/reduce_scatter | solution.py:54
  325.0 448.8 %all-reduce.3.cloned.1.call-start = ((), (), s32[]{:S(2)}) async-start(), calls=%async_computation.8 | async-start | bytes 28688384 | tf_op jit(solution)/shard_map/psum | solution.py:57
  378.5 4.7 copy-start.7
  384.9 2.9 copy-start.5
  384.9 3.2 copy-start.3
  384.9 3.8 copy-start.10
  773.7 5.7 copy-start.13
  773.7 7.4 copy-start.1
  779.5 6.1 slice-start
  781.1 4.5 slice-start.1
Sparse Core Ops, SparseCore 0:
  185.2 20.6 reduce-scatter.12
  208.8 13.6 reduce-scatter.8
  317.8 28.9 reduce-scatter.6
  349.5 18.5 reduce-scatter.10
  375.0 398.7 all-reduce.2

commit v2 on v1

--- a/solution.py
+++ b/solution.py
@@ -330,8 +330,24 @@
     pl.semaphore_wait(barrier, peers - 1 + (1 if group_too else 0))
 
 
-def exchange_body(direction, with_places, nweights, *refs):
+def halves(ref, mode, which):
+    if mode == "whole":
+        return ref
+    if mode == "rows":
+        size = ref.shape[0] // 2
+        return ref.at[pl.ds(pl.multiple_of(which * size, 16), size)]
+    size = ref.shape[1] // 2
+    return ref.at[:, pl.ds(pl.multiple_of(which * size, 128), size)]
+
+
+def half_shape(array, mode):
+    rows, columns = array.shape
+    return {"whole": (rows, columns), "rows": (rows // 2, columns), "columns": (rows, columns // 2)}[mode]
+
+
+def exchange_body(direction, with_places, modes, *refs):
     refs = list(refs)
+    nweights = len(modes)
     chunk, last = refs.pop(0), refs.pop(0)
     places = refs.pop(0) if with_places else None
     weights = [refs.pop(0) for _ in range(nweights)]
@@ -351,7 +367,7 @@
     loads, copies = [], []
     for i in range(nweights):
         copy = pltpu.make_async_remote_copy(
-            weights[i],
+            halves(weights[i], modes[i], 1 - group),
             weights_out[i].at[group],
             weight_send.at[i],
             weight_recv.at[i],
@@ -360,7 +376,9 @@
         )
         copy.start()
         copies.append(copy)
-        load = pltpu.make_async_copy(weights[i], bounce[i], weight_own.at[i])
+        load = pltpu.make_async_copy(
+            halves(weights[i], modes[i], group), bounce[i], weight_own.at[i]
+        )
         load.start()
         loads.append(load)
     for slot in range(2):
@@ -432,15 +450,17 @@
             copy.wait()
 
 
-def exchange(ident, direction, chunk, last, places=None, weights=()):
+def exchange(ident, direction, chunk, last, places=None, shares=()):
     peers = chunk.shape[0]
+    weights = [array for array, _ in shares]
+    modes = [mode for _, mode in shares]
     any_spec = pl.BlockSpec(memory_space=pl.ANY)
     with_places = places is not None
     args = [chunk, last] + ([places] if with_places else []) + list(weights)
     shapes = [(chunk.shape, chunk.dtype), (last.shape, last.dtype)]
     if with_places:
         shapes.append(((peers,) + places.shape, places.dtype))
-    shapes += [((2,) + weight.shape, weight.dtype) for weight in weights]
+    shapes += [((2,) + half_shape(*item), item[0].dtype) for item in shares]
     dma = pltpu.SemaphoreType.DMA
     scratch = [dma((peers,)), dma((peers,)), dma((2,)), dma((2,)), dma((2,))]
     if with_places:
@@ -448,9 +468,9 @@
     if weights:
         count = len(weights)
         scratch += [dma((count,)), dma((count,)), dma((count,))]
-        scratch += [pltpu.VMEM(weight.shape, weight.dtype) for weight in weights]
+        scratch += [pltpu.VMEM(half_shape(*item), item[0].dtype) for item in shares]
     return pl.pallas_call(
-        functools.partial(exchange_body, direction, with_places, len(weights)),
+        functools.partial(exchange_body, direction, with_places, modes),
         out_shape=[jax.ShapeDtypeStruct(*shape) for shape in shapes],
         in_specs=[any_spec] * len(args),
         out_specs=[any_spec] * len(shapes),
@@ -696,6 +716,281 @@
     )(got, last, limit, places, out_f, lse, grad_got, grad_last)
 
 
+ROWS = 272
+PART = 80
+PADDED = 4 * PART
+
+
+def chunk_plan(wide_widths, tall_widths):
+    plan = []
+    for array in (2, 0, 1):
+        if array == 2:
+            for row in (0, ROWS):
+                start = 0
+                for width in tall_widths:
+                    plan.append((2, width, row, start))
+                    start += width
+        else:
+            start = 0
+            for width in wide_widths:
+                plan.append((array, width, 0, start))
+                start += width
+    return plan
+
+
+def piece(ref, item, first, second):
+    array, width, row, start = item
+    if array == 2:
+        at = first * (4 * ROWS) + second * (2 * ROWS) + row
+        return ref.at[pl.ds(pl.multiple_of(at, 16), ROWS), pl.ds(start, width)]
+    column = pl.multiple_of(second * 2176 + start, 128)
+    return ref.at[pl.ds(pl.multiple_of(first * ROWS, 16), ROWS), pl.ds(column, width)]
+
+
+def sum_grads_body(plan, *refs):
+    nchunks = len(plan)
+    sources, small, results, small_out = refs[0:3], refs[3], refs[4:7], refs[7]
+    refs = list(refs[8:])
+    own, came, second_in, quarter, parts, gathered, other = (
+        [refs.pop(0) for _ in range(nchunks)] for _ in range(7)
+    )
+    small_half, small_sum, small_all = (refs.pop(0) for _ in range(3))
+    (load_sem, s1, r1, s2, r2, s3, r3, s4, r4, s5, r5, s6, r6, store_sem, sp, rp, sa, ra) = refs
+    here, group = lax.axis_index("replica"), lax.axis_index("group")
+    peers = small_all.shape[0]
+    bit_x, bit_y, place = here % 2, (here // 2) % 2, here // 4
+    bit_one = bit_x + group * (bit_y - bit_x)
+    bit_two = bit_x + bit_y - bit_one
+    peer_one = here + (1 + group) * (1 - 2 * bit_one)
+    peer_two = here + (2 - group) * (1 - 2 * bit_two)
+    greet(peers, here, True)
+    pending = []
+
+    def send(source, target, send_sem, recv_sem, peer):
+        copy = pltpu.make_async_remote_copy(
+            source, target, send_sem, recv_sem, device_id={"replica": peer}, device_id_type=MESH
+        )
+        copy.start()
+        pending.append(copy)
+        return copy
+
+    small_copy = pltpu.make_async_remote_copy(
+        small.at[1 - group],
+        small_half,
+        sp,
+        rp,
+        device_id={"group": 1 - group},
+        device_id_type=MESH,
+    )
+    small_copy.start()
+    first_copies, loads = [], []
+    for c, item in enumerate(plan):
+        source = sources[item[0]]
+        group_of = []
+        for j in range(2):
+            group_of.append(
+                send(
+                    piece(source, item, 1 - bit_one, j),
+                    came[c].at[j],
+                    s1.at[c, j],
+                    r1.at[c, j],
+                    peer_one,
+                )
+            )
+        first_copies.append(group_of)
+        pair = []
+        for j in range(2):
+            load = pltpu.make_async_copy(
+                piece(source, item, bit_one, j), own[c].at[j], load_sem.at[c, j]
+            )
+            load.start()
+            pair.append(load)
+        loads.append(pair)
+    for c in range(nchunks):
+        quarter[c][ROWS:, :] = jnp.zeros((PADDED - ROWS, quarter[c].shape[1]), jnp.bfloat16)
+    small_copy.wait()
+    small_sum[...] = small[group] + small_half[...]
+    small_all[here] = small_sum[...]
+    small_copies = []
+    for step in range(1, peers):
+        copy = pltpu.make_async_remote_copy(
+            small_sum,
+            small_all.at[here],
+            sa.at[step],
+            ra.at[step],
+            device_id={"replica": lax.rem(here + step, peers)},
+            device_id_type=MESH,
+        )
+        copy.start()
+        small_copies.append(copy)
+
+    def by_rows(rows, fn):
+        lax.fori_loop(0, rows // 16, lambda i, carry: (fn(pl.ds(pl.multiple_of(i * 16, 16), 16)), carry)[1], 0)
+
+    second_copies, part_copies, gather_copies, other_copies, last_copies = {}, {}, {}, {}, {}
+    stores = []
+
+    def stage_one(c):
+        for j in range(2):
+            loads[c][j].wait()
+            first_copies[c][j].wait_recv()
+
+        def add(rows):
+            both = own[c][1 - bit_two, rows].astype(jnp.float32) + came[c][
+                1 - bit_two, rows
+            ].astype(jnp.float32)
+            own[c][1 - bit_two, rows] = both.astype(jnp.bfloat16)
+
+        by_rows(ROWS, add)
+        second_copies[c] = send(
+            own[c].at[1 - bit_two], second_in[c], s2.at[c], r2.at[c], peer_two
+        )
+
+    def stage_two(c):
+        second_copies[c].wait_recv()
+
+        def add(rows):
+            total = own[c][bit_two, rows].astype(jnp.float32) + came[c][bit_two, rows].astype(
+                jnp.float32
+            )
+            total = total + second_in[c][rows].astype(jnp.float32)
+            quarter[c][rows] = total.astype(jnp.bfloat16)
+
+        by_rows(ROWS, add)
+        part_copies[c] = [
+            send(
+                quarter[c].at[pl.ds(pl.multiple_of(lax.rem(place + k, 4) * PART, 16), PART)],
+                parts[c].at[k - 1],
+                s3.at[c, k - 1],
+                r3.at[c, k - 1],
+                lax.rem(here + 4 * k, peers),
+            )
+            for k in (1, 2, 3)
+        ]
+
+    def stage_three(c):
+        for copy in part_copies[c]:
+            copy.wait_recv()
+
+        def add(rows):
+            at = pl.ds(pl.multiple_of(place * PART + rows.start, 16), 16)
+            total = quarter[c][at].astype(jnp.float32)
+            for k in range(3):
+                total = total + parts[c][k, rows].astype(jnp.float32)
+            gathered[c][at] = total.astype(jnp.bfloat16)
+
+        by_rows(PART, add)
+        block = pl.ds(pl.multiple_of(place * PART, 16), PART)
+        gather_copies[c] = [
+            send(
+                gathered[c].at[block],
+                gathered[c].at[block],
+                s4.at[c, k - 1],
+                r4.at[c, k - 1],
+                lax.rem(here + 4 * k, peers),
+            )
+            for k in (1, 2, 3)
+        ]
+
+    def stage_four(c):
+        item = plan[c]
+        result = results[item[0]]
+        for copy in gather_copies[c]:
+            copy.wait_recv()
+        whole = gathered[c].at[pl.ds(0, ROWS)]
+        other_copies[c] = send(whole, other[c], s5.at[c], r5.at[c], peer_two)
+        last_copies[c] = [
+            send(whole, piece(result, item, bit_one, bit_two), s6.at[c, 0], r6.at[c, 0], peer_one)
+        ]
+        store = pltpu.make_async_copy(
+            whole, piece(result, item, bit_one, bit_two), store_sem.at[c, 0]
+        )
+        store.start()
+        stores.append(store)
+
+    def stage_five(c):
+        item = plan[c]
+        result = results[item[0]]
+        other_copies[c].wait_recv()
+        last_copies[c].append(
+            send(
+                other[c],
+                piece(result, item, bit_one, 1 - bit_two),
+                s6.at[c, 1],
+                r6.at[c, 1],
+                peer_one,
+            )
+        )
+        store = pltpu.make_async_copy(
+            other[c], piece(result, item, bit_one, 1 - bit_two), store_sem.at[c, 1]
+        )
+        store.start()
+        stores.append(store)
+
+    stages = (stage_one, stage_two, stage_three, stage_four, stage_five)
+    for tick in range(nchunks + len(stages) - 1):
+        for number in reversed(range(len(stages))):
+            c = tick - number
+            if 0 <= c < nchunks:
+                stages[number](c)
+    for copy in small_copies:
+        copy.wait()
+    total = small_all[0]
+    for i in range(1, peers):
+        total = total + small_all[i]
+    small_out[...] = total
+    for c in range(nchunks):
+        for copy in last_copies[c]:
+            copy.wait_recv()
+    for copy in pending:
+        copy.wait_send()
+    for store in stores:
+        store.wait()
+
+
+def sum_grads(ident, grad_fc, grad_rest, grad_proj, small):
+    plan = chunk_plan((1152, 1024), (1088,))
+    nchunks = len(plan)
+    peers = lax.axis_size("replica")
+    bf, f32 = jnp.bfloat16, jnp.float32
+    any_spec = pl.BlockSpec(memory_space=pl.ANY)
+    vmem = pl.BlockSpec(memory_space=pltpu.VMEM)
+    dma = pltpu.SemaphoreType.DMA
+    arrays = (grad_fc, grad_rest, grad_proj)
+    buffers = []
+    for shape in (
+        lambda w: (2, ROWS, w),
+        lambda w: (2, ROWS, w),
+        lambda w: (ROWS, w),
+        lambda w: (PADDED, w),
+        lambda w: (3, PART, w),
+        lambda w: (PADDED, w),
+        lambda w: (ROWS, w),
+    ):
+        buffers += [pltpu.VMEM(shape(item[1]), bf) for item in plan]
+    one_small = small.shape[1:]
+    buffers += [
+        pltpu.VMEM(one_small, f32),
+        pltpu.VMEM(one_small, f32),
+        pltpu.VMEM((peers,) + one_small, f32),
+    ]
+    pairs, triples, ones = dma((nchunks, 2)), dma((nchunks, 3)), dma((nchunks,))
+    sems = [pairs, pairs, pairs, ones, ones, triples, triples, triples, triples, ones, ones]
+    sems += [pairs, pairs, pairs, dma, dma, dma((peers,)), dma((peers,))]
+    return pl.pallas_call(
+        functools.partial(sum_grads_body, plan),
+        out_shape=[jax.ShapeDtypeStruct(a.shape, bf) for a in arrays]
+        + [jax.ShapeDtypeStruct(one_small, f32)],
+        in_specs=[any_spec] * 3 + [vmem],
+        out_specs=[any_spec] * 3 + [vmem],
+        scratch_shapes=buffers + sems,
+        compiler_params=pltpu.CompilerParams(
+            collective_id=ident, has_side_effects=True, vmem_limit_bytes=56 << 20
+        ),
+        name=f"sum_grads{ident}",
+    )(*arrays, small)
+
+
 def split_last(array):
     return jnp.stack([array[:, :128], array[:, 128:]])
 
@@ -763,13 +1058,14 @@
     )
     tails = jnp.repeat(tails, half, axis=0)
     chunk = jnp.concatenate(main + [tails], axis=1)
-    got, got_last, all_places, mat_out, mat_fc, mat_proj = exchange(
+    grad_low = out_grad.reshape(count, width)
+    got, got_last, all_places, mat_out, mat_fc, mat_proj, firsts, grad_lows = exchange(
         2,
         1,
         chunk,
         split_last(queries[cut:]),
         positions.reshape(micro, rows_here),
-        (w_attn_out, w_fc, w_proj),
+        [(item, "whole") for item in (w_attn_out, w_fc, w_proj, first, grad_low)],
     )
     mat_out = mat_out.reshape(width, width)
     mat_fc = mat_fc.reshape(width, hidden_width)
@@ -808,25 +1104,46 @@
     output_rows = middle + jnp.dot(hidden, mat_proj, preferred_element_type=f32) + bias_proj
     result = output_rows.astype(bf).reshape(micro, 1, rows_here, width)
 
-    grad_low = out_grad.reshape(count, width)
     grad_top = grad_low.astype(f32)
     grad_bias_proj = jnp.sum(grad_top, 0)
-    grad_mat_proj = contract(hidden, grad_low, 0, 0)
     (grad_hidden_in,) = gelu_pull(times_transposed(grad_low, mat_proj))
     grad_hidden_in = grad_hidden_in.astype(bf)
     grad_bias_fc = jnp.sum(grad_hidden_in, 0, dtype=f32)
-    grad_mat_fc = contract(second, grad_hidden_in, 0, 0)
     grad_second = times_transposed(grad_hidden_in, mat_fc)
     grad_middle_norm, grad_gain_two, grad_shift_two = norm_two_pull(grad_second)
     grad_middle = grad_top + grad_middle_norm
     grad_bias_out = jnp.sum(grad_middle, 0)
     grad_branch = grad_middle.astype(bf)
-    grad_mat_out = contract(attended, grad_branch, 1, 0)
     grad_attended = contract(mat_out, grad_branch, 1, 1).astype(bf)
 
-    grad_got, grad_got_last = exchange(
-        4, 1, grad_attended[:cut].reshape(peers, HEAD_DIM, count), split_last(grad_attended[cut:])
-    )
+    grad_got, grad_got_last, hiddens, seconds, grad_ins, attendeds, branches = exchange(
+        4,
+        1,
+        grad_attended[:cut].reshape(peers, HEAD_DIM, count),
+        split_last(grad_attended[cut:]),
+        None,
+        [
+            (hidden, "columns"),
+            (second, "whole"),
+            (grad_hidden_in, "whole"),
+            (attended, "rows"),
+            (grad_branch, "whole"),
+        ],
+    )
+    group = lax.axis_index("group")
+
+    def own_columns(pair):
+        return lax.dynamic_slice_in_dim(pair, group * part, part, 2)
+
+    def both(left, right, left_dims, right_dims):
+        return lax.dot_general(
+            left, right, ((left_dims, right_dims), ((), ())), preferred_element_type=f32
+        ).astype(bf)
+
+    grad_mat_proj = both(hiddens, grad_lows, (0, 1), (0, 1))
+    grad_mat_fc = both(own_columns(seconds), grad_ins, (0, 1), (0, 1))
+    grad_mat_out = both(attendeds, branches, (0, 2), (0, 1))
+
     grad_sent, grad_sent_last = attend_grad(
         got, got_last, limit, unit_places, out_f, lse, grad_got, grad_got_last
     )
@@ -853,12 +1170,12 @@
     grad_bias_query = jnp.sum(grad_query, 1, dtype=f32)
     grad_bias_value = jnp.sum(grad_value, 1, dtype=f32)
     grad_joined = jnp.concatenate([grad_query, grad_key, grad_value], 0)
-    grad_mat_qkv = contract(first, grad_joined, 0, 1)
+    (joined_pair,) = share(6, grad_joined)
+    grad_mat_qkv = both(own_columns(firsts), joined_pair, (0, 1), (0, 2))
     grad_first = contract(grad_joined, mat_qkv, 0, 1)
     grad_rows_norm, grad_gain_one, grad_shift_one = norm_one_pull(grad_first)
     tokens_grad = (grad_middle + grad_rows_norm).astype(bf).reshape(micro, 1, rows_here, width)
 
-    matrices = reduce_grads((grad_mat_qkv, grad_mat_out, grad_mat_fc, grad_mat_proj))
     small_grads = jnp.concatenate(
         [
             item.reshape(2, -1)
@@ -876,24 +1193,34 @@
         ],
         1,
     )
-    small_grads = lax.psum(small_grads, ("group", "replica"))
-    small_own = lax.dynamic_index_in_dim(small_grads, lax.axis_index("group"), 0, False)
-    vec = [small_own[i * part : (i + 1) * part] for i in range(8)] + [small_own[8 * part :]]
+    lanes = 128
+    rows = -(-small_grads.shape[1] // (8 * lanes)) * 8
+    small_rows = jnp.pad(small_grads, ((0, 0), (0, rows * lanes - small_grads.shape[1])))
+    sum_fc, sum_rest, sum_proj, small_own = sum_grads(
+        7,
+        grad_mat_fc,
+        jnp.concatenate([grad_mat_qkv, grad_mat_out], 1),
+        grad_mat_proj,
+        small_rows.reshape(2, rows, lanes),
+    )
+    small_own = small_own.reshape(-1)
+    vec = [small_own[i * part : (i + 1) * part] for i in range(8)]
+    vec.append(small_own[8 * part : 8 * part + hidden_width // 2])
     return (
         result,
         tokens_grad,
         vec[0],
         vec[1],
-        matrices[0],
+        sum_rest[:, : 3 * width].astype(f32),
         vec[2],
         vec[3],
-        matrices[1],
+        sum_rest[:, 3 * width :].astype(f32),
         vec[4],
         vec[5],
         vec[6],
-        matrices[2],
+        sum_fc.astype(f32),
         vec[8],
-        matrices[3],
+        sum_proj.astype(f32),
         vec[7],
     )
 

time: 802 us -> 643 us (0.80)
  waiting for transfers between devices: 373 us -> 0 us
  Pallas kernels: 194 us -> 459 us
  blocking collectives: 45.2 us -> 0 us
  between operations: 14.7 us -> 1.64 us
  other arithmetic: 27.9 us -> 40.6 us
  matrix products: 72.8 us -> 63.3 us
    psum x1 -> x0, waiting for transfers between devices: 338 us -> none  [reduce_grads(): lax.psum(for_sending(owned), 'replica')]
    pallas_call x4 -> x5, Pallas kernels: 130 us -> 390 us  [the longest x1 262 us: sum_grads(): pl.pallas_call(functools.partial(sum_grads_body, plan), out_shape=[jax.Sh...]
    psum x1 -> x0, blocking collectives: 45.2 us -> none  [per_device_heads(): small_grads = lax.psum(small_grads, ('group', 'replica'))]
    reduce_scatter x3 -> x0, waiting for transfers between devices: 34.5 us -> none  [reduce_grads(): lax.psum_scatter(for_sending(terms), 'group', scatter_dimension=0, tiled=...]
    dot_general x8 -> x4, matrix products: 37.9 us -> 16.8 us  [contract(): lax.dot_general(left, right, (((left_dim,), (right_dim,)), ((), ())), pre...]
    dot_general x0 -> x4, matrix products: none -> 17.9 us  [both(): lax.dot_general(left, right, ((left_dims, right_dims), ((), ())), preferr...]
    unnamed x48 -> x111, local copies, waits for them, and re-layouts: 42.3 us -> 27.7 us
    reshape x9, local copies, waits for them, and re-layouts: 0.64 us -> 9.49 us  [per_device_heads(): item.reshape(2, -1)]
  transfers between devices with their start and end apart: 5 -> 0, of which waited for: 3 -> 0; matrix products, arithmetic and copies ran while one was open for 10% -> 0% of each run, Pallas kernels for 11% -> 0%
where the time goes in v2:
time: 643 us; the launch traced here: 636 us
  Pallas kernels  459 us (71%)
  local copies, waits for them, and re-layouts  71.4 us (11%)
  matrix products  63.3 us (10%)
  other arithmetic  40.6 us (6%)
    pallas_call x1, Pallas kernels, sum_grads(): pl.pallas_call(functools.partial(sum_grads_body, plan), out_shape=[jax.Sh...  262 us
    pallas_call x4, Pallas kernels, exchange(): pl.pallas_call(functools.partial(exchange_body, direction, with_places, m...  129 us
    pallas_call x1, Pallas kernels, attend_grad(): pl.pallas_call(attend_grad_body, out_shape=[jax.ShapeDtypeStruct((peers,...  33.4 us
    unnamed x111, local copies, waits for them, and re-layouts  27.7 us
    pallas_call x1, Pallas kernels, attend(): pl.pallas_call(attend_body, out_shape=[jax.ShapeDtypeStruct((peers, 64, 2...  24.4 us
    dot_general x4, matrix products, both(): lax.dot_general(left, right, ((left_dims, right_dims), ((), ())), preferr...  17.9 us
    dot_general x4, matrix products, contract(): lax.dot_general(left, right, (((left_dim,), (right_dim,)), ((), ())), pre...  16.8 us

profile of v2, /device:TPU:0, one launch (start us, length us, event | category | flops | bytes accessed | tf_op | source)
XLA Modules:
  0.0 636.1 jit_solution(4402348140458753832)
XLA Ops:
  0.6 6.2 concatenate.55
  7.5 6.9 %share1.1 = (bf16[2,544,3264]{2,1,0:T(8,128)(2,1)}, bf16[2,1,6528]{2,1,0:T(2,128)(2,1)}) custom-call(bf16[544,3264]{1,0:T(8,128)(2,1)} %refs_0_.1, bf16[1,6528]{1,0:T(2,128)(2,1)} %reshape.270.refs_1_), custom_call_target="tpu_custom_call" | custom-call | tf_op jit(solution)/shard_map/share1/pallas_call | solution.py:519
  14.4 0.8 copy.101
  17.4 5.6 fusion.1
  23.3 1.5 pad_maximum_fusion.1.refs_0_
  25.7 1.1 add_convert_fusion.2.refs_6_
  26.8 1.1 copy.71
  27.9 8.4 %copy.72.refs_5_ = bf16[2176,1088]{1,0:T(8,128)(2,1)} copy(bf16[2176,1088]{0,1:T(8,128)(2,1)} %param.32) | data formatting | bytes 9469952 | tf_op args[15]
  36.3 43.9 %exchange2.1 = (bf16[16,256,256]{2,1,0:T(8,128)(2,1)}, bf16[2,64,128]{2,1,0:T(8,128)(2,1)}, s32[16,2,128]{2,1,0:T(2,128)}, bf16[2,544,1088]{2,1,0:T(8,128)(2,1)}...) custom-call(bf16[16,256,256]{2,1,0:T(8,128)(2,1)} %pad_maximum_fusio, ...), custom_call_target="tpu_custom_call" | custom-call | tf_op jit(solution)/shard_map/exchange2/pallas_call | solution.py:472
  80.8 1.4 add_maximum_fusion
  82.2 0.7 pad_add_fusion
  82.9 2.6 broadcast_in_dim.35.places
  86.4 24.4 %attend.1 = (bf16[16,64,256]{2,1,0:T(8,128)(2,1)}, bf16[2,64,128]{2,1,0:T(8,128)(2,1)}, f32[17,64,256]{2,1,0:T(8,128)}, f32[17,1,256]{2,1,0:T(1,128)}) custom-call(bf16[16,256,256]{2,1,0:T(8,128)(2,1)} %get-tuple-element.48.got, bf16[2,64,128]{2,1,0:T(8,128)(2,1)} %get-tuple-element.49.last, s32[17,1,256]{2,1,0:T(1,128)} %broadcast_in_dim.34.limit, ...), custom_call_target="tpu_custom_call" | custom-call | tf_op jit(solution)/shard_map/attend/pallas_call | solution.py:597
  110.9 28.1 %exchange3.1 = (bf16[16,64,256]{2,1,0:T(8,128)(2,1)}, bf16[2,64,128]{2,1,0:T(8,128)(2,1)}) custom-call(bf16[16,64,256]{2,1,0:T(8,128)(2,1)} %get-tuple-element.51.refs_0_, bf16[2,64,128]{2,1,0:T(8,128)(2,1)} %get-tuple-element.52.refs_1_), custom_call_target="tpu_custom_call" | custom-call | tf_op jit(solution)/shard_map/exchange3/pallas_call | solution.py:472
  139.0 0.7 slice_bitcast_fusion.11
  139.7 1.9 maximum_maximum_fusion.refs_5_
  141.7 3.0 fusion.29
  146.0 8.9 %multiply_convert_fusion = (bf16[256,4352]{1,0:T(8,128)(2,1)}, f32[256,4352]{1,0:T(8,128)S(1)}) fusion(f32[4352]{0:T(1024)S(1)} %add.178, bf16[256,1088]{1,0:T(8,128)(2,1)S(1)} %add_convert_fusion.1.refs_3_, bf16[1088,4352]{1,0:T(8,128)(2,1)} %bitcast.159), kind=kOutput, calls=%fused_computation.19 | convolution fusion | flops 2435448832 | bytes 16729088 | tf_op jit(solution)/shard_map/dot_general | solution.py:1101
  154.9 7.7 %convert_reduce_fusion = (f32[4352]{0:T(1024)}, bf16[256,4352]{1,0:T(8,128)(2,1)S(1)}) fusion(f32[256,4352]{1,0:T(8,128)S(1)} %get-tuple-element.178, bf16[4352,1088]{1,0:T(8,128)(2,1)} %bitcast.157, bf16[256,1088]{1,0:T(8,128)(2,1)S(1)} %bitcast.131), kind=kOutput, calls=%fused_computation.18 | convolution fusion | flops 2448813824 | bytes 16729088 | tf_op jit(solution)/shard_map/dot_general | solution.py:40
  162.7 4.3 fusion.31
  167.0 1.6 copy.77
  168.6 1.9 multiply_reduce_fusion
  170.5 1.8 fusion.23
  172.4 0.9 fusion.20
  173.3 0.9 convolution_convert_fusion
  174.8 0.8 slice.226
  175.7 16.1 %exchange4.1 = (bf16[16,64,256]{2,1,0:T(8,128)(2,1)}, bf16[2,64,128]{2,1,0:T(8,128)(2,1)}, bf16[2,256,2176]{2,1,0:T(8,128)(2,1)}, bf16[2,256,1088]{2,1,0:T(8,128...) custom-call(bf16[16,64,256]{2,1,0:T(8,128)(2,1)} %bitcast.139, ...), custom_call_target="tpu_custom_call" | custom-call | tf_op jit(solution)/shard_map/exchange4/pallas_call | solution.py:472
  191.7 33.4 %attend_grad.1 = (bf16[16,256,256]{2,1,0:T(8,128)(2,1)}, bf16[2,64,128]{2,1,0:T(8,128)(2,1)}) custom-call(bf16[16,256,256]{2,1,0:T(8,128)(2,1)} %get-tuple-element.48.got, bf16[2,64,128]{2,1,0:T(8,128)(2,1)} %get-tuple-element.49.last, s32[17,1,256]{2,1,0:T(1,128)} %broadcast_in_dim.34.limit, s32[3,2048,128]{2,1,0:T(8,128)} %broadcast_in_dim.35.places, ...), custom_call_target="tpu_custom_call" | custom-call | tf_op jit(solution)/shard_map/attend_grad/pallas_call | solution.py:696
  225.2 40.7 %exchange5.1 = (bf16[16,256,256]{2,1,0:T(8,128)(2,1)}, bf16[2,64,128]{2,1,0:T(8,128)(2,1)}) custom-call(bf16[16,256,256]{2,1,0:T(8,128)(2,1)} %get-tuple-element.62.refs_0_, bf16[2,64,128]{2,1,0:T(8,128)(2,1)} %get-tuple-element.63.refs_1_), custom_call_target="tpu_custom_call" | custom-call | tf_op jit(solution)/shard_map/exchange5/pallas_call | solution.py:472
  265.8 2.5 fusion.24
  268.3 1.3 bitcast_reduce_fusion
  271.8 0.7 slice_bitcast_fusion.9
  273.1 1.3 convert_reduce_fusion.3
  274.4 0.7 reshape.296
  275.1 1.1 constant_dynamic-update-slice_fusion.2
  276.3 0.7 maximum_dynamic-update-slice_fusion.2
  277.0 1.1 constant_dynamic-update-slice_fusion.1
  278.2 7.3 %fusion.30 = (f32[1088]{0:T(1024)}, f32[256,1088]{0,1:T(8,128)}) fusion(bf16[1088,3264]{1,0:T(8,128)(2,1)} %bitcast.164, bf16[3264,256]{1,0:T(8,128)(2,1)S(1)} %maximum_dynamic-update-slice_fusion.refs_0_), kind=kOutput, calls=%fused_computation.114 | convolution fusion | flops 1818508288 | bytes 9892096 | tf_op jit(solution)/shard_map/dot_general | solution.py:313
  285.5 2.6 copy.78
  288.2 2.4 multiply_reduce_fusion.1
  290.5 1.4 reshape.294
  291.9 1.4 reshape.295
  293.3 1.4 reshape.298
  295.3 1.4 reshape.300
  296.7 1.3 reshape.302
  298.0 1.3 convert_reduce_fusion.1
  300.0 1.6 concatenate.72
  301.6 0.8 pad_bitcast_fusion
  303.0 6.9 %fusion = bf16[2176,1088]{0,1:T(8,128)(2,1)} fusion(bf16[2,256,2176]{2,1,0:T(8,128)(2,1)} %get-tuple-element.71, bf16[2,256,1088]{2,1,0:T(8,128)(2,1)} %get-tuple-element.72), kind=kOutput, calls=%fused_computation.1 | convolution fusion | flops 2426675200 | bytes 8077312 | tf_op jit(solution)/shard_map/dot_general | solution.py:1139
  309.9 8.7 %copy.85.refs_2_ = bf16[2176,1088]{1,0:T(8,128)(2,1)} copy(bf16[2176,1088]{0,1:T(8,128)(2,1)} %fusion) | data formatting | bytes 9469952 | tf_op jit(solution)/shard_map/convert_element_type | solution.py:1141
  318.6 4.0 share6.1
  322.6 5.0 bitcast_convert_fusion.1
  327.7 0.9 fusion.9
  328.6 3.0 pad_maximum_fusion.refs_1_
  331.6 5.1 bitcast_convert_fusion.refs_0_
  336.7 261.7 %sum_grads7.1 = (bf16[544,4352]{1,0:T(8,128)(2,1)}, bf16[544,4352]{1,0:T(8,128)(2,1)}, bf16[2176,1088]{1,0:T(8,128)(2,1)}, f32[56,128]{1,0:T(8,128)}) custom-call(bf16[544,4352]{1,0:T(8,128)(2,1)} %bitcast_convert_fusion.refs_0_, bf16[544,4352]{1,0:T(8,128)(2,1)} %pad_maximum_fusion.refs_1_, bf16[2176,1088]{1,0:T(8,128)(2,1)} %copy.85.refs_2_, ...), custom_call_target="tpu_custom_call" | custom-call | tf_op jit(solution)/shard_map/sum_grads7/pallas_call | solution.py:980
  598.4 6.8 %convert_element_type.128 = f32[544,4352]{1,0:T(8,128)} convert(bf16[544,4352]{1,0:T(8,128)(2,1)} %get-tuple-element.75) | non-fusion elementwise | flops 2367488 | bytes 14204928 | tf_op jit(solution)/shard_map/convert_element_type | solution.py:1221
  605.2 9.2 %copy.88 = f32[2176,1088]{0,1:T(8,128)} copy(bf16[2176,1088]{1,0:T(8,128)(2,1)} %get-tuple-element.76) | data formatting | bytes 14204928
  614.4 5.6 slice_convert_fusion
  620.0 3.4 slice_convert_fusion.1
  623.4 0.7 fusion.28
  626.1 1.1 copy.87
  627.3 7.6 %fusion.12 = bf16[256,1088]{1,0:T(8,128)(2,1)S(1)} fusion(f32[256,1088]{1,0:T(8,128)S(1)} %get-tuple-element.176, bf16[256,4352]{1,0:T(8,128)(2,1)} %get-tuple-element.177.refs_2_, bf16[4352,1088]{1,0:T(8,128)(2,1)} %bitcast.158, f32[1088]{0:T(1024)S(1)} %add.184), kind=kOutput, calls=%fused_computation.28 | convolution fusion | flops 2425143296 | bytes 13373696 | tf_op jit(solution)/shard_map/dot_general | solution.py:1104
  634.9 1.1 copy.86
  (165 shorter events, 14.2 us)
Async XLA Ops:
  7.5 8.6 %copy-start.5 = (bf16[2,1,128,1088]{2,3,1,0:T(8,128)(2,1)S(1)}, bf16[2,1,128,1088]{2,3,1,0:T(8,128)(2,1)}, u32[]{:S(2)}) copy-start(bf16[2,1,128,1088]{2,3,1,0:T(8,128)(2,1)} %param.17) | copy-start | bytes 1671172
  16.3 9.5 %copy-start.30 = (f32[256]{0:T(256)}, f32[256]{0:T(256)S(1)}, u32[]{:S(2)}) copy-start(f32[256]{0:T(256)S(1)} %get-tuple-element.173) | copy-start | bytes 3076
  16.4 9.0 %copy-start.28 = (f32[2,128]{1,0:T(2,128)}, f32[2,128]{1,0:T(2,128)S(1)}, u32[]{:S(2)}) copy-start(f32[2,128]{1,0:T(2,128)S(1)} %multiply_reduce_fusion.5) | copy-start | bytes 3076
  25.4 1.4 copy-start.32
  25.5 1.4 copy-start.12
  36.3 43.9 %copy-start.44 = (s32[2,1]{0,1:T(1,128)S(1)}, s32[2,1]{0,1:T(1,128)}, u32[]{:S(2)}) copy-start(s32[2,1]{0,1:T(1,128)} %param.20) | copy-start | bytes 28
  80.2 5.3 copy-start.20
  144.7 1.2 copy-start.25
  145.0 0.6 copy-start.38
  145.0 0.9 copy-start.34
  145.9 9.0 %copy-start.9 = (bf16[256,1088]{1,0:T(8,128)(2,1)}, bf16[256,1088]{1,0:T(8,128)(2,1)S(1)}, u32[]{:S(2)}) copy-start(bf16[256,1088]{1,0:T(8,128)(2,1)S(1)} %add_convert_fusion.1.refs_3_) | copy-start | bytes 1671172
  146.0 8.9 %copy-start.2 = (bf16[2,1,128,1088]{3,2,0,1:T(8,128)(2,1)S(1)}, bf16[2,1,128,1088]{3,2,0,1:T(8,128)(2,1)}, u32[]{:S(2)}) copy-start(bf16[2,1,128,1088]{3,2,0,1:T(8,128)(2,1)} %copy.71) | copy-start | bytes 1671172
  146.0 16.7 %slice-start.2 = ((s8[9469952]{0:T(1024)(128)(4,1)}), s8[4194304]{0:T(1024)(128)(4,1)S(1)}, s32[]{:S(2)}) async-start(s8[9469952]{0:T(1024)(128)(4,1)} %bitcast.160), calls=%async_computation.2 | async-start | bytes 8388608
  146.0 16.7 %slice-start.3 = ((s8[9469952]{0:T(1024)(128)(4,1)}), s8[4194304]{0:T(1024)(128)(4,1)S(1)}, s32[]{:S(2)}) async-start(s8[9469952]{0:T(1024)(128)(4,1)} %bitcast.160), calls=%async_computation.3 | async-start | bytes 8388608
  154.9 7.8 %slice-start.4 = ((s8[9469952]{0:T(1024)(128)(4,1)}), s8[1081344]{0:T(1024)(128)(4,1)S(1)}, s32[]{:S(2)}) async-start(s8[9469952]{0:T(1024)(128)(4,1)} %bitcast.160), calls=%async_computation.4 | async-start | bytes 2162688
  162.7 4.3 copy-start.11
  168.6 1.9 copy-start.1
  168.6 1.9 copy-start.39
  168.6 1.9 copy-start.26
  168.6 1.9 copy-start.35
  170.5 1.9 copy-start.3
  170.5 2.7 copy-start.41
  172.4 0.9 copy-start.36
  173.3 0.9 copy-start.10
  268.3 1.9 copy-start.6
  270.3 0.6 copy-start.16
  270.3 0.6 copy-start.18
  272.5 0.6 copy-start.14
  272.5 0.6 copy-start.15
  275.1 3.0 copy-start.22
  275.1 3.0 copy-start.23
  275.1 3.0 copy-start.7
  275.1 3.1 copy-start.17
  275.1 3.1 copy-start.19
  278.2 7.3 %copy-start.8 = (bf16[3264,256]{1,0:T(8,128)(2,1)}, bf16[3264,256]{1,0:T(8,128)(2,1)S(1)}, u32[]{:S(2)}) copy-start(bf16[3264,256]{1,0:T(8,128)(2,1)S(1)} %maximum_dynamic-update-slice_fusion.refs_0_) | copy-start | bytes 5013508
  288.2 6.5 %copy-start.24 = (f32[1088]{0:T(1024)S(1)}, f32[1088]{0:T(1024)}, u32[]{:S(2)}) copy-start(f32[1088]{0:T(1024)} %get-tuple-element.122) | copy-start | bytes 13060
  322.6 5.0 copy-start.42
  322.6 5.0 copy-start.43
  327.7 3.9 slice-start
  328.6 3.0 slice-start.1
  328.6 3.0 copy-start.13
  620.0 3.4 copy-start.21
  620.0 4.7 copy-start.29
  620.0 4.7 copy-start.40
  620.0 4.7 copy-start
  620.0 4.8 copy-start.31
  620.0 4.8 copy-start.33
  624.7 1.1 copy-start.4
  624.8 1.1 copy-start.37
  625.8 1.4 copy-start.27

commit v3 on v1

--- a/solution.py
+++ b/solution.py
@@ -330,8 +330,24 @@
     pl.semaphore_wait(barrier, peers - 1 + (1 if group_too else 0))
 
 
-def exchange_body(direction, with_places, nweights, *refs):
+def halves(ref, mode, which):
+    if mode == "whole":
+        return ref
+    if mode == "rows":
+        size = ref.shape[0] // 2
+        return ref.at[pl.ds(pl.multiple_of(which * size, 16), size)]
+    size = ref.shape[1] // 2
+    return ref.at[:, pl.ds(pl.multiple_of(which * size, 128), size)]
+
+
+def half_shape(array, mode):
+    rows, columns = array.shape
+    return {"whole": (rows, columns), "rows": (rows // 2, columns), "columns": (rows, columns // 2)}[mode]
+
+
+def exchange_body(direction, with_places, modes, *refs):
     refs = list(refs)
+    nweights = len(modes)
     chunk, last = refs.pop(0), refs.pop(0)
     places = refs.pop(0) if with_places else None
     weights = [refs.pop(0) for _ in range(nweights)]
@@ -351,7 +367,7 @@
     loads, copies = [], []
     for i in range(nweights):
         copy = pltpu.make_async_remote_copy(
-            weights[i],
+            halves(weights[i], modes[i], 1 - group),
             weights_out[i].at[group],
             weight_send.at[i],
             weight_recv.at[i],
@@ -360,7 +376,9 @@
         )
         copy.start()
         copies.append(copy)
-        load = pltpu.make_async_copy(weights[i], bounce[i], weight_own.at[i])
+        load = pltpu.make_async_copy(
+            halves(weights[i], modes[i], group), bounce[i], weight_own.at[i]
+        )
         load.start()
         loads.append(load)
     for slot in range(2):
@@ -432,15 +450,17 @@
             copy.wait()
 
 
-def exchange(ident, direction, chunk, last, places=None, weights=()):
+def exchange(ident, direction, chunk, last, places=None, shares=()):
     peers = chunk.shape[0]
+    weights = [array for array, _ in shares]
+    modes = [mode for _, mode in shares]
     any_spec = pl.BlockSpec(memory_space=pl.ANY)
     with_places = places is not None
     args = [chunk, last] + ([places] if with_places else []) + list(weights)
     shapes = [(chunk.shape, chunk.dtype), (last.shape, last.dtype)]
     if with_places:
         shapes.append(((peers,) + places.shape, places.dtype))
-    shapes += [((2,) + weight.shape, weight.dtype) for weight in weights]
+    shapes += [((2,) + half_shape(*item), item[0].dtype) for item in shares]
     dma = pltpu.SemaphoreType.DMA
     scratch = [dma((peers,)), dma((peers,)), dma((2,)), dma((2,)), dma((2,))]
     if with_places:
@@ -448,9 +468,9 @@
     if weights:
         count = len(weights)
         scratch += [dma((count,)), dma((count,)), dma((count,))]
-        scratch += [pltpu.VMEM(weight.shape, weight.dtype) for weight in weights]
+        scratch += [pltpu.VMEM(half_shape(*item), item[0].dtype) for item in shares]
     return pl.pallas_call(
-        functools.partial(exchange_body, direction, with_places, len(weights)),
+        functools.partial(exchange_body, direction, with_places, modes),
         out_shape=[jax.ShapeDtypeStruct(*shape) for shape in shapes],
         in_specs=[any_spec] * len(args),
         out_specs=[any_spec] * len(shapes),
@@ -696,6 +716,354 @@
     )(got, last, limit, places, out_f, lse, grad_got, grad_last)
 
 
+ROWS = 272
+PART = 80
+PADDED = 4 * PART
+PROJ, FC, OUT, QKV = range(4)
+TILES = {PROJ: (9, 8), FC: (9, 8), OUT: (5,), QKV: (7, 6)}
+
+
+def chunk_plan():
+    plan = []
+    for array in (PROJ, FC, OUT, QKV):
+        start = 0
+        for tiles in TILES[array]:
+            plan.append((array, tiles * 128, start))
+            start += tiles * 128
+    return plan
+
+
+def piece(ref, item, first, second):
+    array, width, start = item
+    if array == PROJ:
+        row = first * (2 * ROWS) + second * ROWS
+        return ref.at[pl.ds(pl.multiple_of(row, 16), ROWS), pl.ds(start, width)]
+    column = second * (sum(TILES[array]) * 128) + start
+    return ref.at[
+        pl.ds(pl.multiple_of(first * ROWS, 16), ROWS), pl.ds(pl.multiple_of(column, 128), width)
+    ]
+
+
+def by_rows(rows, fn):
+    def one(i, carry):
+        fn(pl.multiple_of(i * 16, 16))
+        return carry
+
+    lax.fori_loop(0, rows // 16, one, 0)
+
+
+class Summer:
+    def __init__(self, plan, sources, results, own, came, second_in, quarter, parts, gathered, sems):
+        self.plan, self.sources, self.results = plan, sources, results
+        self.own, self.came, self.second_in = own, came, second_in
+        self.quarter, self.parts, self.gathered = quarter, parts, gathered
+        self.load_sem, self.store_sem = sems[0], sems[1]
+        self.pairs = [tuple(sems[2 + 2 * i : 4 + 2 * i]) for i in range(6)]
+        here, group = lax.axis_index("replica"), lax.axis_index("group")
+        bit_x, bit_y = here % 2, (here // 2) % 2
+        self.here, self.place = here, here // 4
+        self.one = bit_x + group * (bit_y - bit_x)
+        self.two = bit_x + bit_y - self.one
+        self.peer_one = here + (1 + group) * (1 - 2 * self.one)
+        self.peer_two = here + (2 - group) * (1 - 2 * self.two)
+
+    def copy(self, stage, at, source, target, peer):
+        send, recv = self.pairs[stage]
+        return pltpu.make_async_remote_copy(
+            source,
+            target,
+            send.at[at],
+            recv.at[at],
+            device_id={"replica": peer},
+            device_id_type=MESH,
+        )
+
+    def z_peer(self, k):
+        return lax.rem(self.here + 4 * k, 16)
+
+    def block(self, place):
+        return pl.ds(pl.multiple_of(place * PART, 16), PART)
+
+    def load(self, c, j):
+        item = self.plan[c]
+        source = piece(self.sources[item[0]], item, self.one, j)
+        return pltpu.make_async_copy(source, self.own[c].at[j], self.load_sem.at[c, j])
+
+    def first(self, c, j):
+        item = self.plan[c]
+        source = piece(self.sources[item[0]], item, 1 - self.one, j)
+        return self.copy(0, (c, j), source, self.came[c].at[j], self.peer_one)
+
+    def second(self, c):
+        return self.copy(1, (c,), self.own[c].at[1 - self.two], self.second_in[c], self.peer_two)
+
+    def spread(self, c, k):
+        source = self.quarter[c].at[self.block(lax.rem(self.place + k, 4))]
+        return self.copy(2, (c, k - 1), source, self.parts[c].at[k - 1], self.z_peer(k))
+
+    def gather(self, c, k):
+        block = self.gathered[c].at[self.block(self.place)]
+        return self.copy(3, (c, k - 1), block, block, self.z_peer(k))
+
+    def result(self, c, other):
+        item = self.plan[c]
+        second = self.two + other * (1 - 2 * self.two)
+        return piece(self.results[item[0]], item, self.one, second)
+
+    def cross(self, c):
+        return self.copy(
+            4, (c,), self.gathered[c].at[pl.ds(0, ROWS)], self.result(c, 0), self.peer_two
+        )
+
+    def crossed(self, c):
+        return self.copy(
+            4, (c,), self.gathered[c].at[pl.ds(0, ROWS)], self.result(c, 1), self.peer_two
+        )
+
+    def final(self, c, other):
+        source = self.result(c, 1) if other else self.gathered[c].at[pl.ds(0, ROWS)]
+        return self.copy(5, (c, other), source, self.result(c, other), self.peer_one)
+
+    def finalled(self, c, other):
+        item = self.plan[c]
+        second = self.two + other * (1 - 2 * self.two)
+        target = piece(self.results[item[0]], item, 1 - self.one, second)
+        source = self.result(c, 1) if other else self.gathered[c].at[pl.ds(0, ROWS)]
+        return self.copy(5, (c, other), source, target, self.peer_one)
+
+    def store(self, c):
+        return pltpu.make_async_copy(
+            self.gathered[c].at[pl.ds(0, ROWS)], self.result(c, 0), self.store_sem.at[c]
+        )
+
+    def begin(self, c):
+        for j in range(2):
+            self.first(c, j).start()
+            self.load(c, j).start()
+        width = self.quarter[c].shape[1]
+        self.quarter[c][ROWS:, :] = jnp.zeros((PADDED - ROWS, width), jnp.bfloat16)
+
+    def stage_one(self, c):
+        for j in range(2):
+            self.load(c, j).wait()
+            self.first(c, j).wait_recv()
+        away, own, came = 1 - self.two, self.own[c], self.came[c]
+
+        def add(start):
+            rows = pl.ds(start, 16)
+            total = own[away, rows].astype(jnp.float32) + came[away, rows].astype(jnp.float32)
+            own[away, rows] = total.astype(jnp.bfloat16)
+
+        by_rows(ROWS, add)
+        self.second(c).start()
+
+    def stage_two(self, c):
+        self.second(c).wait_recv()
+        keep, own, came = self.two, self.own[c], self.came[c]
+
+        def add(start):
+            rows = pl.ds(start, 16)
+            total = own[keep, rows].astype(jnp.float32) + came[keep, rows].astype(jnp.float32)
+            total = total + self.second_in[c][rows].astype(jnp.float32)
+            self.quarter[c][rows] = total.astype(jnp.bfloat16)
+
+        by_rows(ROWS, add)
+        for k in (1, 2, 3):
+            self.spread(c, k).start()
+
+    def stage_three(self, c):
+        for k in (1, 2, 3):
+            self.spread(c, k).wait_recv()
+
+        def add(start):
+            at = pl.ds(pl.multiple_of(self.place * PART + start, 16), 16)
+            total = self.quarter[c][at].astype(jnp.float32)
+            for k in range(3):
+                total = total + self.parts[c][k, pl.ds(start, 16)].astype(jnp.float32)
+            self.gathered[c][at] = total.astype(jnp.bfloat16)
+
+        by_rows(PART, add)
+        for k in (1, 2, 3):
+            self.gather(c, k).start()
+
+    def stage_four(self, c):
+        for k in (1, 2, 3):
+            self.spread(c, k).wait_send()
+            self.gather(c, k).wait_recv()
+        self.cross(c).start()
+        self.final(c, 0).start()
+        self.store(c).start()
+
+    def stage_five(self, c):
+        self.crossed(c).wait_recv()
+        self.final(c, 1).start()
+
+    def end(self, c):
+        for j in range(2):
+            self.finalled(c, j).wait_recv()
+            self.first(c, j).wait_send()
+            self.final(c, j).wait_send()
+        self.second(c).wait_send()
+        for k in (1, 2, 3):
+            self.gather(c, k).wait_send()
+        self.cross(c).wait_send()
+        self.store(c).wait()
+
+    def run(self, stage, c):
+        steps = (self.stage_one, self.stage_two, self.stage_three, self.stage_four, self.stage_five)
+        steps[stage](c)
+
+
+def wavefront(chunks):
+    order = []
+    for tick in range(len(chunks) + 4):
+        for stage in reversed(range(5)):
+            if 0 <= tick - stage < len(chunks):
+                order.append((stage, chunks[tick - stage]))
+    return order
+
+
+class SmallSum:
+    def __init__(self, source, result, from_core, own, everyone, sems):
+        self.source, self.result, self.from_core = source, result, from_core
+        self.own, self.everyone = own, everyone
+        (self.sp, self.rp, self.sa, self.ra, self.sb, self.rb) = sems
+        self.here, self.group = lax.axis_index("replica"), lax.axis_index("group")
+        self.peers = everyone.shape[0]
+
+    def core_copy(self, source, target, send, recv):
+        return pltpu.make_async_remote_copy(
+            source,
+            target,
+            send,
+            recv,
+            device_id={"group": 1 - self.group},
+            device_id_type=MESH,
+        )
+
+    def give(self):
+        return self.core_copy(self.source.at[1 - self.group], self.from_core, self.sp, self.rp)
+
+    def tell(self, step):
+        return pltpu.make_async_remote_copy(
+            self.own,
+            self.everyone.at[self.here],
+            self.sa.at[step],
+            self.ra.at[step],
+            device_id={"replica": lax.rem(self.here + step, self.peers)},
+            device_id_type=MESH,
+        )
+
+    def back(self):
+        return self.core_copy(
+            self.result.at[self.group], self.result.at[self.group], self.sb, self.rb
+        )
+
+    def begin(self):
+        self.give().start()
+
+    def middle(self):
+        self.give().wait()
+        self.own[...] = self.source[self.group] + self.from_core[...]
+        self.everyone[self.here] = self.own[...]
+        for step in range(1, self.peers):
+            self.tell(step).start()
+
+    def finish(self):
+        for step in range(1, self.peers):
+            self.tell(step).wait()
+        total = self.everyone[0]
+        for i in range(1, self.peers):
+            total = total + self.everyone[i]
+        self.result[self.group] = total
+        self.back().start()
+
+    def end(self):
+        self.back().wait()
+
+
+def sum_grads_body(plan, *refs):
+    nchunks = len(plan)
+    sources, small, results, small_out = refs[0:4], refs[4], refs[5:9], refs[9]
+    refs = list(refs[10:])
+    buffers = [[refs.pop(0) for _ in range(nchunks)] for _ in range(6)]
+    from_core, own_small, everyone = (refs.pop(0) for _ in range(3))
+    summer = Summer(plan, sources, results, *buffers, refs[:14])
+    smalls = SmallSum(small, small_out, from_core, own_small, everyone, refs[14:20])
+    greet(everyone.shape[0], lax.axis_index("replica"), True)
+    smalls.begin()
+    for c in range(nchunks):
+        summer.begin(c)
+    smalls.middle()
+    for stage, c in wavefront(range(nchunks)):
+        summer.run(stage, c)
+    smalls.finish()
+    smalls.end()
+    for c in range(nchunks):
+        summer.end(c)
+
+
+def sum_buffers(plan):
+    bf = jnp.bfloat16
+    shapes = ((2, ROWS), (2, ROWS), (ROWS,), (PADDED,), (3, PART), (PADDED,))
+    return [pltpu.VMEM(shape + (item[1],), bf) for shape in shapes for item in plan]
+
+
+def sum_sems(plan):
+    dma = pltpu.SemaphoreType.DMA
+    count = len(plan)
+    pairs, triples, ones = dma((count, 2)), dma((count, 3)), dma((count,))
+    stages = (pairs, ones, triples, triples, ones, pairs)
+    return [pairs, ones] + [sem for stage in stages for sem in (stage, stage)]
+
+
+def small_scratch(shape, peers):
+    f32 = jnp.float32
+    return [pltpu.VMEM(shape, f32), pltpu.VMEM(shape, f32), pltpu.VMEM((peers,) + shape, f32)]
+
+
+def small_sems(peers):
+    dma = pltpu.SemaphoreType.DMA
+    return [dma, dma, dma((peers,)), dma((peers,)), dma, dma]
+
+
+def sum_grads(ident, *arrays):
+    *arrays, small = arrays
+    plan = chunk_plan()
+    peers = lax.axis_size("replica")
+    bf, f32 = jnp.bfloat16, jnp.float32
+    any_spec = pl.BlockSpec(memory_space=pl.ANY)
+    vmem = pl.BlockSpec(memory_space=pltpu.VMEM)
+    return pl.pallas_call(
+        functools.partial(sum_grads_body, plan),
+        out_shape=[jax.ShapeDtypeStruct(a.shape, bf) for a in arrays]
+        + [jax.ShapeDtypeStruct(small.shape, f32)],
+        in_specs=[any_spec] * 4 + [vmem],
+        out_specs=[any_spec] * 4 + [vmem],
+        scratch_shapes=sum_buffers(plan)
+        + small_scratch(small.shape[1:], peers)
+        + sum_sems(plan)
+        + small_sems(peers),
+        compiler_params=pltpu.CompilerParams(
+            collective_id=ident, has_side_effects=True, vmem_limit_bytes=56 << 20
+        ),
+        name=f"sum_grads{ident}",
+    )(*arrays, small)
+
+
+def norm_unit(values):
+    center = values - jnp.mean(values, -1, keepdims=True)
+    spread = lax.rsqrt(jnp.mean(center * center, -1, keepdims=True) + 1e-05)
+    return center * spread, spread
+
+
+def norm_back(grad, unit, spread, gain):
+    grad_unit = grad * gain
+    slope = jnp.mean(grad_unit * unit, -1, keepdims=True)
+    back = spread * (grad_unit - jnp.mean(grad_unit, -1, keepdims=True) - unit * slope)
+    return back, jnp.sum(grad * unit, 0, keepdims=True), jnp.sum(grad, 0, keepdims=True)
+
+
 def split_last(array):
     return jnp.stack([array[:, :128], array[:, 128:]])
 
@@ -729,24 +1097,28 @@
     scale = HEAD_DIM ** (-0.5)
     split = (peers * HEAD_DIM, width)
 
-    small = jnp.concatenate(
-        [ln1_gain, ln1_bias, b_query, b_value, b_attn_out, ln2_gain, ln2_bias, b_proj, b_fc]
-    ).reshape(1, -1)
-    mat_qkv, vectors = share(1, w_qkv, small)
-    mat_qkv = mat_qkv.reshape(width, 3 * width)
-    vectors = vectors[:, 0].astype(f32)
+    vectors = (ln1_gain, ln1_bias, b_query, b_value, b_attn_out, ln2_gain, ln2_bias, b_proj, b_fc)
+    shared = share(1, w_qkv, *(vector.reshape(1, -1) for vector in vectors))
+    mat_qkv = shared[0].reshape(width, 3 * width)
     part = width // 2
-    gain_one, shift_one, bias_query, bias_value, bias_out, gain_two, shift_two, bias_proj = (
-        vectors[:, i * part : (i + 1) * part].reshape(width) for i in range(8)
-    )
-    bias_fc = vectors[:, 8 * part :].reshape(hidden_width)
+    (
+        gain_one,
+        shift_one,
+        bias_query,
+        bias_value,
+        bias_out,
+        gain_two,
+        shift_two,
+        bias_proj,
+        bias_fc,
+    ) = (vector.reshape(1, -1).astype(f32) for vector in shared[1:])
 
     rows_in = tokens.reshape(count, width).astype(f32)
-    normed_one, norm_one_pull = jax.vjp(norm_rows, rows_in, gain_one, shift_one)
-    first = normed_one.astype(bf)
+    unit_one, spread_one = norm_unit(rows_in)
+    first = (unit_one * gain_one + shift_one).astype(bf)
     joined = contract(mat_qkv, first, 0, 1)
-    bias_all = jnp.concatenate([bias_query, jnp.zeros_like(bias_query), bias_value])
-    joined = joined + bias_all[:, None]
+    bias_all = jnp.concatenate([bias_query, jnp.zeros_like(bias_query), bias_value], 1)
+    joined = joined + bias_all.reshape(-1, 1)
     queries = ((joined[:width]).astype(bf).astype(f32) * scale).astype(bf)
     keys = joined[width : 2 * width].astype(bf)
     values = joined[2 * width :].astype(bf)
@@ -763,17 +1135,17 @@
     )
     tails = jnp.repeat(tails, half, axis=0)
     chunk = jnp.concatenate(main + [tails], axis=1)
-    got, got_last, all_places, mat_out, mat_fc, mat_proj = exchange(
+    grad_low = out_grad.reshape(count, width)
+    got, got_last, all_places, mat_out, mat_fc, mat_proj_t, firsts, grad_lows = exchange(
         2,
         1,
         chunk,
         split_last(queries[cut:]),
         positions.reshape(micro, rows_here),
-        (w_attn_out, w_fc, w_proj),
+        [(item, "whole") for item in (w_attn_out, w_fc, w_proj.T, first, grad_low)],
     )
     mat_out = mat_out.reshape(width, width)
     mat_fc = mat_fc.reshape(width, hidden_width)
-    mat_proj = mat_proj.reshape(hidden_width, width)
 
     place_rows = jnp.transpose(all_places, (1, 0, 2)).reshape(micro, peers * rows_here)
     limits = jnp.maximum(place_rows + 1, prefix.reshape(micro, 1))
@@ -800,33 +1172,61 @@
     )
 
     middle = rows_in + contract(attended, mat_out, 0, 0) + bias_out
-    normed_two, norm_two_pull = jax.vjp(norm_rows, middle, gain_two, shift_two)
-    second = normed_two.astype(bf)
+    unit_two, spread_two = norm_unit(middle)
+    second = (unit_two * gain_two + shift_two).astype(bf)
     hidden_in = jnp.dot(second, mat_fc, preferred_element_type=f32) + bias_fc
     hidden_f, gelu_pull = jax.vjp(gelu_tanh, hidden_in)
     hidden = hidden_f.astype(bf)
-    output_rows = middle + jnp.dot(hidden, mat_proj, preferred_element_type=f32) + bias_proj
+    output_rows = middle + bias_proj
+    half_hidden = hidden_width // 2
+    for core in range(2):
+        own_hidden = hidden[:, core * half_hidden : (core + 1) * half_hidden]
+        output_rows = output_rows + contract(own_hidden, mat_proj_t[core], 1, 1)
     result = output_rows.astype(bf).reshape(micro, 1, rows_here, width)
 
-    grad_low = out_grad.reshape(count, width)
     grad_top = grad_low.astype(f32)
-    grad_bias_proj = jnp.sum(grad_top, 0)
-    grad_mat_proj = contract(hidden, grad_low, 0, 0)
-    (grad_hidden_in,) = gelu_pull(times_transposed(grad_low, mat_proj))
+    grad_bias_proj = jnp.sum(grad_top, 0, keepdims=True)
+    grad_hidden = jnp.concatenate([contract(grad_low, mat_proj_t[core], 1, 0) for core in range(2)], 1)
+    (grad_hidden_in,) = gelu_pull(grad_hidden)
     grad_hidden_in = grad_hidden_in.astype(bf)
-    grad_bias_fc = jnp.sum(grad_hidden_in, 0, dtype=f32)
-    grad_mat_fc = contract(second, grad_hidden_in, 0, 0)
+    grad_bias_fc = jnp.sum(grad_hidden_in, 0, keepdims=True, dtype=f32)
     grad_second = times_transposed(grad_hidden_in, mat_fc)
-    grad_middle_norm, grad_gain_two, grad_shift_two = norm_two_pull(grad_second)
+    grad_middle_norm, grad_gain_two, grad_shift_two = norm_back(
+        grad_second, unit_two, spread_two, gain_two
+    )
     grad_middle = grad_top + grad_middle_norm
-    grad_bias_out = jnp.sum(grad_middle, 0)
+    grad_bias_out = jnp.sum(grad_middle, 0, keepdims=True)
     grad_branch = grad_middle.astype(bf)
-    grad_mat_out = contract(attended, grad_branch, 1, 0)
     grad_attended = contract(mat_out, grad_branch, 1, 1).astype(bf)
 
-    grad_got, grad_got_last = exchange(
-        4, 1, grad_attended[:cut].reshape(peers, HEAD_DIM, count), split_last(grad_attended[cut:])
-    )
+    grad_got, grad_got_last, hiddens, seconds, grad_ins, attendeds, branches = exchange(
+        4,
+        1,
+        grad_attended[:cut].reshape(peers, HEAD_DIM, count),
+        split_last(grad_attended[cut:]),
+        None,
+        [
+            (hidden, "columns"),
+            (second, "whole"),
+            (grad_hidden_in, "whole"),
+            (attended, "rows"),
+            (grad_branch, "whole"),
+        ],
+    )
+    group = lax.axis_index("group")
+
+    def own_columns(pair):
+        return lax.dynamic_slice_in_dim(pair, group * part, part, 2)
+
+    def both(left, right, left_dims, right_dims):
+        return lax.dot_general(
+            left, right, ((left_dims, right_dims), ((), ())), preferred_element_type=f32
+        ).astype(bf)
+
+    grad_mat_proj_t = both(grad_lows, hiddens, (0, 1), (0, 1))
+    grad_mat_fc = both(own_columns(seconds), grad_ins, (0, 1), (0, 1))
+    grad_mat_out = both(attendeds, branches, (0, 2), (0, 1))
+
     grad_sent, grad_sent_last = attend_grad(
         got, got_last, limit, unit_places, out_f, lse, grad_got, grad_got_last
     )
@@ -850,50 +1250,58 @@
         ],
         0,
     )
-    grad_bias_query = jnp.sum(grad_query, 1, dtype=f32)
-    grad_bias_value = jnp.sum(grad_value, 1, dtype=f32)
+    grad_bias_query = jnp.sum(grad_query, 1, dtype=f32).reshape(1, width)
+    grad_bias_value = jnp.sum(grad_value, 1, dtype=f32).reshape(1, width)
     grad_joined = jnp.concatenate([grad_query, grad_key, grad_value], 0)
-    grad_mat_qkv = contract(first, grad_joined, 0, 1)
+    (joined_pair,) = share(6, grad_joined)
+    grad_mat_qkv = both(own_columns(firsts), joined_pair, (0, 1), (0, 2))
     grad_first = contract(grad_joined, mat_qkv, 0, 1)
-    grad_rows_norm, grad_gain_one, grad_shift_one = norm_one_pull(grad_first)
+    grad_rows_norm, grad_gain_one, grad_shift_one = norm_back(
+        grad_first, unit_one, spread_one, gain_one
+    )
     tokens_grad = (grad_middle + grad_rows_norm).astype(bf).reshape(micro, 1, rows_here, width)
 
-    matrices = reduce_grads((grad_mat_qkv, grad_mat_out, grad_mat_fc, grad_mat_proj))
     small_grads = jnp.concatenate(
         [
-            item.reshape(2, -1)
-            for item in (
-                grad_gain_one,
-                grad_shift_one,
-                grad_bias_query,
-                grad_bias_value,
-                grad_bias_out,
-                grad_gain_two,
-                grad_shift_two,
-                grad_bias_proj,
-                grad_bias_fc,
-            )
+            grad_gain_one,
+            grad_shift_one,
+            grad_bias_query,
+            grad_bias_value,
+            grad_bias_out,
+            grad_gain_two,
+            grad_shift_two,
+            grad_bias_proj,
+            grad_bias_fc.reshape(-1, width),
+            jnp.zeros((4, width), f32),
         ],
-        1,
-    )
-    small_grads = lax.psum(small_grads, ("group", "replica"))
-    small_own = lax.dynamic_index_in_dim(small_grads, lax.axis_index("group"), 0, False)
-    vec = [small_own[i * part : (i + 1) * part] for i in range(8)] + [small_own[8 * part :]]
+        0,
+    )
+    sum_proj_t, sum_fc, sum_out, sum_qkv, small_sum = sum_grads(
+        7,
+        grad_mat_proj_t,
+        grad_mat_fc,
+        jnp.pad(grad_mat_out, ((0, 0), (0, 1280 - width))),
+        jnp.pad(grad_mat_qkv, ((0, 0), (0, 3328 - 3 * width))),
+        small_grads.reshape(2, 8, width),
+    )
+    own_rows = lax.dynamic_slice_in_dim(small_sum[0], group * part, part, 1)
+    vec = [own_rows[i] for i in range(8)]
+    bias_rows = lax.dynamic_slice_in_dim(small_sum[1], group * 2, 2, 0).reshape(-1)
     return (
         result,
         tokens_grad,
         vec[0],
         vec[1],
-        matrices[0],
+        sum_qkv[:, : 3 * width].astype(f32),
         vec[2],
         vec[3],
-        matrices[1],
+        sum_out[:, :width].astype(f32),
         vec[4],
         vec[5],
         vec[6],
-        matrices[2],
-        vec[8],
-        matrices[3],
+        sum_fc.astype(f32),
+        bias_rows,
+        sum_proj_t.astype(f32).T,
         vec[7],
     )
 

time: 802 us -> 629 us (0.78)
  waiting for transfers between devices: 373 us -> 0 us
  Pallas kernels: 194 us -> 460 us
  blocking collectives: 45.2 us -> 0 us
  local copies, waits for them, and re-layouts: 69.2 us -> 47.8 us
  other arithmetic: 27.9 us -> 41.3 us
  between operations: 14.7 us -> 1.58 us
    psum x1 -> x0, waiting for transfers between devices: 338 us -> none  [reduce_grads(): lax.psum(for_sending(owned), 'replica')]
    pallas_call x4 -> x5, Pallas kernels: 130 us -> 391 us  [the longest x1 262 us: sum_grads(): pl.pallas_call(functools.partial(sum_grads_body, plan), out_shape=[jax.Sh...]
    psum x1 -> x0, blocking collectives: 45.2 us -> none  [per_device_heads(): small_grads = lax.psum(small_grads, ('group', 'replica'))]
    unnamed x48 -> x94, local copies, waits for them, and re-layouts: 42.3 us -> 5.4 us
    reduce_scatter x3 -> x0, waiting for transfers between devices: 34.5 us -> none  [reduce_grads(): lax.psum_scatter(for_sending(terms), 'group', scatter_dimension=0, tiled=...]
    dot_general x2 -> x1, matrix products: 18.4 us -> 8.74 us  [times_transposed(): lax.dot_general(left, right, (((1,), (1,)), ((), ())), preferred_element_...]
    dot_general x1 -> x4, matrix products: 10.2 us -> 16.1 us  [both(): lax.dot_general(left, right, ((left_dims, right_dims), ((), ())), preferr...]
    convert_element_type x5 -> x12, other arithmetic: 16.5 us -> 13.7 us  [the longest x1 4.46 us: per_device_heads(): sum_fc.astype(f32)]
  transfers between devices with their start and end apart: 5 -> 0, of which waited for: 3 -> 0; matrix products, arithmetic and copies ran while one was open for 10% -> 0% of each run, Pallas kernels for 11% -> 0%
where the time goes in v3:
time: 629 us; the launch traced here: 624 us
  Pallas kernels  460 us (73%)
  matrix products  73.1 us (12%)
  local copies, waits for them, and re-layouts  47.8 us (8%)
  other arithmetic  41.3 us (7%)
    pallas_call x1, Pallas kernels, sum_grads(): pl.pallas_call(functools.partial(sum_grads_body, plan), out_shape=[jax.Sh...  262 us
    pallas_call x4, Pallas kernels, exchange(): pl.pallas_call(functools.partial(exchange_body, direction, with_places, m...  129 us
    dot_general x8, matrix products, contract(): lax.dot_general(left, right, (((left_dim,), (right_dim,)), ((), ())), pre...  36.4 us
    pallas_call x1, Pallas kernels, attend_grad(): pl.pallas_call(attend_grad_body, out_shape=[jax.ShapeDtypeStruct((peers,...  33.4 us
    pallas_call x1, Pallas kernels, attend(): pl.pallas_call(attend_body, out_shape=[jax.ShapeDtypeStruct((peers, 64, 2...  24.4 us
    dot_general x4, matrix products, both(): lax.dot_general(left, right, ((left_dims, right_dims), ((), ())), preferr...  16.1 us

profile of v3, /device:TPU:0, one launch (start us, length us, event | category | flops | bytes accessed | tf_op | source)
XLA Modules:
  0.0 623.7 jit_solution(2597044597691360112)
XLA Ops:
  0.6 1.3 reshape.359.refs_9_
  1.9 1.3 reshape.351.refs_1_
  3.2 1.3 reshape.352.refs_2_
  4.5 1.3 reshape.353.refs_3_
  5.7 1.3 reshape.354.refs_4_
  7.0 1.3 reshape.355.refs_5_
  8.3 1.3 reshape.356.refs_6_
  9.5 1.3 reshape.357.refs_7_
  10.8 1.3 reshape.358.refs_8_
  12.0 7.1 %share1.1 = (bf16[2,544,3264]{2,1,0:T(8,128)(2,1)}, bf16[2,1,544]{2,1,0:T(2,128)(2,1)}, bf16[2,1,544]{2,1,0:T(2,128)(2,1)}, bf16[2,1,544]{2,1,0:T(2,128)(2,1)}, ...) custom-call(bf16[544,3264]{1,0:T(8,128)(2,1)} %refs_0_.1, ...), custom_call_target="tpu_custom_call" | custom-call | tf_op jit(solution)/shard_map/share1/pallas_call | solution.py:519
  19.2 0.7 convert_reduce_fusion.12
  21.5 5.6 fusion.1
  27.5 1.5 pad_maximum_fusion.1.refs_0_
  29.9 1.1 add_convert_fusion.2.refs_6_
  31.0 1.1 copy.71
  32.0 44.0 %exchange2.1 = (bf16[16,256,256]{2,1,0:T(8,128)(2,1)}, bf16[2,64,128]{2,1,0:T(8,128)(2,1)}, s32[16,2,128]{2,1,0:T(2,128)}, bf16[2,544,1088]{2,1,0:T(8,128)(2,1)}...) custom-call(bf16[16,256,256]{2,1,0:T(8,128)(2,1)} %pad_maximum_fusio, ...), custom_call_target="tpu_custom_call" | custom-call | tf_op jit(solution)/shard_map/exchange2/pallas_call | solution.py:472
  76.7 1.4 add_maximum_fusion
  78.8 2.6 broadcast_in_dim.47.places
  82.3 24.4 %attend.1 = (bf16[16,64,256]{2,1,0:T(8,128)(2,1)}, bf16[2,64,128]{2,1,0:T(8,128)(2,1)}, f32[17,64,256]{2,1,0:T(8,128)}, f32[17,1,256]{2,1,0:T(1,128)}) custom-call(bf16[16,256,256]{2,1,0:T(8,128)(2,1)} %get-tuple-element.60.got, bf16[2,64,128]{2,1,0:T(8,128)(2,1)} %get-tuple-element.61.last, s32[17,1,256]{2,1,0:T(1,128)} %broadcast_in_dim.46.limit, ...), custom_call_target="tpu_custom_call" | custom-call | tf_op jit(solution)/shard_map/attend/pallas_call | solution.py:597
  106.7 28.3 %exchange3.1 = (bf16[16,64,256]{2,1,0:T(8,128)(2,1)}, bf16[2,64,128]{2,1,0:T(8,128)(2,1)}) custom-call(bf16[16,64,256]{2,1,0:T(8,128)(2,1)} %get-tuple-element.63.refs_0_, bf16[2,64,128]{2,1,0:T(8,128)(2,1)} %get-tuple-element.64.refs_1_), custom_call_target="tpu_custom_call" | custom-call | tf_op jit(solution)/shard_map/exchange3/pallas_call | solution.py:472
  135.8 1.9 maximum_maximum_fusion.refs_5_
  138.4 3.0 fusion.61
  143.1 1.0 add_convert_fusion.1.refs_3_
  144.1 5.6 fusion.21
  149.7 5.4 fusion.24
  155.2 11.8 %convert_reduce_fusion = (f32[4352]{0:T(1024)}, bf16[256,4352]{1,0:T(8,128)(2,1)S(1)}, bf16[256,4352]{1,0:T(8,128)(2,1)}) fusion(f32[256,2176]{1,0:T(8,128)} %fusion.24, f32[256,2176]{1,0:T(8,128)} %fusion.21, f32[4352]{0:T(1024)S(1)} %reshape.393, bf16[256,1088]{1,0:T(8,128)(2,1)S(1)} %add_convert_fusion.1.refs_3_, bf16[1088,4352]{1,0:T(8,128)(2,1)} %bitcast.157), kind=kOutput, calls=%fused_computation.26 | convolution fusion | flops 2453270272 | bytes 18974720 | tf_op jit(solution)/shard_map/dot_general | solution.py:1177
  167.0 8.7 %fusion.63 = (f32[1088]{0:T(1024)}, f32[256,1088]{0,1:T(8,128)}) fusion(bf16[256,4352]{1,0:T(8,128)(2,1)S(1)} %get-tuple-element.155.refs_4_, bf16[1088,4352]{1,0:T(8,128)(2,1)} %bitcast.158), kind=kOutput, calls=%fused_computation.148 | convolution fusion | flops 2424585216 | bytes 12816640 | tf_op jit(solution)/shard_map/dot_general | solution.py:40
  175.8 1.6 copy.79
  177.4 2.0 multiply_reduce_fusion
  179.5 2.5 fusion.56
  182.1 0.9 convolution_convert_fusion
  183.6 0.8 slice.209
  184.5 16.1 %exchange4.1 = (bf16[16,64,256]{2,1,0:T(8,128)(2,1)}, bf16[2,64,128]{2,1,0:T(8,128)(2,1)}, bf16[2,256,2176]{2,1,0:T(8,128)(2,1)}, bf16[2,256,1088]{2,1,0:T(8,128...) custom-call(bf16[16,64,256]{2,1,0:T(8,128)(2,1)} %bitcast.142, ...), custom_call_target="tpu_custom_call" | custom-call | tf_op jit(solution)/shard_map/exchange4/pallas_call | solution.py:472
  200.6 33.4 %attend_grad.1 = (bf16[16,256,256]{2,1,0:T(8,128)(2,1)}, bf16[2,64,128]{2,1,0:T(8,128)(2,1)}) custom-call(bf16[16,256,256]{2,1,0:T(8,128)(2,1)} %get-tuple-element.60.got, bf16[2,64,128]{2,1,0:T(8,128)(2,1)} %get-tuple-element.61.last, s32[17,1,256]{2,1,0:T(1,128)} %broadcast_in_dim.46.limit, s32[3,2048,128]{2,1,0:T(8,128)} %broadcast_in_dim.47.places, ...), custom_call_target="tpu_custom_call" | custom-call | tf_op jit(solution)/shard_map/attend_grad/pallas_call | solution.py:696
  234.0 40.4 %exchange5.1 = (bf16[16,256,256]{2,1,0:T(8,128)(2,1)}, bf16[2,64,128]{2,1,0:T(8,128)(2,1)}) custom-call(bf16[16,256,256]{2,1,0:T(8,128)(2,1)} %get-tuple-element.79.refs_0_, bf16[2,64,128]{2,1,0:T(8,128)(2,1)} %get-tuple-element.80.refs_1_), custom_call_target="tpu_custom_call" | custom-call | tf_op jit(solution)/shard_map/exchange5/pallas_call | solution.py:472
  274.4 1.5 fusion.57
  275.9 1.1 bitcast_reduce_fusion
  278.4 7.3 %fusion.62 = (f32[1088]{0:T(1024)}, f32[256,1088]{0,1:T(8,128)}) fusion(bf16[1088,3264]{1,0:T(8,128)(2,1)} %bitcast.160, bf16[3264,256]{1,0:T(8,128)(2,1)S(1)} %maximum_dynamic-update-slice_fusion.refs_0_), kind=kOutput, calls=%fused_computation.147 | convolution fusion | flops 1818508288 | bytes 9892096 | tf_op jit(solution)/shard_map/dot_general | solution.py:313
  285.7 2.6 copy.80
  288.4 2.5 multiply_reduce_fusion.1
  293.8 1.4 reshape_broadcast_in_dim.3
  295.2 1.3 convert_reduce_fusion.1
  297.7 2.8 concatenate.68
  300.6 3.9 share6.1
  304.5 4.9 bitcast_convert_fusion.1
  309.4 2.1 pad.9.refs_3_
  311.5 0.9 fusion.27
  312.4 1.2 pad.8.refs_2_
  313.6 0.9 copy-done.13
  314.5 5.1 bitcast_convert_fusion.refs_1_
  319.6 5.2 fusion.refs_0_
  324.8 262.3 %sum_grads7.1 = (bf16[1088,2176]{1,0:T(8,128)(2,1)}, bf16[544,4352]{1,0:T(8,128)(2,1)}, bf16[544,1280]{1,0:T(8,128)(2,1)}, bf16[544,3328]{1,0:T(8,128)(2,1)}, f32[2,8,1088]{2,1,0:T(8,128)}) custom-call(bf16[1088,2176]{1,0:T(8,128)(2,1)} %fusion.refs_0_, bf16[544,4352]{1,0:T(8,128)(2,1)} %bitcast_convert_fusion.refs_1_, bf16[544,1280]{1,0:T(8,128)(2,1)} %pad.8.refs_2_, ...), custom_call_target="tpu_custom_call" | custom-call | tf_op jit(solution)/shard_map/sum_grads7/pallas_call | solution.py:1037
  587.1 6.9 %convert_bitcast_fusion = f32[2176,1088]{0,1:T(8,128)} fusion(bf16[1088,2176]{1,0:T(8,128)(2,1)} %get-tuple-element.94), kind=kLoop, calls=%fused_computation.3 | loop fusion | flops 2367488 | bytes 14204928 | tf_op jit(solution)/shard_map/transpose | solution.py:1304
  594.0 4.5 convert_element_type.243
  598.4 3.6 slice_convert_fusion
  602.0 1.6 slice_convert_fusion.1
  604.3 1.9 fusion.45
  606.1 1.4 constant_dynamic-slice_fusion.7
  607.5 1.4 reshape.383
  608.9 2.7 add_convert_fusion
  611.6 2.1 copy.88
  613.8 4.5 fusion.29
  618.3 4.1 fusion.35
  622.4 1.1 copy.87
  (163 shorter events, 15.0 us)
Async XLA Ops:
  12.0 8.0 %copy-start.1 = (bf16[2,1,128,1088]{2,3,1,0:T(8,128)(2,1)S(1)}, bf16[2,1,128,1088]{2,3,1,0:T(8,128)(2,1)}, u32[]{:S(2)}) copy-start(bf16[2,1,128,1088]{2,3,1,0:T(8,128)(2,1)} %param.17) | copy-start | bytes 1671172
  20.1 1.0 copy-start.32
  20.1 1.0 copy-start.33
  20.2 9.6 %copy-start.23 = (f32[256]{0:T(256)}, f32[256]{0:T(256)S(1)}, u32[]{:S(2)}) copy-start(f32[256]{0:T(256)S(1)} %get-tuple-element.186) | copy-start | bytes 3076
  20.4 9.4 %copy-start.24 = (f32[256]{0:T(256)}, f32[256]{0:T(256)S(1)}, u32[]{:S(2)}) copy-start(f32[256]{0:T(256)S(1)} %get-tuple-element.188) | copy-start | bytes 3076
  29.6 1.4 copy-start.11
  32.0 44.1 %copy-start.41 = (s32[2,1]{0,1:T(1,128)S(1)}, s32[2,1]{0,1:T(1,128)}, u32[]{:S(2)}) copy-start(s32[2,1]{0,1:T(1,128)} %param.20) | copy-start | bytes 28
  76.1 5.3 copy-start.14
  106.7 31.0 %copy-start.30 = (bf16[2,1,544]{2,1,0:T(2,128)(2,1)S(1)}, bf16[2,1,544]{2,1,0:T(2,128)(2,1)}, u32[]{:S(2)}) copy-start(bf16[2,1,544]{2,1,0:T(2,128)(2,1)} %get-tuple-element.68) | copy-start | bytes 6532
  106.7 31.0 %copy-start.31 = (bf16[2,1,544]{2,1,0:T(2,128)(2,1)S(1)}, bf16[2,1,544]{2,1,0:T(2,128)(2,1)}, u32[]{:S(2)}) copy-start(bf16[2,1,544]{2,1,0:T(2,128)(2,1)} %get-tuple-element.69) | copy-start | bytes 6532
  138.4 3.9 copy-start.28
  138.4 3.9 copy-start.29
  141.4 2.7 copy-start.2
  141.5 1.0 copy-start.19
  144.1 11.1 %copy-start.8 = (bf16[256,1088]{1,0:T(8,128)(2,1)}, bf16[256,1088]{1,0:T(8,128)(2,1)S(1)}, u32[]{:S(2)}) copy-start(bf16[256,1088]{1,0:T(8,128)(2,1)S(1)} %add_convert_fusion.1.refs_3_) | copy-start | bytes 1671172
  149.7 5.4 copy-start.22
  167.0 8.7 %copy-start.10 = (bf16[256,4352]{1,0:T(8,128)(2,1)}, bf16[256,4352]{1,0:T(8,128)(2,1)S(1)}, u32[]{:S(2)}) copy-start(bf16[256,4352]{1,0:T(8,128)(2,1)S(1)} %get-tuple-element.155.refs_4_) | copy-start | bytes 6684676
  177.4 2.1 copy-start
  177.4 2.1 copy-start.3
  177.4 2.1 copy-start.20
  177.4 2.1 copy-start.25
  179.5 2.6 copy-start.36
  182.1 0.9 copy-start.7
  274.4 3.0 copy-start.18
  278.4 7.3 %copy-start.6 = (bf16[3264,256]{1,0:T(8,128)(2,1)}, bf16[3264,256]{1,0:T(8,128)(2,1)S(1)}, u32[]{:S(2)}) copy-start(bf16[3264,256]{1,0:T(8,128)(2,1)S(1)} %maximum_dynamic-update-slice_fusion.refs_0_) | copy-start | bytes 5013508
  288.3 3.1 copy-start.27
  288.3 3.7 copy-start.17
  288.4 4.3 copy-start.16
  288.4 4.9 copy-start.26
  309.4 2.1 copy-start.39
  309.4 2.1 copy-start.40
  309.4 4.2 slice-start
  311.5 2.1 slice-start.1
  312.4 2.1 copy-start.13
  314.5 5.1 copy-start.37
  314.5 5.1 copy-start.38
  587.1 6.9 %copy-start.4 = (bf16[544,4352]{1,0:T(8,128)(2,1)S(1)}, bf16[544,4352]{1,0:T(8,128)(2,1)}, u32[]{:S(2)}) copy-start(bf16[544,4352]{1,0:T(8,128)(2,1)} %get-tuple-element.93) | copy-start | bytes 14204932
  594.0 4.5 copy-start.5
  598.4 3.6 copy-start.12
  602.0 1.6 copy-start.15
  602.0 6.9 %copy-start.35 = (f32[256]{0:T(256)S(1)}, f32[256]{0:T(256)}, u32[]{:S(2)}) copy-start(f32[256]{0:T(256)} %get-tuple-element.143) | copy-start | bytes 3076
  602.0 6.9 %copy-start.34 = (f32[256]{0:T(256)S(1)}, f32[256]{0:T(256)}, u32[]{:S(2)}) copy-start(f32[256]{0:T(256)} %get-tuple-element.144) | copy-start | bytes 3076
  608.9 4.8 copy-start.21
  613.8 4.6 copy-start.9

commit v4 on v3

--- a/solution.py
+++ b/solution.py
@@ -565,7 +565,7 @@
     def block(b, carry):
         u = b // per_unit
         scores = jnp.dot(keys[u], queries[b], preferred_element_type=jnp.float32)
-        place = places[u]
+        place = places[jnp.where(u == 2, lax.axis_index("replica") // (peers // 2), u)]
         place = jnp.concatenate([place, place], axis=1)
         scores = jnp.where(place < limit[b], scores, -1e30)
         high = jnp.max(scores, axis=0, keepdims=True)
@@ -613,109 +613,6 @@
     )(got, last, limit, places)
 
 
-def attend_grad_body(
-    got,
-    last,
-    limit,
-    places,
-    out_f,
-    lse,
-    grad_got,
-    grad_last,
-    sent,
-    last_sent,
-    keys,
-    keys_t,
-    values,
-    queries,
-    grads,
-    queries_n,
-    grads_n,
-    dqs,
-    dk,
-    dv,
-):
-    peers = got.shape[0]
-    nblocks = queries.shape[0]
-    per_unit = (nblocks - 1) // 2
-    unpack_units(got, last, 0, queries)
-    unpack_units(grad_got, grad_last, 0, grads)
-    for u in range(3):
-        for s in range(peers):
-            span = slice(s * 128, (s + 1) * 128)
-            part = unit_source(got, u, s, 64)
-            keys[u, span, :] = part.T
-            keys_t[u, :, span] = part
-            values[u, span, :] = unit_source(got, u, s, 128).T
-    for b in range(nblocks):
-        queries_n[b] = queries[b].T
-        grads_n[b] = grads[b].T
-    dk[...] = jnp.zeros_like(dk)
-    dv[...] = jnp.zeros_like(dv)
-
-    def block(b, carry):
-        u = b // per_unit
-        grad = grads[b]
-        delta = jnp.sum(grad.astype(jnp.float32) * out_f[b], axis=0, keepdims=True)
-        scores = jnp.dot(keys[u], queries[b], preferred_element_type=jnp.float32)
-        place = places[u]
-        place = jnp.concatenate([place, place], axis=1)
-        scores = jnp.where(place < limit[b], scores, -1e30)
-        probs = jnp.exp(scores - lse[b])
-        grad_probs = jnp.dot(values[u], grad, preferred_element_type=jnp.float32)
-        grad_scores = (probs * (grad_probs - delta)).astype(jnp.bfloat16)
-        dqs[b] = jnp.dot(keys_t[u], grad_scores, preferred_element_type=jnp.float32)
-        dk[u] += jnp.dot(grad_scores, queries_n[b], preferred_element_type=jnp.float32)
-        dv[u] += jnp.dot(probs.astype(jnp.bfloat16), grads_n[b], preferred_element_type=jnp.float32)
-        return carry
-
-    lax.fori_loop(0, nblocks, block, 0)
-    half = BLOCK // 128
-    scale = HEAD_DIM ** (-0.5)
-    for m in range(2):
-        for s in range(peers):
-            at = slice(m * 128, (m + 1) * 128)
-            span = slice(s * 128, (s + 1) * 128)
-            dq = dqs[m * per_unit + s // half, :, (s % half) * 128 : (s % half + 1) * 128]
-            sent[s, 0:64, at] = (dq * scale).astype(jnp.bfloat16)
-            sent[s, 64:128, at] = dk[m, span, :].T.astype(jnp.bfloat16)
-            sent[s, 128:192, at] = dv[m, span, :].T.astype(jnp.bfloat16)
-    for s in range(peers):
-        span = slice(s * 128, (s + 1) * 128)
-        sent[s, 192:256, 0:128] = dk[2, span, :].T.astype(jnp.bfloat16)
-        sent[s, 192:256, 128:256] = dv[2, span, :].T.astype(jnp.bfloat16)
-    for j in range(2):
-        last_sent[j] = (dqs[nblocks - 1, :, j * 128 : (j + 1) * 128] * scale).astype(jnp.bfloat16)
-
-
-def attend_grad(got, last, limit, places, out_f, lse, grad_got, grad_last):
-    peers = got.shape[0]
-    nblocks = limit.shape[0]
-    length = places.shape[1]
-    bf, f32 = jnp.bfloat16, jnp.float32
-    return pl.pallas_call(
-        attend_grad_body,
-        out_shape=[
-            jax.ShapeDtypeStruct((peers, 256, 256), bf),
-            jax.ShapeDtypeStruct((2, 64, 128), bf),
-        ],
-        scratch_shapes=[
-            pltpu.VMEM((3, length, 64), bf),
-            pltpu.VMEM((3, 64, length), bf),
-            pltpu.VMEM((3, length, 64), bf),
-            pltpu.VMEM((nblocks, 64, BLOCK), bf),
-            pltpu.VMEM((nblocks, 64, BLOCK), bf),
-            pltpu.VMEM((nblocks, BLOCK, 64), bf),
-            pltpu.VMEM((nblocks, BLOCK, 64), bf),
-            pltpu.VMEM((nblocks, 64, BLOCK), f32),
-            pltpu.VMEM((3, length, 64), f32),
-            pltpu.VMEM((3, length, 64), f32),
-        ],
-        compiler_params=pltpu.CompilerParams(vmem_limit_bytes=60 << 20),
-        name="attend_grad",
-    )(got, last, limit, places, out_f, lse, grad_got, grad_last)
-
-
 ROWS = 272
 PART = 80
 PADDED = 4 * PART
@@ -753,12 +650,12 @@
 
 
 class Summer:
-    def __init__(self, plan, sources, results, own, came, second_in, quarter, parts, gathered, sems):
+    def __init__(self, plan, sources, results, own, came, second_in, parts, summed, gathered, sems):
         self.plan, self.sources, self.results = plan, sources, results
         self.own, self.came, self.second_in = own, came, second_in
-        self.quarter, self.parts, self.gathered = quarter, parts, gathered
-        self.load_sem, self.store_sem = sems[0], sems[1]
-        self.pairs = [tuple(sems[2 + 2 * i : 4 + 2 * i]) for i in range(6)]
+        self.parts, self.summed, self.gathered = parts, summed, gathered
+        self.load_sem, self.store_sem, self.keep_sem = sems[0], sems[1], sems[2]
+        self.pairs = [tuple(sems[3 + 2 * i : 5 + 2 * i]) for i in range(6)]
         here, group = lax.axis_index("replica"), lax.axis_index("group")
         bit_x, bit_y = here % 2, (here // 2) % 2
         self.here, self.place = here, here // 4
@@ -787,7 +684,8 @@
     def load(self, c, j):
         item = self.plan[c]
         source = piece(self.sources[item[0]], item, self.one, j)
-        return pltpu.make_async_copy(source, self.own[c].at[j], self.load_sem.at[c, j])
+        target = self.own[c].at[j, pl.ds(0, ROWS)]
+        return pltpu.make_async_copy(source, target, self.load_sem.at[c, j])
 
     def first(self, c, j):
         item = self.plan[c]
@@ -795,15 +693,20 @@
         return self.copy(0, (c, j), source, self.came[c].at[j], self.peer_one)
 
     def second(self, c):
-        return self.copy(1, (c,), self.own[c].at[1 - self.two], self.second_in[c], self.peer_two)
+        source = self.own[c].at[1 - self.two, pl.ds(0, ROWS)]
+        return self.copy(1, (c,), source, self.second_in[c], self.peer_two)
 
     def spread(self, c, k):
-        source = self.quarter[c].at[self.block(lax.rem(self.place + k, 4))]
+        source = self.own[c].at[self.two, self.block(lax.rem(self.place + k, 4))]
         return self.copy(2, (c, k - 1), source, self.parts[c].at[k - 1], self.z_peer(k))
 
     def gather(self, c, k):
-        block = self.gathered[c].at[self.block(self.place)]
-        return self.copy(3, (c, k - 1), block, block, self.z_peer(k))
+        target = self.gathered[c].at[self.block(self.place)]
+        return self.copy(3, (c, k - 1), self.summed[c], target, self.z_peer(k))
+
+    def keep(self, c):
+        target = self.gathered[c].at[self.block(self.place)]
+        return pltpu.make_async_copy(self.summed[c], target, self.keep_sem.at[c])
 
     def result(self, c, other):
         item = self.plan[c]
@@ -831,17 +734,23 @@
         source = self.result(c, 1) if other else self.gathered[c].at[pl.ds(0, ROWS)]
         return self.copy(5, (c, other), source, target, self.peer_one)
 
+    def fetch(self, c):
+        target = self.came[c].at[self.two]
+        return pltpu.make_async_copy(
+            self.gathered[c].at[pl.ds(0, ROWS)], target, self.store_sem.at[c]
+        )
+
     def store(self, c):
         return pltpu.make_async_copy(
-            self.gathered[c].at[pl.ds(0, ROWS)], self.result(c, 0), self.store_sem.at[c]
+            self.came[c].at[self.two], self.result(c, 0), self.store_sem.at[c]
         )
 
     def begin(self, c):
         for j in range(2):
             self.first(c, j).start()
             self.load(c, j).start()
-        width = self.quarter[c].shape[1]
-        self.quarter[c][ROWS:, :] = jnp.zeros((PADDED - ROWS, width), jnp.bfloat16)
+        width = self.own[c].shape[2]
+        self.own[c][self.two, ROWS:, :] = jnp.zeros((PADDED - ROWS, width), jnp.bfloat16)
 
     def stage_one(self, c):
         for j in range(2):
@@ -865,7 +774,7 @@
             rows = pl.ds(start, 16)
             total = own[keep, rows].astype(jnp.float32) + came[keep, rows].astype(jnp.float32)
             total = total + self.second_in[c][rows].astype(jnp.float32)
-            self.quarter[c][rows] = total.astype(jnp.bfloat16)
+            own[keep, rows] = total.astype(jnp.bfloat16)
 
         by_rows(ROWS, add)
         for k in (1, 2, 3):
@@ -877,26 +786,30 @@
 
         def add(start):
             at = pl.ds(pl.multiple_of(self.place * PART + start, 16), 16)
-            total = self.quarter[c][at].astype(jnp.float32)
+            total = self.own[c][self.two, at].astype(jnp.float32)
             for k in range(3):
                 total = total + self.parts[c][k, pl.ds(start, 16)].astype(jnp.float32)
-            self.gathered[c][at] = total.astype(jnp.bfloat16)
+            self.summed[c][pl.ds(start, 16)] = total.astype(jnp.bfloat16)
 
         by_rows(PART, add)
         for k in (1, 2, 3):
             self.gather(c, k).start()
+        self.keep(c).start()
 
     def stage_four(self, c):
         for k in (1, 2, 3):
             self.spread(c, k).wait_send()
             self.gather(c, k).wait_recv()
+        self.keep(c).wait()
         self.cross(c).start()
         self.final(c, 0).start()
-        self.store(c).start()
+        self.fetch(c).start()
 
     def stage_five(self, c):
         self.crossed(c).wait_recv()
         self.final(c, 1).start()
+        self.fetch(c).wait()
+        self.store(c).start()
 
     def end(self, c):
         for j in range(2):
@@ -982,30 +895,9 @@
         self.back().wait()
 
 
-def sum_grads_body(plan, *refs):
-    nchunks = len(plan)
-    sources, small, results, small_out = refs[0:4], refs[4], refs[5:9], refs[9]
-    refs = list(refs[10:])
-    buffers = [[refs.pop(0) for _ in range(nchunks)] for _ in range(6)]
-    from_core, own_small, everyone = (refs.pop(0) for _ in range(3))
-    summer = Summer(plan, sources, results, *buffers, refs[:14])
-    smalls = SmallSum(small, small_out, from_core, own_small, everyone, refs[14:20])
-    greet(everyone.shape[0], lax.axis_index("replica"), True)
-    smalls.begin()
-    for c in range(nchunks):
-        summer.begin(c)
-    smalls.middle()
-    for stage, c in wavefront(range(nchunks)):
-        summer.run(stage, c)
-    smalls.finish()
-    smalls.end()
-    for c in range(nchunks):
-        summer.end(c)
-
-
 def sum_buffers(plan):
     bf = jnp.bfloat16
-    shapes = ((2, ROWS), (2, ROWS), (ROWS,), (PADDED,), (3, PART), (PADDED,))
+    shapes = ((2, PADDED), (2, ROWS), (ROWS,), (3, PART), (PART,))
     return [pltpu.VMEM(shape + (item[1],), bf) for shape in shapes for item in plan]
 
 
@@ -1014,7 +906,7 @@
     count = len(plan)
     pairs, triples, ones = dma((count, 2)), dma((count, 3)), dma((count,))
     stages = (pairs, ones, triples, triples, ones, pairs)
-    return [pairs, ones] + [sem for stage in stages for sem in (stage, stage)]
+    return [pairs, ones, ones] + [sem for stage in stages for sem in (stage, stage)]
 
 
 def small_scratch(shape, peers):
@@ -1027,28 +919,316 @@
     return [dma, dma, dma((peers,)), dma((peers,)), dma, dma]
 
 
-def sum_grads(ident, *arrays):
-    *arrays, small = arrays
+def small_body(small, result, from_core, own, everyone, *sems):
+    smalls = SmallSum(small, result, from_core, own, everyone, sems)
+    greet(everyone.shape[0], lax.axis_index("replica"), True)
+    smalls.begin()
+    smalls.middle()
+    smalls.finish()
+    smalls.end()
+
+
+def sum_small(ident, small):
+    peers = lax.axis_size("replica")
+    vmem = pl.BlockSpec(memory_space=pltpu.VMEM)
+    return pl.pallas_call(
+        small_body,
+        out_shape=jax.ShapeDtypeStruct(small.shape, small.dtype),
+        in_specs=[vmem],
+        out_specs=vmem,
+        scratch_shapes=small_scratch(small.shape[1:], peers) + small_sems(peers),
+        compiler_params=pltpu.CompilerParams(collective_id=ident, has_side_effects=True),
+        name=f"small{ident}",
+    )(small)
+
+
+JOINED = 3328
+
+
+def backward_body(plan, *refs):
+    refs = list(refs)
+    nchunks = len(plan)
+    got, last, limit, places, out_f, lse, grad_got, grad_last, firsts = (
+        refs.pop(0) for _ in range(9)
+    )
+    sources = [refs.pop(0) for _ in range(3)]
+    results = [refs.pop(0) for _ in range(4)]
+    joined_out = refs.pop(0)
+    gathered = [refs.pop(0) for _ in range(nchunks)]
+    buffers = [[refs.pop(0) for _ in range(nchunks)] for _ in range(5)]
+    (
+        keys,
+        keys_t,
+        values,
+        queries,
+        grads,
+        queries_n,
+        grads_n,
+        dqs,
+        dk,
+        dv,
+        sent,
+        back,
+        last_sent,
+        back_last,
+        joined,
+        rest,
+    ) = (refs.pop(0) for _ in range(16))
+    back_send, back_recv, last_send, last_recv, joined_send, joined_recv, joined_own = (
+        refs.pop(0) for _ in range(7)
+    )
+    summer = Summer(plan, sources + [rest], results, *buffers, gathered, refs)
+    here, group = lax.axis_index("replica"), lax.axis_index("group")
+    peers = got.shape[0]
+    half_peers = peers // 2
+    nblocks = queries.shape[0]
+    per_unit = (nblocks - 1) // 2
+    half = BLOCK // 128
+    scale = HEAD_DIM ** (-0.5)
+    greet(peers, here, True)
+    summer.begin(0)
+    summer.begin(1)
+
+    kinds = (
+        (pl.ds(192, 64), pl.ds(0, 256)),
+        (pl.ds(0, 192), pl.ds(0, 128)),
+        (pl.ds(0, 192), pl.ds(128, 128)),
+    )
+
+    def back_copy(kind, step):
+        peer = lax.rem(here + step, peers)
+        rows, columns = kinds[kind]
+        return pltpu.make_async_remote_copy(
+            sent.at[peer, rows, columns],
+            back.at[here, rows, columns],
+            back_send.at[kind, step],
+            back_recv.at[kind, step],
+            device_id={"replica": peer},
+            device_id_type=MESH,
+        )
+
+    def last_copy(slot, target_slot):
+        target = lax.rem(here - 1 + peers, half_peers) + half_peers * slot
+        return pltpu.make_async_remote_copy(
+            last_sent.at[slot],
+            back_last.at[target_slot],
+            last_send.at[slot],
+            last_recv.at[target_slot],
+            device_id={"replica": target},
+            device_id_type=MESH,
+        )
+
+    unpack_units(got, last, 0, queries)
+    unpack_units(grad_got, grad_last, 0, grads)
+    for u in range(3):
+        for s in range(peers):
+            span = slice(s * 128, (s + 1) * 128)
+            part = unit_source(got, u, s, 64)
+            keys[u, span, :] = part.T
+            keys_t[u, :, span] = part
+            values[u, span, :] = unit_source(got, u, s, 128).T
+
+    def natural(b, carry):
+        queries_n[b] = queries[b].T
+        grads_n[b] = grads[b].T
+        return carry
+
+    lax.fori_loop(0, nblocks, natural, 0)
+
+    def clear():
+        dk[...] = jnp.zeros_like(dk)
+        dv[...] = jnp.zeros_like(dv)
+
+    def finish_last():
+        for s in range(peers):
+            span = slice(s * 128, (s + 1) * 128)
+            sent[s, 192:256, 0:128] = dk[span, :].T.astype(jnp.bfloat16)
+            sent[s, 192:256, 128:256] = dv[span, :].T.astype(jnp.bfloat16)
+        for j in range(2):
+            last_sent[j] = (dqs[nblocks - 1, :, j * 128 : (j + 1) * 128] * scale).astype(
+                jnp.bfloat16
+            )
+        for slot in range(2):
+            last_copy(slot, here // half_peers).start()
+        for step in range(1, peers):
+            back_copy(0, step).start()
+        clear()
+
+    def finish_unit(m):
+        at = slice(m * 128, (m + 1) * 128)
+        for s in range(peers):
+            span = slice(s * 128, (s + 1) * 128)
+            dq = dqs[m * per_unit + s // half, :, (s % half) * 128 : (s % half + 1) * 128]
+            sent[s, 0:64, at] = (dq * scale).astype(jnp.bfloat16)
+            sent[s, 64:128, at] = dk[span, :].T.astype(jnp.bfloat16)
+            sent[s, 128:192, at] = dv[span, :].T.astype(jnp.bfloat16)
+        for step in range(1, peers):
+            back_copy(1 + m, step).start()
+        clear()
+
+    def block(i, carry):
+        is_last = i == 0
+        b = jnp.where(is_last, nblocks - 1, i - 1)
+        u = jnp.where(is_last, 2, (i - 1) // per_unit)
+        grad = grads[b]
+        delta = jnp.sum(grad.astype(jnp.float32) * out_f[b], axis=0, keepdims=True)
+        scores = jnp.dot(keys[u], queries[b], preferred_element_type=jnp.float32)
+        place = places[jnp.where(is_last, here // half_peers, u)]
+        place = jnp.concatenate([place, place], axis=1)
+        scores = jnp.where(place < limit[b], scores, -1e30)
+        probs = jnp.exp(scores - lse[b])
+        grad_probs = jnp.dot(values[u], grad, preferred_element_type=jnp.float32)
+        grad_scores = (probs * (grad_probs - delta)).astype(jnp.bfloat16)
+        dqs[b] = jnp.dot(keys_t[u], grad_scores, preferred_element_type=jnp.float32)
+        dk[...] += jnp.dot(grad_scores, queries_n[b], preferred_element_type=jnp.float32)
+        dv[...] += jnp.dot(probs.astype(jnp.bfloat16), grads_n[b], preferred_element_type=jnp.float32)
+        pl.when(is_last)(finish_last)
+
+        @pl.when(i == per_unit - 1)
+        def _():
+            summer.stage_one(0)
+
+        @pl.when(i == per_unit)
+        def _():
+            finish_unit(0)
+            summer.begin(2)
+
+        @pl.when(i == 2 * per_unit - 3)
+        def _():
+            summer.stage_one(1)
+            summer.stage_two(0)
+
+        return carry
+
+    clear()
+    lax.fori_loop(0, nblocks, block, 0)
+    finish_unit(1)
+    back[here] = sent[here]
+    summer.begin(3)
+    summer.begin(4)
+    done = {(0, 0), (0, 1), (1, 0)}
+    order = [step for step in wavefront(range(nchunks)) if step not in done]
+    early = [(0, 2), (1, 1), (2, 0)]
+    for step in early:
+        summer.run(*step)
+        order.remove(step)
+
+    for slot in range(2):
+        last_copy(slot, slot).wait_recv()
+    for kind in range(3):
+        for step in range(1, peers):
+            back_copy(kind, step).wait_recv()
+    for h in range(peers):
+        for part in range(3):
+            row = part * (HEADS * HEAD_DIM) + h * HEAD_DIM
+            joined[group, row : row + HEAD_DIM, :] = back[h, part * 64 : part * 64 + 64, :]
+    width = HEADS * HEAD_DIM
+    tail = (HEADS - 1) * HEAD_DIM
+    for m in range(2):
+        at = slice(m * 128, (m + 1) * 128)
+        joined[group, tail:width, at] = back_last[m]
+        for part in (1, 2):
+            columns = slice((part - 1) * 128, part * 128)
+            total = back[m * half_peers, 192:256, columns].astype(jnp.float32)
+            for i in range(1, half_peers):
+                total = total + back[m * half_peers + i, 192:256, columns].astype(jnp.float32)
+            row = part * width + tail
+            joined[group, row : row + HEAD_DIM, at] = total.astype(jnp.bfloat16)
+    joined[group, 3 * width :, :] = jnp.zeros((JOINED - 3 * width, 256), jnp.bfloat16)
+    share_joined = pltpu.make_async_remote_copy(
+        joined.at[group],
+        joined.at[group],
+        joined_send,
+        joined_recv,
+        device_id={"group": 1 - group},
+        device_id_type=MESH,
+    )
+    share_joined.start()
+    keep_joined = pltpu.make_async_copy(joined.at[group], joined_out, joined_own)
+    keep_joined.start()
+    for step in [(1, 2), (2, 1), (0, 3)]:
+        summer.run(*step)
+        order.remove(step)
+    share_joined.wait_recv()
+
+    def weights(n, carry):
+        columns = pl.ds(pl.multiple_of(n * 256, 256), 256)
+        total = jnp.zeros((firsts.shape[1], 256), jnp.float32)
+        for core in range(2):
+            total = total + lax.dot_general(
+                firsts[core],
+                joined[core, columns, :],
+                (((1,), (1,)), ((), ())),
+                preferred_element_type=jnp.float32,
+            )
+        rest[:, columns] = total.astype(jnp.bfloat16)
+        return carry
+
+    lax.fori_loop(0, JOINED // 256, weights, 0)
+    summer.begin(5)
+    summer.begin(6)
+    for step in order:
+        summer.run(*step)
+    share_joined.wait_send()
+    keep_joined.wait()
+    for slot in range(2):
+        last_copy(slot, slot).wait_send()
+    for kind in range(3):
+        for step in range(1, peers):
+            back_copy(kind, step).wait_send()
+    for c in range(nchunks):
+        summer.end(c)
+
+
+def backward(ident, attention, firsts, arrays):
     plan = chunk_plan()
-    peers = lax.axis_size("replica")
+    got, _, limit = attention[:3]
+    peers, nblocks = got.shape[0], limit.shape[0]
+    length = peers * 128
     bf, f32 = jnp.bfloat16, jnp.float32
     any_spec = pl.BlockSpec(memory_space=pl.ANY)
     vmem = pl.BlockSpec(memory_space=pltpu.VMEM)
+    dma = pltpu.SemaphoreType.DMA
+    rest_shape = (firsts.shape[1], JOINED)
+    shapes = [a.shape for a in arrays] + [rest_shape, (JOINED, 256)]
+    shapes += [(PADDED, item[1]) for item in plan]
     return pl.pallas_call(
-        functools.partial(sum_grads_body, plan),
-        out_shape=[jax.ShapeDtypeStruct(a.shape, bf) for a in arrays]
-        + [jax.ShapeDtypeStruct(small.shape, f32)],
-        in_specs=[any_spec] * 4 + [vmem],
-        out_specs=[any_spec] * 4 + [vmem],
+        functools.partial(backward_body, plan),
+        out_shape=[jax.ShapeDtypeStruct(shape, bf) for shape in shapes],
+        in_specs=[vmem] * 9 + [any_spec] * 3,
+        out_specs=[any_spec] * len(shapes),
         scratch_shapes=sum_buffers(plan)
-        + small_scratch(small.shape[1:], peers)
-        + sum_sems(plan)
-        + small_sems(peers),
+        + [
+            pltpu.VMEM((3, length, 64), bf),
+            pltpu.VMEM((3, 64, length), bf),
+            pltpu.VMEM((3, length, 64), bf),
+            pltpu.VMEM((nblocks, 64, BLOCK), bf),
+            pltpu.VMEM((nblocks, 64, BLOCK), bf),
+            pltpu.VMEM((nblocks, BLOCK, 64), bf),
+            pltpu.VMEM((nblocks, BLOCK, 64), bf),
+            pltpu.VMEM((nblocks, 64, BLOCK), f32),
+            pltpu.VMEM((length, 64), f32),
+            pltpu.VMEM((length, 64), f32),
+            pltpu.VMEM((peers, 256, 256), bf),
+            pltpu.VMEM((peers, 256, 256), bf),
+            pltpu.VMEM((2, 64, 128), bf),
+            pltpu.VMEM((2, 64, 128), bf),
+            pltpu.VMEM((2, JOINED, 256), bf),
+            pltpu.VMEM(rest_shape, bf),
+            dma((3, peers)),
+            dma((3, peers)),
+            dma((2,)),
+            dma((2,)),
+            dma,
+            dma,
+            dma,
+        ]
+        + sum_sems(plan),
         compiler_params=pltpu.CompilerParams(
-            collective_id=ident, has_side_effects=True, vmem_limit_bytes=56 << 20
+            collective_id=ident, has_side_effects=True, vmem_limit_bytes=67043328
         ),
-        name=f"sum_grads{ident}",
-    )(*arrays, small)
+        name="backward",
+    )(*attention, firsts, *arrays)
 
 
 def norm_unit(values):
@@ -1142,7 +1322,8 @@
         chunk,
         split_last(queries[cut:]),
         positions.reshape(micro, rows_here),
-        [(item, "whole") for item in (w_attn_out, w_fc, w_proj.T, first, grad_low)],
+        [(item, "whole") for item in (w_attn_out, w_fc, w_proj.T)]
+        + [(first.T, "rows"), (grad_low, "whole")],
     )
     mat_out = mat_out.reshape(width, width)
     mat_fc = mat_fc.reshape(width, hidden_width)
@@ -1160,12 +1341,9 @@
         1,
     )
     limit = jnp.concatenate([limits.reshape(-1, BLOCK), own_limits], 0)[:, None, :]
-    unit_places = jnp.concatenate(
-        [place_rows, lax.dynamic_index_in_dim(place_rows, mine, 0, True)], 0
-    )
-    unit_places = jnp.broadcast_to(unit_places[:, :, None], unit_places.shape + (128,))
-
-    sent, sent_last, out_f, lse = attend(got, got_last, limit, unit_places)
+    key_places = jnp.broadcast_to(place_rows[:, :, None], place_rows.shape + (128,))
+
+    sent, sent_last, out_f, lse = attend(got, got_last, limit, key_places)
     heads_out, heads_last = exchange(3, -1, sent, sent_last)
     attended = jnp.concatenate(
         [heads_out.reshape(cut, count), jnp.concatenate([heads_last[0], heads_last[1]], 1)], 0
@@ -1227,34 +1405,16 @@
     grad_mat_fc = both(own_columns(seconds), grad_ins, (0, 1), (0, 1))
     grad_mat_out = both(attendeds, branches, (0, 2), (0, 1))
 
-    grad_sent, grad_sent_last = attend_grad(
-        got, got_last, limit, unit_places, out_f, lse, grad_got, grad_got_last
-    )
-    back, back_last = exchange(5, -1, grad_sent, grad_sent_last)
-    last_parts = back[:, 192:256, :].astype(f32).reshape(2, half, HEAD_DIM, 256)
-    last_sums = jnp.sum(last_parts, 1).astype(bf)
-    grad_query = jnp.concatenate(
-        [back[:, 0:64].reshape(cut, count), jnp.concatenate([back_last[0], back_last[1]], 1)], 0
-    )
-    grad_key = jnp.concatenate(
-        [
-            back[:, 64:128].reshape(cut, count),
-            jnp.concatenate([last_sums[0, :, :128], last_sums[1, :, :128]], 1),
-        ],
-        0,
-    )
-    grad_value = jnp.concatenate(
-        [
-            back[:, 128:192].reshape(cut, count),
-            jnp.concatenate([last_sums[0, :, 128:], last_sums[1, :, 128:]], 1),
-        ],
-        0,
-    )
-    grad_bias_query = jnp.sum(grad_query, 1, dtype=f32).reshape(1, width)
-    grad_bias_value = jnp.sum(grad_value, 1, dtype=f32).reshape(1, width)
-    grad_joined = jnp.concatenate([grad_query, grad_key, grad_value], 0)
-    (joined_pair,) = share(6, grad_joined)
-    grad_mat_qkv = both(own_columns(firsts), joined_pair, (0, 1), (0, 2))
+    sums = backward(
+        5,
+        (got, got_last, limit, key_places, out_f, lse, grad_got, grad_got_last),
+        firsts,
+        (grad_mat_proj_t, grad_mat_fc, jnp.pad(grad_mat_out, ((0, 0), (0, 1280 - width)))),
+    )
+    sum_proj_t, sum_fc, sum_out, sum_qkv, grad_joined = sums[:5]
+    grad_joined = grad_joined[: 3 * width]
+    grad_bias_query = jnp.sum(grad_joined[:width], 1, dtype=f32).reshape(1, width)
+    grad_bias_value = jnp.sum(grad_joined[2 * width :], 1, dtype=f32).reshape(1, width)
     grad_first = contract(grad_joined, mat_qkv, 0, 1)
     grad_rows_norm, grad_gain_one, grad_shift_one = norm_back(
         grad_first, unit_one, spread_one, gain_one
@@ -1276,14 +1436,7 @@
         ],
         0,
     )
-    sum_proj_t, sum_fc, sum_out, sum_qkv, small_sum = sum_grads(
-        7,
-        grad_mat_proj_t,
-        grad_mat_fc,
-        jnp.pad(grad_mat_out, ((0, 0), (0, 1280 - width))),
-        jnp.pad(grad_mat_qkv, ((0, 0), (0, 3328 - 3 * width))),
-        small_grads.reshape(2, 8, width),
-    )
+    small_sum = sum_small(6, small_grads.reshape(2, 8, width))
     own_rows = lax.dynamic_slice_in_dim(small_sum[0], group * part, part, 1)
     vec = [own_rows[i] for i in range(8)]
     bias_rows = lax.dynamic_slice_in_dim(small_sum[1], group * 2, 2, 0).reshape(-1)

time: 629 us -> 570 us (0.906)
  Pallas kernels: 460 us -> 425 us
  local copies, waits for them, and re-layouts: 47.8 us -> 34 us
  other arithmetic: 41.3 us -> 31.9 us
    pallas_call x4 -> x3, Pallas kernels: 129 us -> 89 us  [exchange(): pl.pallas_call(functools.partial(exchange_body, direction, with_places, m...]
    pallas_call x2, Pallas kernels: 296 us -> 305 us  [the longest x1 282 us: backward(): pl.pallas_call(functools.partial(backward_body, plan), out_shape=[jax.Sha...]
    dot_general x4 -> x3, matrix products: 16.1 us -> 15 us  [both(): lax.dot_general(left, right, ((left_dims, right_dims), ((), ())), preferr...]
where the time goes in v4:
time: 570 us; the launch traced here: 560 us
  Pallas kernels  425 us (75%)
  matrix products  68.2 us (12%)
  local copies, waits for them, and re-layouts  34 us (6%)
  other arithmetic  31.9 us (6%)
    pallas_call x1, Pallas kernels, backward(): pl.pallas_call(functools.partial(backward_body, plan), out_shape=[jax.Sha...  282 us
    pallas_call x3, Pallas kernels, exchange(): pl.pallas_call(functools.partial(exchange_body, direction, with_places, m...  89 us
    dot_general x8, matrix products, contract(): lax.dot_general(left, right, (((left_dim,), (right_dim,)), ((), ())), pre...  33 us
    pallas_call x1, Pallas kernels, attend(): pl.pallas_call(attend_body, out_shape=[jax.ShapeDtypeStruct((peers, 64, 2...  24.2 us
    pallas_call x1, Pallas kernels, sum_small(): pl.pallas_call(small_body, out_shape=jax.ShapeDtypeStruct(small.shape, sm...  22.1 us
    dot_general x3, matrix products, both(): lax.dot_general(left, right, ((left_dims, right_dims), ((), ())), preferr...  15 us
    dot_general x1, matrix products, per_device_heads(): hidden_in = jnp.dot(second, mat_fc, preferred_element_type=f32) + bias_fc  11.5 us

profile of v4, /device:TPU:0, one launch (start us, length us, event | category | flops | bytes accessed | tf_op | source)
XLA Modules:
  0.0 560.5 jit_solution(6437886942807452827)
XLA Ops:
  0.6 1.3 reshape.336.refs_1_
  1.9 1.3 reshape.337.refs_2_
  3.2 1.3 reshape.338.refs_3_
  4.4 1.3 reshape.339.refs_4_
  5.7 1.3 reshape.340.refs_5_
  7.0 1.3 reshape.341.refs_6_
  8.2 1.3 reshape.342.refs_7_
  9.5 1.3 reshape.343.refs_8_
  10.7 1.3 reshape.344.refs_9_
  12.0 7.1 %share1.1 = (bf16[2,544,3264]{2,1,0:T(8,128)(2,1)}, bf16[2,1,544]{2,1,0:T(2,128)(2,1)}, bf16[2,1,544]{2,1,0:T(2,128)(2,1)}, bf16[2,1,544]{2,1,0:T(2,128)(2,1)}, ...) custom-call(bf16[544,3264]{1,0:T(8,128)(2,1)} %refs_0_.1, ...), custom_call_target="tpu_custom_call" | custom-call | tf_op jit(solution)/shard_map/share1/pallas_call | solution.py:519
  19.2 0.7 convert_reduce_fusion.12
  21.5 5.6 fusion.1
  27.5 1.5 pad_maximum_fusion.1.refs_0_
  29.0 0.6 pad_maximum_fusion.3.refs_1_
  30.2 1.0 copy.72.refs_6_
  31.4 1.1 copy.71
  32.4 44.3 %exchange2.1 = (bf16[16,256,256]{2,1,0:T(8,128)(2,1)}, bf16[2,64,128]{2,1,0:T(8,128)(2,1)}, s32[16,2,128]{2,1,0:T(2,128)}, bf16[2,544,1088]{2,1,0:T(8,128)(2,1)}...) custom-call(bf16[16,256,256]{2,1,0:T(8,128)(2,1)} %pad_maximum_fusio, ...), custom_call_target="tpu_custom_call" | custom-call | tf_op jit(solution)/shard_map/exchange2/pallas_call | solution.py:472
  76.8 0.6 dynamic-slice.2
  77.4 1.4 fusion.44
  78.8 0.7 bitcast_add_fusion
  79.8 0.6 broadcast_in_dim.45.limit.refs_2_
  80.4 2.9 broadcast_in_dim.46.places.refs_3_
  83.3 24.2 %attend.1 = (bf16[16,64,256]{2,1,0:T(8,128)(2,1)}, bf16[2,64,128]{2,1,0:T(8,128)(2,1)}, f32[17,64,256]{2,1,0:T(8,128)}, f32[17,1,256]{2,1,0:T(1,128)}) custom-call(bf16[16,256,256]{2,1,0:T(8,128)(2,1)} %get-tuple-element.56.got.refs_0_, bf16[2,64,128]{2,1,0:T(8,128)(2,1)} %get-tuple-element.57.last.refs_1_, s32[17,1,256]{2,1,0:T(1,128)} %broadcast_in_dim.45.limit.refs_2_, ...), custom_call_target="tpu_custom_call" | custom-call | tf_op jit(solution)/shard_map/attend/pallas_call | solution.py:597
  107.5 28.2 %exchange3.1 = (bf16[16,64,256]{2,1,0:T(8,128)(2,1)}, bf16[2,64,128]{2,1,0:T(8,128)(2,1)}) custom-call(bf16[16,64,256]{2,1,0:T(8,128)(2,1)} %get-tuple-element.59.refs_0_, bf16[2,64,128]{2,1,0:T(8,128)(2,1)} %get-tuple-element.60.refs_1_), custom_call_target="tpu_custom_call" | custom-call | tf_op jit(solution)/shard_map/exchange3/pallas_call | solution.py:472
  135.7 0.7 slice_bitcast_fusion.5
  136.5 3.1 fusion.61
  139.6 6.0 %fusion.24 = f32[256,2176]{1,0:T(8,128)} fusion(bf16[256,1088]{1,0:T(8,128)(2,1)S(1)} %bitcast.112, bf16[2,1088,2176]{2,1,0:T(8,128)(2,1)} %get-tuple-element.70), kind=kOutput, calls=%fused_computation.32 | convolution fusion | flops 1212153856 | bytes 7520256 | tf_op jit(solution)/shard_map/dot_general | solution.py:313
  145.6 3.1 fusion.21
  149.6 1.3 copy-done.37
  150.8 11.5 %convert_reduce_fusion = (f32[4352]{0:T(1024)}, bf16[256,4352]{1,0:T(8,128)(2,1)}, bf16[256,4352]{1,0:T(8,128)(2,1)}) fusion(f32[256,2176]{1,0:T(8,128)S(1)} %copy-done.37, f32[256,2176]{1,0:T(8,128)} %fusion.21, f32[4352]{0:T(1024)S(1)} %reshape.373, bf16[256,1088]{1,0:T(8,128)(2,1)S(1)} %add_convert_fusion.1.refs_3_, bf16[1088,4352]{1,0:T(8,128)(2,1)} %bitcast.133), kind=kOutput, calls=%fused_computation.25 | convolution fusion | flops 2453270272 | bytes 18974720 | tf_op jit(solution)/shard_map/dot_general | solution.py:1355
  162.5 4.5 fusion.29
  167.0 4.1 fusion.35
  171.1 1.1 copy.87
  172.2 8.6 %fusion.63 = (f32[1088]{0:T(1024)}, f32[256,1088]{0,1:T(8,128)}) fusion(bf16[256,4352]{1,0:T(8,128)(2,1)} %get-tuple-element.149.refs_4_, bf16[1088,4352]{1,0:T(8,128)(2,1)} %bitcast.134), kind=kOutput, calls=%fused_computation.132 | convolution fusion | flops 2424585216 | bytes 12816640 | tf_op jit(solution)/shard_map/dot_general | solution.py:40
  180.8 1.6 copy.80
  182.4 1.0 multiply_reduce_fusion
  183.4 1.1 fusion.57
  184.5 1.0 copy-done.2
  185.6 0.9 convolution_convert_fusion
  186.6 0.9 slice.183
  187.4 0.6 pad_maximum_fusion.4.refs_1_
  188.0 0.8 maximum_maximum_fusion.refs_5_
  188.9 16.5 %exchange4.1 = (bf16[16,64,256]{2,1,0:T(8,128)(2,1)}, bf16[2,64,128]{2,1,0:T(8,128)(2,1)}, bf16[2,256,2176]{2,1,0:T(8,128)(2,1)}, bf16[2,256,1088]{2,1,0:T(8,128...) custom-call(bf16[16,64,256]{2,1,0:T(8,128)(2,1)} %bitcast.119, ...), custom_call_target="tpu_custom_call" | custom-call | tf_op jit(solution)/shard_map/exchange4/pallas_call | solution.py:472
  205.5 6.7 %fusion.refs_9_ = bf16[1088,2176]{1,0:T(8,128)(2,1)} fusion(bf16[2,256,1088]{2,1,0:T(8,128)(2,1)S(1)} %copy-done.33, bf16[2,256,2176]{2,1,0:T(8,128)(2,1)} %get-tuple-element.77), kind=kOutput, calls=%fused_computation.1 | convolution fusion | flops 2426675200 | bytes 8077312 | tf_op jit(solution)/shard_map/dot_general | solution.py:1400
  212.2 7.4 %bitcast_convert_fusion.refs_10_ = bf16[544,4352]{1,0:T(8,128)(2,1)} fusion(bf16[2,256,4352]{2,1,0:T(8,128)(2,1)} %get-tuple-element.79, bf16[2,256,1088]{2,1,0:T(8,128)(2,1)S(1)} %copy-done.13, s32[]{:T(128)S(6)} %select_n.27), kind=kOutput, calls=%fused_computation.2 | convolution fusion | flops 2426675200 | bytes 9846788 | tf_op jit(solution)/shard_map/dot_general | solution.py:1400
  219.6 0.9 fusion.27
  220.5 1.2 pad.4.refs_11_
  221.7 282.5 %backward.1 = (bf16[1088,2176]{1,0:T(8,128)(2,1)}, bf16[544,4352]{1,0:T(8,128)(2,1)}, bf16[544,1280]{1,0:T(8,128)(2,1)}, bf16[544,3328]{1,0:T(8,128)(2,1)}, bf16...) custom-call(bf16[16,256,256]{2,1,0:T(8,128)(2,1)} %get-tuple-element, ...), custom_call_target="tpu_custom_call" | custom-call | tf_op jit(solution)/shard_map/backward/pallas_call | solution.py:1195
  504.2 5.7 %fusion.62 = (f32[1088]{0:T(1024)S(1)}, f32[256,1088]{0,1:T(8,128)S(1)}) fusion(bf16[1088,3264]{1,0:T(8,128)(2,1)} %bitcast.136, bf16[3328,256]{1,0:T(8,128)(2,1)} %get-tuple-element.82), kind=kOutput, calls=%fused_computation.131 | convolution fusion | flops 1818508288 | bytes 10031360 | tf_op jit(solution)/shard_map/dot_general | solution.py:313
  510.3 0.9 copy-done.1
  511.2 0.5 multiply_reduce_fusion.1
  511.7 0.8 copy-done.3
  512.4 0.4 add_convert_fusion
  512.9 1.1 copy.88
  514.0 1.6 convert_reduce_fusion.2
  516.1 1.3 concatenate.39
  517.4 22.1 %small6.1 = f32[2,8,1088]{2,1,0:T(8,128)} custom-call(f32[2,8,1088]{2,1,0:T(8,128)} %bitcast.128), custom_call_target="tpu_custom_call" | custom-call | tf_op jit(solution)/shard_map/small6/pallas_call | solution.py:934
  539.5 0.8 fusion.60
  540.3 0.7 fusion.46
  541.0 5.7 %slice_convert_fusion = f32[544,3264]{1,0:T(8,128)} fusion(bf16[544,3328]{1,0:T(8,128)(2,1)} %get-tuple-element.83), kind=kLoop, calls=%fused_computation.33 | loop fusion | flops 1775616 | bytes 10653696 | tf_op jit(solution)/shard_map/convert_element_type | solution.py:1448
  546.7 1.6 slice_convert_fusion.1
  548.4 4.5 convert_element_type.233
  552.8 0.7 reshape.363
  553.5 6.7 %convert_bitcast_fusion = f32[2176,1088]{0,1:T(8,128)} fusion(bf16[1088,2176]{1,0:T(8,128)(2,1)} %get-tuple-element.86), kind=kLoop, calls=%fused_computation.3 | loop fusion | flops 2367488 | bytes 14204928 | tf_op jit(solution)/shard_map/transpose | solution.py:1457
  (140 shorter events, 4.8 us)
Async XLA Ops:
  12.0 8.0 %copy-start.4 = (bf16[2,1,128,1088]{2,3,1,0:T(8,128)(2,1)S(1)}, bf16[2,1,128,1088]{2,3,1,0:T(8,128)(2,1)}, u32[]{:S(2)}) copy-start(bf16[2,1,128,1088]{2,3,1,0:T(8,128)(2,1)} %param.17) | copy-start | bytes 1671172
  20.1 9.8 %copy-start.14 = (f32[1088]{0:T(1024)}, f32[1088]{0:T(1024)S(1)}, u32[]{:S(2)}) copy-start(f32[1088]{0:T(1024)S(1)} %reshape.365) | copy-start | bytes 13060
  20.2 9.6 %copy-start.20 = (f32[256]{0:T(256)}, f32[256]{0:T(256)S(1)}, u32[]{:S(2)}) copy-start(f32[256]{0:T(256)S(1)} %get-tuple-element.169) | copy-start | bytes 3076
  20.3 0.9 copy-start.29
  20.3 0.9 copy-start.30
  20.4 9.4 %copy-start.22 = (f32[256]{0:T(256)}, f32[256]{0:T(256)S(1)}, u32[]{:S(2)}) copy-start(f32[256]{0:T(256)S(1)} %get-tuple-element.171) | copy-start | bytes 3076
  29.9 106.6 %copy-start = (f32[2,1,128,1088]{3,2,0,1:T(8,128)}, f32[2,1,128,1088]{3,2,0,1:T(8,128)S(1)}, u32[]{:S(2)}) copy-start(f32[2,1,128,1088]{3,2,0,1:T(8,128)S(1)} %copy.69) | copy-start | bytes 3342340
  29.9 1.5 copy-start.9
  32.4 44.3 %copy-start.27 = (bf16[2,1,544]{2,1,0:T(2,128)(2,1)S(1)}, bf16[2,1,544]{2,1,0:T(2,128)(2,1)}, u32[]{:S(2)}) copy-start(bf16[2,1,544]{2,1,0:T(2,128)(2,1)} %get-tuple-element.64) | copy-start | bytes 6532
  32.4 44.3 %copy-start.28 = (bf16[2,1,544]{2,1,0:T(2,128)(2,1)S(1)}, bf16[2,1,544]{2,1,0:T(2,128)(2,1)}, u32[]{:S(2)}) copy-start(bf16[2,1,544]{2,1,0:T(2,128)(2,1)} %get-tuple-element.65) | copy-start | bytes 6532
  32.4 44.4 %copy-start.36 = (s32[2,1]{0,1:T(1,128)S(1)}, s32[2,1]{0,1:T(1,128)}, u32[]{:S(2)}) copy-start(s32[2,1]{0,1:T(1,128)} %param.20) | copy-start | bytes 28
  136.5 3.1 copy-start.5
  136.5 9.1 %copy-start.31 = (bf16[2,1088,2176]{2,1,0:T(8,128)(2,1)S(1)}, bf16[2,1088,2176]{2,1,0:T(8,128)(2,1)}, u32[]{:S(2)}) copy-start(bf16[2,1088,2176]{2,1,0:T(8,128)(2,1)} %get-tuple-element.70) | copy-start | bytes 28409860
  145.6 3.1 copy-start.19
  145.6 3.2 copy-start.25
  145.6 3.2 copy-start.26
  149.0 1.8 copy-start.37
  149.6 12.8 %copy-start.7 = (bf16[256,1088]{1,0:T(8,128)(2,1)}, bf16[256,1088]{1,0:T(8,128)(2,1)S(1)}, u32[]{:S(2)}) copy-start(bf16[256,1088]{1,0:T(8,128)(2,1)S(1)} %add_convert_fusion.1.refs_3_) | copy-start | bytes 1671172
  162.5 4.6 copy-start.8
  183.4 2.2 copy-start.32
  184.5 1.0 copy-start.2
  185.6 0.9 copy-start.6
  186.5 1.5 copy-start.12
  188.9 16.6 %copy-start.33 = (bf16[2,256,1088]{2,1,0:T(8,128)(2,1)S(1)}, bf16[2,256,1088]{2,1,0:T(8,128)(2,1)}, u32[]{:S(2)}) copy-start(bf16[2,256,1088]{2,1,0:T(8,128)(2,1)} %get-tuple-element.76) | copy-start | bytes 3342340
  205.5 6.7 %copy-start.13 = (bf16[2,256,1088]{2,1,0:T(8,128)(2,1)S(1)}, bf16[2,256,1088]{2,1,0:T(8,128)(2,1)}, u32[]{:S(2)}) copy-start(bf16[2,256,1088]{2,1,0:T(8,128)(2,1)} %get-tuple-element.78) | copy-start | bytes 3342340
  212.2 7.4 %copy-start.34 = (bf16[2,256,1088]{2,1,0:T(8,128)(2,1)S(1)}, bf16[2,256,1088]{2,1,0:T(8,128)(2,1)}, u32[]{:S(2)}) copy-start(bf16[2,256,1088]{2,1,0:T(8,128)(2,1)} %get-tuple-element.81) | copy-start | bytes 3342340
  212.2 7.4 %copy-start.35 = (bf16[2,544,256]{2,1,0:T(8,128)(2,1)S(1)}, bf16[2,544,256]{2,1,0:T(8,128)(2,1)}, u32[]{:S(2)}) copy-start(bf16[2,544,256]{2,1,0:T(8,128)(2,1)} %get-tuple-element.80) | copy-start | bytes 1671172
  509.9 1.3 copy-start.1
  509.9 1.3 copy-start.15
  509.9 1.3 copy-start.21
  509.9 1.3 copy-start.23
  511.2 1.3 copy-start.3
  512.9 2.8 copy-start.17
  512.9 2.8 copy-start.16
  512.9 2.8 copy-start.24
  512.9 2.8 copy-start.10
  512.9 3.0 copy-start.18
  541.0 7.4 %slice-start = ((s8[4734976]{0:T(1024)(128)(4,1)}), s8[4194304]{0:T(1024)(128)(4,1)S(1)}, s32[]{:S(2)}) async-start(s8[4734976]{0:T(1024)(128)(4,1)} %bitcast.115), calls=%async_computation | async-start | bytes 8388608
  541.0 5.7 %copy-start.11 = (bf16[544,1280]{1,0:T(8,128)(2,1)S(1)}, bf16[544,1280]{1,0:T(8,128)(2,1)}, u32[]{:S(2)}) copy-start(bf16[544,1280]{1,0:T(8,128)(2,1)} %get-tuple-element.84) | copy-start | bytes 4177924
  541.0 7.4 %slice-start.1 = ((s8[4734976]{0:T(1024)(128)(4,1)}), s8[540672]{0:T(1024)(128)(4,1)S(1)}, s32[]{:S(2)}) async-start(s8[4734976]{0:T(1024)(128)(4,1)} %bitcast.115), calls=%async_computation.1 | async-start | bytes 1081344
